TPU v7x, 512 devices: a whole 4x8x8 slice. The times are simulated.
512 devices in a mesh: dp: 16 (over z, core), expert: 8 (over y), sequence: 4 (over x).
Axes of the slice: x: 4, y: 8, z: 8, core: 2. Of those that a mesh axis runs over, the one named last changes fastest.
Arguments:
- tokens: bfloat16 [1536, 3072], P(('dp', 'sequence')), may hold values from -6 to 6
- cotangent: bfloat16 [1536, 3072], P(('dp', 'sequence')), may hold values from -4 to 4
- experts: int32 [1536, 2], P(('dp', 'sequence')), may hold values from 0 to 7, all different within a row; in each aligned block of 24 rows (0 to 23, 24 to 47, ...) at most 10 rows name the same one
- gate_weights: float32 [1536, 2], P(('dp', 'sequence')), may hold values from 0.1 to 1
- w_gate: bfloat16 [8, 8192, 3072], P('expert', ('dp', 'sequence')), may hold values from -0.109375 to 0.109375
- w_up: bfloat16 [8, 8192, 3072], P('expert', ('dp', 'sequence')), may hold values from -0.109375 to 0.109375
- w_down: bfloat16 [8, 8192, 3072], P('expert', ('dp', 'sequence')), may hold values from -0.0625 to 0.0625
Outputs:
- output: bfloat16 [1536, 3072], P(('dp', 'sequence'), 'expert')
- grad_tokens: bfloat16 [1536, 3072], P(('dp', 'sequence'), 'expert')
- grad_w_gate: bfloat16 [8, 8192, 3072], P('expert', ('dp', 'sequence'))
- grad_w_up: bfloat16 [8, 8192, 3072], P('expert', ('dp', 'sequence'))
- grad_w_down: bfloat16 [8, 8192, 3072], P('expert', ('dp', 'sequence'))
Inputs may be any that keep to these rules, and one draw needn't show every extreme that they name: `experts`: A token's two ids differ. Within the rows of one device (aligned blocks of 24 rows) no id is named by more than 10 rows, a bound that some block reaches.
All inputs are finite; a program needn't handle non-finite values.
Results may differ from a plain program's by a relative error of at most 0.019.
Values may be sent and summed in bfloat16 or wider, within the bound.
No kernel may reach another device: no remote copies, remote signals or barrier semaphores. Data moves between devices by JAX's collectives and lax.ppermute only.
A program may use at most 128 MiB of HBM per device.

v0:
```python
import jax
import jax.numpy as jnp
from jax import lax
from jax.sharding import PartitionSpec as P

C = 10


HIGH = lax.Precision.HIGHEST


def on_device(tokens, cotangent, experts, gate_weights, w_gate, w_up, w_down):
    local = w_gate.shape[0]
    model_width = tokens.shape[1]
    first_id = lax.axis_index("expert") * local
    local_ids = first_id + jnp.arange(local, dtype=jnp.int32)
    chosen = (experts[:, :, None] == local_ids[None, None, :]).astype(jnp.int32)
    routed = jnp.sum(chosen, axis=1)
    gate_of = jnp.sum(gate_weights[:, :, None] * chosen.astype(jnp.float32), axis=1)
    slot_of = jnp.cumsum(routed, axis=0) - routed
    slot_ids = jnp.arange(C, dtype=jnp.int32)
    placing = (
        (slot_of.T[:, None, :] == slot_ids[None, :, None]) & (routed.T[:, None, :] == 1)
    ).astype(jnp.float32)
    placing_half = placing.astype(jnp.bfloat16)
    slot_gate = jnp.einsum("ect,te->ec", placing, gate_of, precision=HIGH)
    slot_tokens = jnp.einsum(
        "ect,td->ecd", placing_half, tokens, preferred_element_type=jnp.float32
    ).astype(jnp.bfloat16)
    picked_grad = jnp.einsum(
        "ect,td->ecd", placing_half, cotangent, preferred_element_type=jnp.float32
    )
    scaled_grad = (picked_grad * slot_gate[:, :, None]).astype(jnp.bfloat16)
    dp_count = lax.axis_size("dp")
    seq_count = lax.axis_size("sequence")
    seq_index = lax.axis_index("sequence")
    every_tok, every_grad = (
        lax.all_gather(slot_tokens, ("dp", "sequence"), axis=1, tiled=True),
        lax.all_gather(scaled_grad, ("dp", "sequence"), axis=1, tiled=True),
    )
    grid_tok = every_tok.reshape(local, dp_count, seq_count, C, model_width)
    grid_grad = every_grad.reshape(local, dp_count, seq_count, C, model_width)
    own_tok = lax.dynamic_index_in_dim(grid_tok, seq_index, 2, keepdims=False).reshape(
        local, dp_count * C, model_width
    )
    own_grad = lax.dynamic_index_in_dim(grid_grad, seq_index, 2, keepdims=False).reshape(
        local, dp_count * C, model_width
    )
    gate_rows, up_rows, down_rows = (
        lax.all_gather(w_gate, "sequence", axis=1, tiled=True),
        lax.all_gather(w_up, "sequence", axis=1, tiled=True),
        lax.all_gather(w_down, "sequence", axis=1, tiled=True),
    )
    pre_gate = jnp.einsum("erd,ehd->erh", own_tok, gate_rows, preferred_element_type=jnp.float32)
    pre_up = jnp.einsum("erd,ehd->erh", own_tok, up_rows, preferred_element_type=jnp.float32)
    sigmoid_gate = jax.nn.sigmoid(pre_gate)
    activated = pre_gate * sigmoid_gate
    hidden = (activated * pre_up).astype(jnp.bfloat16)
    out_part = jnp.einsum("erh,ehd->erd", hidden, down_rows, preferred_element_type=jnp.float32)
    out_part = lax.optimization_barrier(out_part.astype(jnp.bfloat16)).astype(jnp.float32)
    grad_hidden = jnp.einsum(
        "erd,ehd->erh", own_grad, down_rows, preferred_element_type=jnp.float32
    )
    grad_gate = (
        grad_hidden * pre_up * sigmoid_gate * (1.0 + pre_gate * (1.0 - sigmoid_gate))
    ).astype(jnp.bfloat16)
    grad_up = (grad_hidden * activated).astype(jnp.bfloat16)
    din_part = jnp.einsum("erh,ehd->erd", grad_gate, gate_rows, preferred_element_type=jnp.float32)
    din_part = din_part + jnp.einsum(
        "erh,ehd->erd", grad_up, up_rows, preferred_element_type=jnp.float32
    )
    din_part = lax.optimization_barrier(din_part.astype(jnp.bfloat16)).astype(jnp.float32)
    gate_cols, up_cols, hidden_cols = (
        lax.all_to_all(grad_gate, "sequence", split_axis=2, concat_axis=1, tiled=True),
        lax.all_to_all(grad_up, "sequence", split_axis=2, concat_axis=1, tiled=True),
        lax.all_to_all(hidden, "sequence", split_axis=2, concat_axis=1, tiled=True),
    )
    block_units = gate_cols.shape[2]
    gate_grid = gate_cols.reshape(local, seq_count, dp_count, C, block_units)
    up_grid = up_cols.reshape(local, seq_count, dp_count, C, block_units)
    hidden_grid = hidden_cols.reshape(local, seq_count, dp_count, C, block_units)
    form = "espch,epscd->ehd"
    grad_w_gate = jnp.einsum(form, gate_grid, grid_tok, preferred_element_type=jnp.float32).astype(
        jnp.bfloat16
    )
    grad_w_up = jnp.einsum(form, up_grid, grid_tok, preferred_element_type=jnp.float32).astype(
        jnp.bfloat16
    )
    grad_w_down = jnp.einsum(
        form, hidden_grid, grid_grad, preferred_element_type=jnp.float32
    ).astype(jnp.bfloat16)
    expert_out, expert_din = (
        lax.psum_scatter(
            out_part.astype(jnp.bfloat16), "dp", scatter_dimension=1, tiled=True
        ).astype(jnp.float32),
        lax.psum_scatter(
            din_part.astype(jnp.bfloat16), "dp", scatter_dimension=1, tiled=True
        ).astype(jnp.float32),
    )
    out_term = jnp.einsum(
        "ect,ecd->td", placing * slot_gate[:, :, None], expert_out, precision=HIGH
    )
    din_term = jnp.einsum("ect,ecd->td", placing, expert_din, precision=HIGH)
    out_total, din_total = (
        lax.psum_scatter(
            out_term.astype(jnp.bfloat16), "expert", scatter_dimension=1, tiled=True
        ).astype(jnp.float32),
        lax.psum_scatter(
            din_term.astype(jnp.bfloat16), "expert", scatter_dimension=1, tiled=True
        ).astype(jnp.float32),
    )
    return (
        out_total.astype(jnp.bfloat16),
        din_total.astype(jnp.bfloat16),
        grad_w_gate,
        grad_w_up,
        grad_w_down,
    )


def solution(mesh):
    return jax.shard_map(
        on_device,
        mesh=mesh,
        in_specs=(
            P(("dp", "sequence"), None),
            P(("dp", "sequence"), None),
            P(("dp", "sequence"), None),
            P(("dp", "sequence"), None),
            P("expert", ("dp", "sequence"), None),
            P("expert", ("dp", "sequence"), None),
            P("expert", ("dp", "sequence"), None),
        ),
        out_specs=(
            P(("dp", "sequence"), "expert"),
            P(("dp", "sequence"), "expert"),
            P("expert", ("dp", "sequence"), None),
            P("expert", ("dp", "sequence"), None),
            P("expert", ("dp", "sequence"), None),
        ),
        check_vma=False,
    )
```

profile of v0, /device:TPU:2, one launch (start us, length us, event | category | flops | bytes accessed | tf_op | source)
XLA Modules:
  0.0 552.4 jit_solution(13933945983895416042)
XLA Ops:
  10.0 1.7 fusion.11
  13.7 88.2 %all-gather.16.cloned.1.call-done = bf16[64,10,3072]{2,1,0:T(8,128)(2,1)} async-done(((bf16[1,10,3072]{2,1,0:T(8,128)(2,1)}), bf16[64,10,3072]{2,1,0:T(8,128)(2,1)}) %all-gather.16.cloned.1.call-update) | async-done | bytes 3932176 | tf_op jit(solution)/shard_map/all_gather | solution.py:38
  103.8 85.1 %all-gather.18.cloned.1.call-done = bf16[64,10,3072]{2,1,0:T(8,128)(2,1)} async-done(((bf16[1,10,3072]{2,1,0:T(8,128)(2,1)}), bf16[64,10,3072]{2,1,0:T(8,128)(2,1)}) %all-gather.18.cloned.1.call-update) | async-done | bytes 3932176 | tf_op jit(solution)/shard_map/all_gather | solution.py:39
  191.7 41.3 %all-gather.10.cloned.1.call-done = bf16[1,512,3072]{2,1,0:T(8,128)(2,1)} async-done(((bf16[1,128,3072]{2,1,0:T(8,128)(2,1)}), bf16[1,512,3072]{2,1,0:T(8,128)(2,1)}) %all-gather.10.cloned.1.call-update) | async-done | bytes 3145744 | tf_op jit(solution)/shard_map/all_gather | solution.py:50
  232.9 3.1 fusion.20
  236.0 43.9 %all-gather.12.cloned.1.call-done = bf16[1,512,3072]{2,1,0:T(8,128)(2,1)} async-done(((bf16[1,128,3072]{2,1,0:T(8,128)(2,1)}), bf16[1,512,3072]{2,1,0:T(8,128)(2,1)}) %all-gather.12.cloned.1.call-update) | async-done | bytes 3145744 | tf_op jit(solution)/shard_map/all_gather | solution.py:51
  280.0 3.1 fusion.16
  283.0 43.9 %all-gather.14.cloned.1.call-done = bf16[1,512,3072]{2,1,0:T(8,128)(2,1)} async-done(((bf16[1,128,3072]{2,1,0:T(8,128)(2,1)}), bf16[1,512,3072]{2,1,0:T(8,128)(2,1)}) %all-gather.14.cloned.1.call-update) | async-done | bytes 3145744 | tf_op jit(solution)/shard_map/all_gather | solution.py:52
  327.0 3.3 multiply_convert_fusion
  330.3 1.7 fusion.5
  334.0 1.7 fusion.4
  336.7 2.3 reduce.5
  340.1 4.6 all-to-all-start
  347.1 2.3 reduce.6
  350.5 4.8 all-to-all-start.1
  355.8 2.3 reduce.7
  360.1 4.8 all-to-all-start.2
  365.7 4.7 fusion.8
  370.4 88.1 %all-reduce.5.cloned.1.call-done = (bf16[1,160,3072]{2,1,0:T(8,128)(2,1)}, bf16[1,160,3072]{2,1,0:T(8,128)(2,1)}) async-done(((bf16[1,160,3072]{2,1,0:T(8,128)(2,1)}, bf16[1,160,3072]{2,1,0:T(8,128)(2,1)}), (bf16[1,160,3072]{2,1,0:T(8,128)(2,1)}, bf16[1,160,3072]{2,1,0:T(8,128)(2,1)})) %all-reduce.5.cloned.1.call-update) | async-done | bytes 1966096
  461.0 4.7 fusion.7
  468.9 4.7 fusion.6
  473.6 27.9 %reduce-scatter.9.cloned.1.call-done = bf16[384,24]{1,0:T(8,128)(2,1)} async-done(((bf16[3072,24]{1,0:T(8,128)(2,1)}), bf16[384,24]{1,0:T(8,128)(2,1)}) %reduce-scatter.9.cloned.1.call-update) | async-done | bytes 18448
  501.5 1.6 copy.55
  503.0 41.0 %reduce-scatter.11.cloned.1.call-done = bf16[384,24]{1,0:T(8,128)(2,1)} async-done(((bf16[3072,24]{1,0:T(8,128)(2,1)}), bf16[384,24]{1,0:T(8,128)(2,1)}) %reduce-scatter.11.cloned.1.call-update) | async-done | bytes 18448
  (66 shorter events, 26.6 us)
Async XLA Ops:
  7.2 1.1 copy-start
  7.2 94.7 %all-gather.16.cloned.1.call-start = ((), (), s32[]{:S(2)}) async-start(), calls=%async_computation.8 | async-start | bytes 6389760 | tf_op jit(solution)/shard_map/all_gather | solution.py:38
  9.1 179.9 %all-gather.18.cloned.1.call-start = ((), (), s32[]{:S(2)}) async-start(), calls=%async_computation.9 | async-start | bytes 6389760 | tf_op jit(solution)/shard_map/all_gather | solution.py:39
  11.7 221.2 %all-gather.10.cloned.1.call-start = ((), (), s32[]{:S(2)}) async-start(), calls=%async_computation.5 | async-start | bytes 3932160 | tf_op jit(solution)/shard_map/all_gather | solution.py:50
  12.4 267.5 %all-gather.12.cloned.1.call-start = ((), (), s32[]{:S(2)}) async-start(), calls=%async_computation.6 | async-start | bytes 3932160 | tf_op jit(solution)/shard_map/all_gather | solution.py:51
  13.0 314.0 %all-gather.14.cloned.1.call-start = ((), (), s32[]{:S(2)}) async-start(), calls=%async_computation.7 | async-start | bytes 3932160 | tf_op jit(solution)/shard_map/all_gather | solution.py:52
  13.6 444.9 %all-reduce.5.cloned.1.call-start = ((), (), s32[]{:S(2)}) async-start(), calls=%async_computation.12 | async-start | bytes 3932160
  236.0 91.0 %copy-start.4 = (bf16[160,3072]{1,0:T(8,128)(2,1)S(1)}, bf16[160,3072]{1,0:T(8,128)(2,1)}, u32[]{:S(2)}) copy-start(bf16[160,3072]{1,0:T(8,128)(2,1)} %reshape.384) | copy-start | bytes 2949124
  327.0 3.3 copy-start.3
  330.3 2.2 copy-start.1
  332.0 2.0 copy-start.2
  340.1 10.4 %all-to-all-start = ((bf16[4,2,10240]{2,1,0:T(2,128)(2,1)}), bf16[4,2,10240]{2,1,0:T(2,128)(2,1)S(1)}, u32[]{:S(2)}, u32[]{:S(2)}) async-start(bf16[4,2,10240]{2,1,0:T(2,128)(2,1)} %reshape.421), calls=%async_computation | async-start | bytes 327680 | tf_op jit(solution)/shard_map/all_to_all | solution.py:74
  350.5 9.6 %all-to-all-start.1 = ((bf16[4,2,10240]{2,1,0:T(2,128)(2,1)}), bf16[4,2,10240]{2,1,0:T(2,128)(2,1)S(1)}, u32[]{:S(2)}, u32[]{:S(2)}) async-start(bf16[4,2,10240]{2,1,0:T(2,128)(2,1)} %reshape.423), calls=%async_computation.1 | async-start | bytes 327680 | tf_op jit(solution)/shard_map/all_to_all | solution.py:75
  360.1 105.6 %all-to-all-start.2 = ((bf16[4,2,10240]{2,1,0:T(2,128)(2,1)}), bf16[4,2,10240]{2,1,0:T(2,128)(2,1)S(1)}, u32[]{:S(2)}, u32[]{:S(2)}) async-start(bf16[4,2,10240]{2,1,0:T(2,128)(2,1)} %reshape.425), calls=%async_computation.2 | async-start | bytes 327680 | tf_op jit(solution)/shard_map/all_to_all | solution.py:76
  364.9 136.6 %reduce-scatter.9.cloned.1.call-start = ((), (), s32[]{:S(2)}) async-start(), calls=%async_computation.10 | async-start | bytes 884736
  461.0 83.1 %reduce-scatter.11.cloned.1.call-start = ((), (), s32[]{:S(2)}) async-start(), calls=%async_computation.11 | async-start | bytes 884736
Sparse Core Ops, SparseCore 0:
  11.9 89.9 all-gather.15
  105.8 83.1 all-gather.17
  191.0 41.8 all-gather.9
  234.9 45.0 all-gather.11
  281.9 45.0 all-gather.13
  335.8 122.6 all-reduce.4
  461.3 40.0 reduce-scatter.8
  504.3 39.6 reduce-scatter.10
where the time goes:
time: 553 us; the launch traced here: 552 us
  waiting for transfers between devices  461 us (83%)
  matrix products  32.6 us (6%)
  local copies, waits for them, and re-layouts  20.4 us (4%)
  between operations  15 us (3%)
  starting transfers between devices  14.5 us (3%)
  other arithmetic  8.64 us (2%)
    unnamed x11, waiting for transfers between devices  159 us
    all_gather x1, waiting for transfers between devices, on_device(): lax.all_gather(slot_tokens, ('dp', 'sequence'), axis=1, tiled=True)  88.2 us
    all_gather x1, waiting for transfers between devices, on_device(): lax.all_gather(scaled_grad, ('dp', 'sequence'), axis=1, tiled=True)  85.1 us
    all_gather x1, waiting for transfers between devices, on_device(): lax.all_gather(w_down, 'sequence', axis=1, tiled=True)  43.9 us
    all_gather x1, waiting for transfers between devices, on_device(): lax.all_gather(w_up, 'sequence', axis=1, tiled=True)  43.9 us
    all_gather x1, waiting for transfers between devices, on_device(): lax.all_gather(w_gate, 'sequence', axis=1, tiled=True)  41.3 us
    unnamed x24, local copies, waits for them, and re-layouts  16.3 us
  transfers between devices with their start and end apart: 11, of which 8 were waited for; matrix products, arithmetic and copies ran while one was open for 9% of the time, Pallas kernels for 0%

commit v1 on v0

v1 whole, which is shorter than its diff:
```python
import jax
import jax.numpy as jnp
from jax import lax
from jax.sharding import Mesh, PartitionSpec as P

C = 10
HIGH = lax.Precision.HIGHEST
F32 = jnp.float32
BF16 = jnp.bfloat16


def spread(block, axis):
    count = lax.axis_size(axis)
    copies = jnp.broadcast_to(block[None], (count,) + block.shape)
    return lax.all_to_all(copies, axis, split_axis=0, concat_axis=0, tiled=True)


def swap(a):
    return lax.ppermute(a, "c", [(0, 1), (1, 0)])


def slot_tables(experts, gate_weights, ids):
    chosen = (experts[:, :, None] == ids[None, None, :]).astype(jnp.int32)
    routed = jnp.sum(chosen, axis=1)
    gate_of = jnp.sum(gate_weights[:, :, None] * chosen.astype(F32), axis=1)
    slot_of = jnp.cumsum(routed, axis=0) - routed
    slot_ids = jnp.arange(C, dtype=jnp.int32)
    placing = (
        (slot_of.T[:, None, :] == slot_ids[None, :, None]) & (routed.T[:, None, :] == 1)
    ).astype(F32)
    return placing, gate_of


def dot(a, b, dims):
    return lax.dot_general(a, b, (dims, ((), ())), preferred_element_type=F32)


def forward_backward(rows_tok, rows_grad, w_gate, w_up, w_down):
    pre_gate = dot(rows_tok, w_gate, ((1,), (1,)))
    pre_up = dot(rows_tok, w_up, ((1,), (1,)))
    grad_hidden = dot(rows_grad, w_down, ((1,), (1,)))
    sigmoid_gate = jax.nn.sigmoid(pre_gate)
    activated = pre_gate * sigmoid_gate
    hidden = (activated * pre_up).astype(BF16)
    grad_gate = (
        grad_hidden * pre_up * sigmoid_gate * (1.0 + pre_gate * (1.0 - sigmoid_gate))
    ).astype(BF16)
    grad_up = (grad_hidden * activated).astype(BF16)
    out_part = dot(hidden, w_down, ((1,), (0,)))
    din_part = dot(grad_gate, w_gate, ((1,), (0,))) + dot(grad_up, w_up, ((1,), (0,)))
    return hidden, grad_gate, grad_up, out_part, din_part


def on_device(tokens, cotangent, experts, gate_weights, w_gate, w_up, w_down):
    w_gate, w_up, w_down = w_gate[0], w_up[0], w_down[0]
    width = tokens.shape[1]
    n_z, n_x, n_y = lax.axis_size("z"), lax.axis_size("x"), lax.axis_size("y")
    own_id = lax.axis_index("y")[None].astype(jnp.int32)
    placing, gate_of = slot_tables(experts, gate_weights, own_id)
    placing = placing[0]
    slot_gate = jnp.sum(placing * gate_of[:, 0][None, :], axis=1)
    picks = placing.astype(BF16)
    slot_tokens = dot(picks, tokens, ((1,), (0,))).astype(BF16)
    picked_grad = dot(picks, cotangent, ((1,), (0,)))
    scaled_grad = (picked_grad * slot_gate[:, None]).astype(BF16)

    block = jnp.concatenate([slot_tokens, scaled_grad], axis=0).reshape(4 * C, width // 2)
    by_z = spread(block, "z").reshape(n_z, 2, C, width)
    by_z = by_z.transpose(1, 0, 2, 3).reshape(2, n_z * C, width)
    own = spread(by_z, "x")
    other = swap(own)

    def rows(a, which):
        return a[:, which].reshape(n_x * n_z * C, width)

    tok_own, grad_own = rows(own, 0), rows(own, 1)
    tok_other, grad_other = rows(other, 0), rows(other, 1)
    hid_b, gg_b, gu_b, out_b, din_b = forward_backward(tok_other, grad_other, w_gate, w_up, w_down)
    hid_a, gg_a, gu_a, out_a, din_a = forward_backward(tok_own, grad_own, w_gate, w_up, w_down)

    def pack(out_part, din_part):
        return jnp.stack(
            [
                out_part.reshape(n_x, n_z * C, width),
                din_part.reshape(n_x, n_z * C, width),
            ],
            axis=1,
        )

    from_partner = swap(pack(out_b.astype(BF16), din_b.astype(BF16)))
    chip_sum = (pack(out_a, din_a) + from_partner.astype(F32)).astype(BF16)

    def weight_grad(left_a, right_a, left_b, right_b):
        total = dot(left_a, right_a, ((0,), (0,))) + dot(left_b, right_b, ((0,), (0,)))
        return total.astype(BF16)[None]

    grad_w_gate = weight_grad(gg_a, tok_own, gg_b, tok_other)
    grad_w_up = weight_grad(gu_a, tok_own, gu_b, tok_other)
    grad_w_down = weight_grad(hid_a, grad_own, hid_b, grad_other)

    sum_x = lax.all_to_all(chip_sum, "x", split_axis=0, concat_axis=0, tiled=True)
    sum_x = jnp.sum(sum_x.astype(F32), axis=0).astype(BF16)
    sum_x = sum_x.reshape(2, n_z, C, width).transpose(1, 0, 2, 3).reshape(n_z, 4 * C, width // 2)
    sum_z = lax.all_to_all(sum_x, "z", split_axis=0, concat_axis=0, tiled=True)
    sum_z = jnp.sum(sum_z.astype(F32), axis=0).astype(BF16)
    part = width // n_y
    to_y = sum_z.reshape(2 * C, n_y, part).transpose(1, 0, 2)
    by_y = lax.all_to_all(to_y, "y", split_axis=0, concat_axis=0, tiled=True)
    by_y = by_y.reshape(n_y, 2, C, part).astype(F32)

    all_placing, all_gates = slot_tables(
        experts, gate_weights, jnp.arange(n_y, dtype=jnp.int32)
    )
    weighted = all_placing * all_gates.T[:, None, :]
    output = jnp.einsum("ect,ecd->td", weighted, by_y[:, 0], precision=HIGH)
    grad_tokens = jnp.einsum("ect,ecd->td", all_placing, by_y[:, 1], precision=HIGH)
    return (
        output.astype(BF16),
        grad_tokens.astype(BF16),
        grad_w_gate,
        grad_w_up,
        grad_w_down,
    )


def solution(mesh):
    shape = mesh.devices.shape
    fine = Mesh(
        mesh.devices.reshape(shape[0] // 2, 2, shape[1], shape[2]), ("z", "c", "y", "x")
    )
    by_token = ("z", "c", "x")
    return jax.shard_map(
        on_device,
        mesh=fine,
        in_specs=(
            P(by_token, None),
            P(by_token, None),
            P(by_token, None),
            P(by_token, None),
            P("y", by_token, None),
            P("y", by_token, None),
            P("y", by_token, None),
        ),
        out_specs=(
            P(by_token, "y"),
            P(by_token, "y"),
            P("y", by_token, None),
            P("y", by_token, None),
            P("y", by_token, None),
        ),
        check_vma=False,
    )
```

time: 553 us -> 233 us (0.42)
  waiting for transfers between devices: 461 us -> 79 us
  blocking collectives: 0 us -> 85 us
  between operations: 15 us -> 0.99 us
  matrix products: 32.6 us -> 22.5 us
  starting transfers between devices: 14.5 us -> 21.9 us
  local copies, waits for them, and re-layouts: 20.4 us -> 13.9 us
    all_gather x5 -> x0, waiting for transfers between devices: 303 us -> none  [the longest x1 88.2 us: on_device(): lax.all_gather(slot_tokens, ('dp', 'sequence'), axis=1, tiled=True)]
    unnamed x11 -> x0, waiting for transfers between devices: 159 us -> none
    all_to_all x0 -> x2, blocking collectives: none -> 85 us  [spread(): return lax.all_to_all(copies, axis, split_axis=0, concat_axis=0, tiled=True)]
    all_to_all x3, waiting for transfers between devices: 0.01 us -> 71 us  [the longest x1 45.1 us: on_device(): lax.all_to_all(chip_sum, 'x', split_axis=0, concat_axis=0, tiled=True)]
    unnamed x24 -> x22, local copies, waits for them, and re-layouts: 16.3 us -> 1.74 us
    dot_general x14 -> x22, matrix products: 32.6 us -> 22.5 us  [the longest x20 20.9 us: dot(): return lax.dot_general(a, b, (dims, ((), ())), preferred_element_type=F32)]
    ppermute x0 -> x2, waiting for transfers between devices: none -> 8.06 us  [swap(): return lax.ppermute(a, 'c', [(0, 1), (1, 0)])]
    unnamed x3 -> x0, other arithmetic: 6.94 us -> none
  transfers between devices with their start and end apart: 11 -> 5, of which waited for: 8 -> 5; matrix products, arithmetic and copies ran while one was open for 9% -> 7% of each run, Pallas kernels for 0% -> 0%
where the time goes in v1:
time: 233 us; the launch traced here: 232 us
  blocking collectives  85 us (36%)
  waiting for transfers between devices  79 us (34%)
  matrix products  22.5 us (10%)
  starting transfers between devices  21.9 us (9%)
  local copies, waits for them, and re-layouts  13.9 us (6%)
  other arithmetic  8.93 us (4%)
    all_to_all x2, blocking collectives, spread(): return lax.all_to_all(copies, axis, split_axis=0, concat_axis=0, tiled=True)  85 us
    all_to_all x1, waiting for transfers between devices, on_device(): lax.all_to_all(chip_sum, 'x', split_axis=0, concat_axis=0, tiled=True)  45.1 us
    dot_general x20, matrix products, dot(): return lax.dot_general(a, b, (dims, ((), ())), preferred_element_type=F32)  20.9 us
    all_to_all x1, waiting for transfers between devices, on_device(): sum_z = lax.all_to_all(sum_x, 'z', split_axis=0, concat_axis=0, tiled=True)  19.3 us
    ppermute x2, waiting for transfers between devices, swap(): return lax.ppermute(a, 'c', [(0, 1), (1, 0)])  8.06 us
    all_to_all x1, starting transfers between devices, on_device(): by_y = lax.all_to_all(to_y, 'y', split_axis=0, concat_axis=0, tiled=True)  7.1 us
    all_to_all x1, waiting for transfers between devices, on_device(): by_y = lax.all_to_all(to_y, 'y', split_axis=0, concat_axis=0, tiled=True)  6.63 us
    all_to_all x1, starting transfers between devices, on_device(): lax.all_to_all(chip_sum, 'x', split_axis=0, concat_axis=0, tiled=True)  6.35 us
  transfers between devices with their start and end apart: 5, of which 5 were waited for; matrix products, arithmetic and copies ran while one was open for 7% of the time, Pallas kernels for 0%

profile of v1, /device:TPU:2, one launch (start us, length us, event | category | flops | bytes accessed | tf_op | source)
XLA Modules:
  0.0 232.3 jit_solution(12863197848419175055)
XLA Ops:
  4.9 37.4 %all_to_all.25 = bf16[8,40,1536]{2,1,0:T(8,128)(2,1)S(1)} all-to-all(bf16[8,40,1536]{2,1,0:T(8,128)(2,1)S(1)} %broadcast_in_dim.15), channel_id=1, replica_groups=mesh['z'=8,'c'=2,'y'=8,'x'=4] {'z'}, dimensions={0} | all-to-all | bytes 1966080 | tf_op jit(solution)/shard_map/all_to_all | solution.py:15
  44.5 47.6 %all_to_all.26 = bf16[4,2,80,3072]{3,2,1,0:T(8,128)(2,1)S(1)} all-to-all(bf16[4,2,80,3072]{3,2,1,0:T(8,128)(2,1)S(1)} %broadcast_in_dim.17), channel_id=1, replica_groups=mesh['z'=8,'c'=2,'y'=8,'x'=4] {'x'}, dimensions={0} | all-to-all | bytes 7864320 | tf_op jit(solution)/shard_map/all_to_all | solution.py:15
  92.1 2.0 collective-permute-start
  94.1 6.8 %collective-permute-done = bf16[4,2,80,3072]{3,2,1,0:T(8,128)(2,1)S(1)} collective-permute-done((bf16[4,2,80,3072]{3,2,1,0:T(8,128)(2,1)S(1)}, bf16[4,2,80,3072]{3,2,1,0:T(8,128)(2,1)S(1)}, u32[]{:S(2)}, u32[]{:S(2)}) %collective-permute-start) | collective-permute-done | bytes 3932192 | tf_op jit(solution)/shard_map/ppermute | solution.py:19
  106.7 2.2 collective-permute-start.1
  114.0 1.3 collective-permute-done.1
  115.4 1.3 fusion
  116.6 2.2 copy.62
  118.8 6.3 %all-to-all-start.2 = ((bf16[4,2,80,3072]{3,2,1,0:T(8,128)(2,1)}), bf16[4,2,80,3072]{3,2,1,0:T(8,128)(2,1)}, u32[]{:S(2)}, u32[]{:S(2)}) async-start(bf16[4,2,80,3072]{3,2,1,0:T(8,128)(2,1)} %copy.62), calls=%async_computation.2 | async-start | bytes 7864320 | tf_op jit(solution)/shard_map/all_to_all | solution.py:101
  125.3 45.1 %all-to-all-done.2 = bf16[4,2,80,3072]{3,2,1,0:T(8,128)(2,1)} async-done(((bf16[4,2,80,3072]{3,2,1,0:T(8,128)(2,1)}), bf16[4,2,80,3072]{3,2,1,0:T(8,128)(2,1)}, u32[]{:S(2)}, u32[]{:S(2)}) %all-to-all-start.2) | async-done | bytes 3932192 | tf_op jit(solution)/shard_map/all_to_all | solution.py:101
  170.4 4.1 %reduce_sum.74 = bf16[2,80,3072]{2,1,0:T(8,128)(2,1)} reduce(bf16[4,2,80,3072]{3,2,1,0:T(8,128)(2,1)} %all-to-all-done.2, bf16[]{:T(256)} %constant.25.clone.1), dimensions={0}, to_apply=%region_7.8 | reduce | flops 1474560 | bytes 4915202 | tf_op jit(solution)/shard_map/reduce_sum | solution.py:102
  174.4 2.2 copy.64
  176.7 1.5 copy.65
  178.2 2.4 %reshape.124 = bf16[8,40,1536]{2,1,0:T(8,128)(2,1)} reshape(bf16[8,2,10,3072]{3,2,1,0:T(8,128)(2,1)} %copy.65) | data formatting | bytes 1966080 | tf_op jit(solution)/shard_map/reshape | solution.py:103
  180.6 4.2 %all-to-all-start.3 = ((bf16[8,40,1536]{2,1,0:T(8,128)(2,1)}), bf16[8,40,1536]{2,1,0:T(8,128)(2,1)}, u32[]{:S(2)}, u32[]{:S(2)}) async-start(bf16[8,40,1536]{2,1,0:T(8,128)(2,1)} %reshape.124), calls=%async_computation.3 | async-start | bytes 1966080 | tf_op jit(solution)/shard_map/all_to_all | solution.py:104
  184.9 2.3 fusion.57
  187.8 1.8 fusion.55
  189.6 1.5 fusion.5
  191.1 1.5 fusion.6
  192.6 19.3 %all-to-all-done.3 = bf16[8,40,1536]{2,1,0:T(8,128)(2,1)} async-done(((bf16[8,40,1536]{2,1,0:T(8,128)(2,1)}), bf16[8,40,1536]{2,1,0:T(8,128)(2,1)}, u32[]{:S(2)}, u32[]{:S(2)}) %all-to-all-start.3) | async-done | bytes 983072 | tf_op jit(solution)/shard_map/all_to_all | solution.py:104
  211.8 1.3 reduce_sum.75
  213.9 7.1 %all-to-all-start.4 = ((bf16[8,20,384]{2,1,0:T(8,128)(2,1)}), bf16[8,20,384]{2,1,0:T(8,128)(2,1)S(1)}, u32[]{:S(2)}, u32[]{:S(2)}) async-start(bf16[8,20,384]{2,1,0:T(8,128)(2,1)} %copy.66), calls=%async_computation.4 | async-start | bytes 294912 | tf_op jit(solution)/shard_map/all_to_all | solution.py:108
  221.0 3.0 %fusion.7 = bf16[1,128,3072]{2,1,0:T(8,128)(2,1)} fusion(f32[128,3072]{1,0:T(8,128)} %fusion.55, bf16[320,128]{1,0:T(8,128)(2,1)S(1)} %get-tuple-element.10, bf16[320,3072]{1,0:T(8,128)(2,1)S(1)} %bitcast.104), kind=kOutput, calls=%fused_computation.16 | convolution fusion | flops 252444672 | bytes 4407296 | tf_op jit(solution)/shard_map/dot_general | solution.py:35
  224.0 6.6 %all-to-all-done.4 = bf16[8,20,384]{2,1,0:T(8,128)(2,1)S(1)} async-done(((bf16[8,20,384]{2,1,0:T(8,128)(2,1)}), bf16[8,20,384]{2,1,0:T(8,128)(2,1)S(1)}, u32[]{:S(2)}, u32[]{:S(2)}) %all-to-all-start.4) | async-done | bytes 122912 | tf_op jit(solution)/shard_map/all_to_all | solution.py:108
  (68 shorter events, 20.4 us)
Async XLA Ops:
  0.6 103.0 %copy-start = (bf16[1,128,3072]{2,1,0:T(8,128)(2,1)S(1)}, bf16[1,128,3072]{2,1,0:T(8,128)(2,1)}, u32[]{:S(2)}) copy-start(bf16[1,128,3072]{2,1,0:T(8,128)(2,1)} %param.12) | copy-start | bytes 2359300
  92.1 9.1 %copy-start.7 = (bf16[1,128,3072]{2,1,0:T(8,128)(2,1)S(1)}, bf16[1,128,3072]{2,1,0:T(8,128)(2,1)}, u32[]{:S(2)}) copy-start(bf16[1,128,3072]{2,1,0:T(8,128)(2,1)} %param.11) | copy-start | bytes 2359300
  92.1 8.8 %collective-permute-start = (bf16[4,2,80,3072]{3,2,1,0:T(8,128)(2,1)S(1)}, bf16[4,2,80,3072]{3,2,1,0:T(8,128)(2,1)S(1)}, u32[]{:S(2)}, u32[]{:S(2)}) collective-permute-start(bf16[4,2,80,3072]{3,2,1,0:T(8,128)(2,1)S(1)} %all_to_all.26), channel_id=1, source_target_pairs={{0,32},{32,0},{1,33},{33,1},{2,34},{34,2},{3,35},{35,3},{4,36},{36... | collective-permute-start | bytes 11796488 | tf_op jit(solution)/shard_map/ppermute | solution.py:19
  101.1 1.4 copy-start.4
  101.2 1.7 copy-start.8
  106.7 8.7 %collective-permute-start.1 = (bf16[4,2,80,3072]{3,2,0,1:T(8,128)(2,1)S(1)}, bf16[4,2,80,3072]{3,2,0,1:T(8,128)(2,1)S(1)}, u32[]{:S(2)}, u32[]{:S(2)}) collective-permute-start(bf16[4,2,80,3072]{3,2,0,1:T(8,128)(2,1)S(1)} %pad_maximum_fusion), channel_id=1, source_target_pairs={{0,32},{32,0},{1,33},{33,1},{2,34},{34,2},{3,35},{35,3},{4,36},{36... | collective-permute-start | bytes 11796488 | tf_op jit(solution)/shard_map/ppermute | solution.py:19
  109.2 1.4 copy-start.6
  109.2 2.1 copy-start.2
  118.8 6.3 %copy-start.9 = (s32[24,2]{0,1:T(2,128)S(1)}, s32[24,2]{0,1:T(2,128)}, u32[]{:S(2)}) copy-start(s32[24,2]{0,1:T(2,128)} %param.9) | copy-start | bytes 580
  118.8 51.6 %all-to-all-start.2 = ((bf16[4,2,80,3072]{3,2,1,0:T(8,128)(2,1)}), bf16[4,2,80,3072]{3,2,1,0:T(8,128)(2,1)}, u32[]{:S(2)}, u32[]{:S(2)}) async-start(bf16[4,2,80,3072]{3,2,1,0:T(8,128)(2,1)} %copy.62), calls=%async_computation.2 | async-start | bytes 7864320 | tf_op jit(solution)/shard_map/all_to_all | solution.py:101
  178.2 6.6 %copy-start.10 = (f32[24,2]{0,1:T(2,128)S(1)}, f32[24,2]{0,1:T(2,128)}, u32[]{:S(2)}) copy-start(f32[24,2]{0,1:T(2,128)} %param.10) | copy-start | bytes 580
  180.6 31.3 %all-to-all-start.3 = ((bf16[8,40,1536]{2,1,0:T(8,128)(2,1)}), bf16[8,40,1536]{2,1,0:T(8,128)(2,1)}, u32[]{:S(2)}, u32[]{:S(2)}) async-start(bf16[8,40,1536]{2,1,0:T(8,128)(2,1)} %reshape.124), calls=%async_computation.3 | async-start | bytes 1966080 | tf_op jit(solution)/shard_map/all_to_all | solution.py:104
  184.9 2.3 copy-start.3
  187.8 1.8 copy-start.5
  213.9 16.7 %all-to-all-start.4 = ((bf16[8,20,384]{2,1,0:T(8,128)(2,1)}), bf16[8,20,384]{2,1,0:T(8,128)(2,1)S(1)}, u32[]{:S(2)}, u32[]{:S(2)}) async-start(bf16[8,20,384]{2,1,0:T(8,128)(2,1)} %copy.66), calls=%async_computation.4 | async-start | bytes 294912 | tf_op jit(solution)/shard_map/all_to_all | solution.py:108
  221.0 11.3 %copy-start.1 = (bf16[1,128,3072]{2,1,0:T(8,128)(2,1)S(1)}, bf16[1,128,3072]{2,1,0:T(8,128)(2,1)}, u32[]{:S(2)}) copy-start(bf16[1,128,3072]{2,1,0:T(8,128)(2,1)} %param.12) | copy-start | bytes 2359300

commit v2 on v1

--- a/solution.py
+++ b/solution.py
@@ -35,10 +35,14 @@
     return lax.dot_general(a, b, (dims, ((), ())), preferred_element_type=F32)
 
 
+def dot2(rows, w):
+    return dot(rows[0], w[0], ((1,), (1,))) + dot(rows[1], w[1], ((1,), (1,)))
+
+
 def forward_backward(rows_tok, rows_grad, w_gate, w_up, w_down):
-    pre_gate = dot(rows_tok, w_gate, ((1,), (1,)))
-    pre_up = dot(rows_tok, w_up, ((1,), (1,)))
-    grad_hidden = dot(rows_grad, w_down, ((1,), (1,)))
+    pre_gate = dot2(rows_tok, w_gate)
+    pre_up = dot2(rows_tok, w_up)
+    grad_hidden = dot2(rows_grad, w_down)
     sigmoid_gate = jax.nn.sigmoid(pre_gate)
     activated = pre_gate * sigmoid_gate
     hidden = (activated * pre_up).astype(BF16)
@@ -46,8 +50,11 @@
         grad_hidden * pre_up * sigmoid_gate * (1.0 + pre_gate * (1.0 - sigmoid_gate))
     ).astype(BF16)
     grad_up = (grad_hidden * activated).astype(BF16)
-    out_part = dot(hidden, w_down, ((1,), (0,)))
-    din_part = dot(grad_gate, w_gate, ((1,), (0,))) + dot(grad_up, w_up, ((1,), (0,)))
+    out_part = [dot(hidden, w_down[i], ((1,), (0,))) for i in range(2)]
+    din_part = [
+        dot(grad_gate, w_gate[i], ((1,), (0,))) + dot(grad_up, w_up[i], ((1,), (0,)))
+        for i in range(2)
+    ]
     return hidden, grad_gate, grad_up, out_part, din_part
 
 
@@ -64,45 +71,76 @@
     picked_grad = dot(picks, cotangent, ((1,), (0,)))
     scaled_grad = (picked_grad * slot_gate[:, None]).astype(BF16)
 
-    block = jnp.concatenate([slot_tokens, scaled_grad], axis=0).reshape(4 * C, width // 2)
-    by_z = spread(block, "z").reshape(n_z, 2, C, width)
-    by_z = by_z.transpose(1, 0, 2, 3).reshape(2, n_z * C, width)
-    own = spread(by_z, "x")
-    other = swap(own)
+    share = width // 2
+    tail = width - share
+    block = jnp.concatenate([slot_tokens, scaled_grad], axis=0)
+    n_rows = n_x * n_z * C
 
-    def rows(a, which):
-        return a[:, which].reshape(n_x * n_z * C, width)
+    first = spread(block[:, :share].reshape(4 * C, share // 2), "z").reshape(n_z, 2, C, share)
+    first = first.transpose(1, 0, 2, 3).reshape(2, n_z * C, share)
+    last = spread(block[:, share:].reshape(4 * C, tail // 2), "x").reshape(n_x, 2, C, tail)
+    last = last.transpose(1, 0, 2, 3).reshape(2, n_x * C, tail)
+    first = spread(first, "x")
+    last = lax.all_gather(last, "z", axis=0)
+    first_other, last_other = swap(first), swap(last)
 
-    tok_own, grad_own = rows(own, 0), rows(own, 1)
-    tok_other, grad_other = rows(other, 0), rows(other, 1)
-    hid_b, gg_b, gu_b, out_b, din_b = forward_backward(tok_other, grad_other, w_gate, w_up, w_down)
-    hid_a, gg_a, gu_a, out_a, din_a = forward_backward(tok_own, grad_own, w_gate, w_up, w_down)
+    at_x = lax.broadcasted_iota(jnp.int32, (n_rows, n_rows), 0)
+    at_z = lax.broadcasted_iota(jnp.int32, (n_rows, n_rows), 1)
+    of_z, of_x, of_slot = at_z // (n_x * C), at_z // C % n_x, at_z % C
+    turn = (at_x == of_x * (n_z * C) + of_z * C + of_slot).astype(BF16)
 
-    def pack(out_part, din_part):
+    def rows(head, rest, which):
+        rest = dot(turn, rest[:, which].reshape(n_rows, tail), ((1,), (0,))).astype(BF16)
+        return head[:, which].reshape(n_rows, share), rest
+
+    tok_own, grad_own = rows(first, last, 0), rows(first, last, 1)
+    tok_other, grad_other = rows(first_other, last_other, 0), rows(first_other, last_other, 1)
+    weights = [(w[:, :share], w[:, share:]) for w in (w_gate, w_up, w_down)]
+    hid_b, gg_b, gu_b, out_b, din_b = forward_backward(tok_other, grad_other, *weights)
+    hid_a, gg_a, gu_a, out_a, din_a = forward_backward(tok_own, grad_own, *weights)
+
+    def pack(out_part, din_part, outer):
         return jnp.stack(
-            [
-                out_part.reshape(n_x, n_z * C, width),
-                din_part.reshape(n_x, n_z * C, width),
-            ],
-            axis=1,
+            [a.reshape(outer, n_rows // outer, a.shape[1]) for a in (out_part, din_part)], axis=1
         )
 
-    from_partner = swap(pack(out_b.astype(BF16), din_b.astype(BF16)))
-    chip_sum = (pack(out_a, din_a) + from_partner.astype(F32)).astype(BF16)
+    def chip_sum(mine, partner, outer):
+        partner = swap(pack(*[a.astype(BF16) for a in partner], outer))
+        return (pack(*mine, outer) + partner.astype(F32)).astype(BF16)
+
+    sum_first = chip_sum((out_a[0], din_a[0]), (out_b[0], din_b[0]), n_x)
+
+    def turned(a):
+        return dot(turn, a, ((0,), (0,))).astype(BF16)
+
+    sum_last = chip_sum((out_a[1], din_a[1]), (out_b[1], din_b[1]), 1)[0]
+    sum_last = pack(turned(sum_last[0]), turned(sum_last[1]), n_z)
 
     def weight_grad(left_a, right_a, left_b, right_b):
-        total = dot(left_a, right_a, ((0,), (0,))) + dot(left_b, right_b, ((0,), (0,)))
-        return total.astype(BF16)[None]
+        parts = [
+            dot(left_a, right_a[i], ((0,), (0,))) + dot(left_b, right_b[i], ((0,), (0,)))
+            for i in range(2)
+        ]
+        return jnp.concatenate([p.astype(BF16) for p in parts], axis=1)[None]
 
     grad_w_gate = weight_grad(gg_a, tok_own, gg_b, tok_other)
     grad_w_up = weight_grad(gu_a, tok_own, gu_b, tok_other)
     grad_w_down = weight_grad(hid_a, grad_own, hid_b, grad_other)
 
-    sum_x = lax.all_to_all(chip_sum, "x", split_axis=0, concat_axis=0, tiled=True)
-    sum_x = jnp.sum(sum_x.astype(F32), axis=0).astype(BF16)
-    sum_x = sum_x.reshape(2, n_z, C, width).transpose(1, 0, 2, 3).reshape(n_z, 4 * C, width // 2)
-    sum_z = lax.all_to_all(sum_x, "z", split_axis=0, concat_axis=0, tiled=True)
-    sum_z = jnp.sum(sum_z.astype(F32), axis=0).astype(BF16)
+    def exchange_sum(a, axis):
+        a = lax.all_to_all(a, axis, split_axis=0, concat_axis=0, tiled=True)
+        return jnp.sum(a.astype(F32), axis=0).astype(BF16)
+
+    def by_block(a, count):
+        wide = a.shape[-1]
+        a = a.reshape(2, count, C, wide).transpose(1, 0, 2, 3)
+        return a.reshape(count, 4 * C, wide // 2)
+
+    sum_last = lax.psum_scatter(sum_last, "z", scatter_dimension=0, tiled=False)
+    sum_first = exchange_sum(sum_first, "x")
+    sum_first = exchange_sum(by_block(sum_first, n_z), "z").reshape(2 * C, share)
+    sum_last = exchange_sum(by_block(sum_last, n_x), "x").reshape(2 * C, tail)
+    sum_z = jnp.concatenate([sum_first, sum_last], axis=1)
     part = width // n_y
     to_y = sum_z.reshape(2 * C, n_y, part).transpose(1, 0, 2)
     by_y = lax.all_to_all(to_y, "y", split_axis=0, concat_axis=0, tiled=True)

time: 233 us -> 221 us (0.948)
  blocking collectives: 85 us -> 0 us
  starting transfers between devices: 21.9 us -> 52.1 us
  between operations: 0.99 us -> 14.8 us
  matrix products: 22.5 us -> 34.9 us
  other arithmetic: 8.93 us -> 17.3 us
  local copies, waits for them, and re-layouts: 13.9 us -> 21.5 us
    all_to_all x2 -> x0, blocking collectives: 85 us -> none  [spread(): return lax.all_to_all(copies, axis, split_axis=0, concat_axis=0, tiled=True)]
    all_to_all x2 -> x6, starting transfers between devices: 10.6 us -> 36 us  [the longest x3 21.1 us: spread(): return lax.all_to_all(copies, axis, split_axis=0, concat_axis=0, tiled=True)]
    dot_general x20 -> x44, matrix products: 20.9 us -> 33.3 us  [dot(): return lax.dot_general(a, b, (dims, ((), ())), preferred_element_type=F32)]
    ppermute x2 -> x4, waiting for transfers between devices: 8.06 us -> 0.01 us  [swap(): return lax.ppermute(a, 'c', [(0, 1), (1, 0)])]
    all_to_all x2 -> x6, waiting for transfers between devices: 64.3 us -> 70.9 us  [the longest x3 40.2 us: spread(): return lax.all_to_all(copies, axis, split_axis=0, concat_axis=0, tiled=True)]
    ppermute x2 -> x4, starting transfers between devices: 4.27 us -> 9.04 us  [swap(): return lax.ppermute(a, 'c', [(0, 1), (1, 0)])]
    broadcast_in_dim x0 -> x3, other arithmetic: none -> 3.99 us  [weight_grad(): return jnp.concatenate([p.astype(BF16) for p in parts], axis=1)[None]]
    slice x2 -> x4, local copies, waits for them, and re-layouts: 0.59 us -> 3.6 us  [the longest x2 3.32 us: rows(): return (head[:, which].reshape(n_rows, share), rest)]
  transfers between devices with their start and end apart: 5 -> 13, of which waited for: 5 -> 7; matrix products, arithmetic and copies ran while one was open for 7% -> 26% of each run, Pallas kernels for 0% -> 0%
where the time goes in v2:
time: 221 us; the launch traced here: 220 us
  waiting for transfers between devices  79.2 us (36%)
  starting transfers between devices  52.1 us (24%)
  matrix products  34.9 us (16%)
  local copies, waits for them, and re-layouts  21.5 us (10%)
  other arithmetic  17.3 us (8%)
  between operations  14.8 us (7%)
    all_to_all x3, waiting for transfers between devices, spread(): return lax.all_to_all(copies, axis, split_axis=0, concat_axis=0, tiled=True)  40.2 us
    dot_general x44, matrix products, dot(): return lax.dot_general(a, b, (dims, ((), ())), preferred_element_type=F32)  33.3 us
    all_to_all x3, waiting for transfers between devices, exchange_sum(): a = lax.all_to_all(a, axis, split_axis=0, concat_axis=0, tiled=True)  30.7 us
    all_to_all x3, starting transfers between devices, spread(): return lax.all_to_all(copies, axis, split_axis=0, concat_axis=0, tiled=True)  21.1 us
    all_to_all x3, starting transfers between devices, exchange_sum(): a = lax.all_to_all(a, axis, split_axis=0, concat_axis=0, tiled=True)  14.9 us
    ppermute x4, starting transfers between devices, swap(): return lax.ppermute(a, 'c', [(0, 1), (1, 0)])  9.04 us
    all_to_all x1, waiting for transfers between devices, on_device(): by_y = lax.all_to_all(to_y, 'y', split_axis=0, concat_axis=0, tiled=True)  8.29 us
    all_to_all x1, starting transfers between devices, on_device(): by_y = lax.all_to_all(to_y, 'y', split_axis=0, concat_axis=0, tiled=True)  7.08 us
  transfers between devices with their start and end apart: 13, of which 7 were waited for; matrix products, arithmetic and copies ran while one was open for 26% of the time, Pallas kernels for 0%

profile of v2, /device:TPU:2, one launch (start us, length us, event | category | flops | bytes accessed | tf_op | source)
XLA Modules:
  0.0 219.8 jit_solution(14446520094360544257)
XLA Ops:
  11.1 9.2 %all-to-all-start.2 = ((bf16[4,40,768]{2,1,0:T(8,128)(2,1)}), bf16[4,40,768]{2,1,0:T(8,128)(2,1)S(1)}, u32[]{:S(2)}, u32[]{:S(2)}) async-start(bf16[4,40,768]{2,1,0:T(8,128)(2,1)} %broadcast_in_dim.46), calls=%async_computation.2 | async-start | bytes 491520 | tf_op jit(solution)/shard_map/all_to_all | solution.py:15
  20.3 5.1 %all-to-all-done.2 = bf16[4,40,768]{2,1,0:T(8,128)(2,1)S(1)} async-done(((bf16[4,40,768]{2,1,0:T(8,128)(2,1)}), bf16[4,40,768]{2,1,0:T(8,128)(2,1)S(1)}, u32[]{:S(2)}, u32[]{:S(2)}) %all-to-all-start.2) | async-done | bytes 245792 | tf_op jit(solution)/shard_map/all_to_all | solution.py:15
  26.3 5.9 %all-to-all-start = ((bf16[8,40,768]{2,1,0:T(8,128)(2,1)}), bf16[8,40,768]{2,1,0:T(8,128)(2,1)S(1)}, u32[]{:S(2)}, u32[]{:S(2)}) async-start(bf16[8,40,768]{2,1,0:T(8,128)(2,1)} %broadcast_in_dim.19), calls=%async_computation | async-start | bytes 983040 | tf_op jit(solution)/shard_map/all_to_all | solution.py:15
  33.3 14.2 %all-to-all-done = bf16[8,40,768]{2,1,0:T(8,128)(2,1)S(1)} async-done(((bf16[8,40,768]{2,1,0:T(8,128)(2,1)}), bf16[8,40,768]{2,1,0:T(8,128)(2,1)S(1)}, u32[]{:S(2)}, u32[]{:S(2)}) %all-to-all-start) | async-done | bytes 491552 | tf_op jit(solution)/shard_map/all_to_all | solution.py:15
  49.8 5.9 %all-to-all-start.1 = ((bf16[4,2,80,1536]{3,2,1,0:T(8,128)(2,1)}), bf16[4,2,80,1536]{3,2,1,0:T(8,128)(2,1)}, u32[]{:S(2)}, u32[]{:S(2)}) async-start(bf16[4,2,80,1536]{3,2,1,0:T(8,128)(2,1)} %broadcast_in_dim.21), calls=%async_computation.1 | async-start | bytes 3932160 | tf_op jit(solution)/shard_map/all_to_all | solution.py:15
  56.1 20.8 %all-to-all-done.1 = bf16[4,2,80,1536]{3,2,1,0:T(8,128)(2,1)} async-done(((bf16[4,2,80,1536]{3,2,1,0:T(8,128)(2,1)}), bf16[4,2,80,1536]{3,2,1,0:T(8,128)(2,1)}, u32[]{:S(2)}, u32[]{:S(2)}) %all-to-all-start.1) | async-done | bytes 1966112 | tf_op jit(solution)/shard_map/all_to_all | solution.py:15
  76.9 1.9 collective-permute-start
  83.8 1.8 copy.106
  85.6 2.6 %collective-permute-start.1 = (bf16[8,2,40,1536]{3,2,0,1:T(8,128)(2,1)S(1)}, bf16[8,2,40,1536]{3,2,0,1:T(8,128)(2,1)S(1)}, u32[]{:S(2)}, u32[]{:S(2)}) collective-permute-start(bf16[8,2,40,1536]{3,2,0,1:T(8,128)(2,1)S(1)} %copy.106), channel_id=1, source_target_pairs={{0,32},{32,0},{1,33},{33,1},{2,34},{34,2},{3,35},{35,3},{4,36},{36... | collective-permute-start | bytes 5898248 | tf_op jit(solution)/shard_map/ppermute | solution.py:19
  103.1 1.9 collective-permute-start.3
  112.1 2.6 %collective-permute-start.2 = (bf16[4,2,80,1536]{3,2,1,0:T(8,128)(2,1)}, bf16[4,2,80,1536]{3,2,1,0:T(8,128)(2,1)}, u32[]{:S(2)}, u32[]{:S(2)}) collective-permute-start(bf16[4,2,80,1536]{3,2,1,0:T(8,128)(2,1)} %pad_maximum_fusion), channel_id=1, source_target_pairs={{0,32},{32,0},{1,33},{33,1},{2,34},{34,2},{3,35},{35,3},{4,36},{36... | collective-permute-start | bytes 5898248 | tf_op jit(solution)/shard_map/ppermute | solution.py:19
  119.2 2.6 %fusion.100 = f32[128,1536]{1,0:T(8,128)} fusion(bf16[320,128]{1,0:T(8,128)(2,1)S(1)} %copy-done.31, bf16[320,1536]{1,0:T(8,128)(2,1)} %copy-done.7), kind=kOutput, calls=%fused_computation.169 | convolution fusion | flops 125829120 | bytes 1851392 | tf_op jit(solution)/shard_map/dot_general | solution.py:35
  122.7 3.6 %fusion = bf16[4,2,80,1536]{3,2,1,0:T(8,128)(2,1)} fusion(f32[4,1,80,1536]{3,2,1,0:T(8,128)S(1)} %bitcast.165, f32[4,1,80,1536]{3,2,1,0:T(8,128)S(1)} %bitcast.164, bf16[4,2,80,1536]{3,2,1,0:T(8,128)(2,1)} %collective-permute-done.2), kind=kLoop, calls=%fused_computation.1 | loop fusion | flops 3932160 | bytes 7864320 | tf_op jit(solution)/shard_map/convert_element_type | solution.py:109
  126.2 6.0 %all-to-all-start.3 = ((bf16[4,2,80,1536]{3,2,1,0:T(8,128)(2,1)}), bf16[4,2,80,1536]{3,2,1,0:T(8,128)(2,1)}, u32[]{:S(2)}, u32[]{:S(2)}) async-start(bf16[4,2,80,1536]{3,2,1,0:T(8,128)(2,1)} %fusion), calls=%async_computation.3 | async-start | bytes 3932160 | tf_op jit(solution)/shard_map/all_to_all | solution.py:131
  138.9 17.4 %all-to-all-done.3 = bf16[4,2,80,1536]{3,2,1,0:T(8,128)(2,1)} async-done(((bf16[4,2,80,1536]{3,2,1,0:T(8,128)(2,1)}), bf16[4,2,80,1536]{3,2,1,0:T(8,128)(2,1)}, u32[]{:S(2)}, u32[]{:S(2)}) %all-to-all-start.3) | async-done | bytes 1966112 | tf_op jit(solution)/shard_map/all_to_all | solution.py:131
  156.3 2.8 %reduce_sum.86 = bf16[2,80,1536]{2,1,0:T(8,128)(2,1)} reduce(bf16[4,2,80,1536]{3,2,1,0:T(8,128)(2,1)} %all-to-all-done.3, bf16[]{:T(256)} %constant.64.clone.1), dimensions={0}, to_apply=%region_7.8 | reduce | flops 737280 | bytes 2457602 | tf_op jit(solution)/shard_map/reduce_sum | solution.py:132
  161.6 2.1 reshape.133
  163.6 4.1 %all-to-all-start.4 = ((bf16[8,40,768]{2,1,0:T(8,128)(2,1)}), bf16[8,40,768]{2,1,0:T(8,128)(2,1)}, u32[]{:S(2)}, u32[]{:S(2)}) async-start(bf16[8,40,768]{2,1,0:T(8,128)(2,1)} %reshape.133), calls=%async_computation.4 | async-start | bytes 983040 | tf_op jit(solution)/shard_map/all_to_all | solution.py:131
  169.4 2.1 maximum_bitcast_fusion.2
  174.4 9.7 %all-to-all-done.4 = bf16[8,40,768]{2,1,0:T(8,128)(2,1)} async-done(((bf16[8,40,768]{2,1,0:T(8,128)(2,1)}), bf16[8,40,768]{2,1,0:T(8,128)(2,1)}, u32[]{:S(2)}, u32[]{:S(2)}) %all-to-all-start.4) | async-done | bytes 491552 | tf_op jit(solution)/shard_map/all_to_all | solution.py:131
  184.2 4.8 %all-to-all-start.5 = ((bf16[4,40,768]{2,1,0:T(8,128)(2,1)}), bf16[4,40,768]{2,1,0:T(8,128)(2,1)S(1)}, u32[]{:S(2)}, u32[]{:S(2)}) async-start(bf16[4,40,768]{2,1,0:T(8,128)(2,1)} %reshape.134), calls=%async_computation.6 | async-start | bytes 491520 | tf_op jit(solution)/shard_map/all_to_all | solution.py:131
  190.6 3.5 %all-to-all-done.5 = bf16[4,40,768]{2,1,0:T(8,128)(2,1)S(1)} async-done(((bf16[4,40,768]{2,1,0:T(8,128)(2,1)}), bf16[4,40,768]{2,1,0:T(8,128)(2,1)S(1)}, u32[]{:S(2)}, u32[]{:S(2)}) %all-to-all-start.5) | async-done | bytes 245792 | tf_op jit(solution)/shard_map/all_to_all | solution.py:131
  195.0 7.1 %all-to-all-start.6 = ((bf16[8,20,384]{2,1,0:T(8,128)(2,1)}), bf16[8,20,384]{2,1,0:T(8,128)(2,1)S(1)}, u32[]{:S(2)}, u32[]{:S(2)}) async-start(bf16[8,20,384]{2,1,0:T(8,128)(2,1)} %copy.120), calls=%async_computation.7 | async-start | bytes 294912 | tf_op jit(solution)/shard_map/all_to_all | solution.py:146
  203.0 8.3 %all-to-all-done.6 = bf16[8,20,384]{2,1,0:T(8,128)(2,1)S(1)} async-done(((bf16[8,20,384]{2,1,0:T(8,128)(2,1)}), bf16[8,20,384]{2,1,0:T(8,128)(2,1)S(1)}, u32[]{:S(2)}, u32[]{:S(2)}) %all-to-all-start.6) | async-done | bytes 122912 | tf_op jit(solution)/shard_map/all_to_all | solution.py:146
  (184 shorter events, 58.9 us)
Async XLA Ops:
  11.1 14.4 %all-to-all-start.2 = ((bf16[4,40,768]{2,1,0:T(8,128)(2,1)}), bf16[4,40,768]{2,1,0:T(8,128)(2,1)S(1)}, u32[]{:S(2)}, u32[]{:S(2)}) async-start(bf16[4,40,768]{2,1,0:T(8,128)(2,1)} %broadcast_in_dim.46), calls=%async_computation.2 | async-start | bytes 491520 | tf_op jit(solution)/shard_map/all_to_all | solution.py:15
  26.3 21.3 %all-to-all-start = ((bf16[8,40,768]{2,1,0:T(8,128)(2,1)}), bf16[8,40,768]{2,1,0:T(8,128)(2,1)S(1)}, u32[]{:S(2)}, u32[]{:S(2)}) async-start(bf16[8,40,768]{2,1,0:T(8,128)(2,1)} %broadcast_in_dim.19), calls=%async_computation | async-start | bytes 983040 | tf_op jit(solution)/shard_map/all_to_all | solution.py:15
  32.1 51.6 %all-gather.2.cloned.1.call-start = ((), (), s32[]{:S(2)}) async-start(), calls=%async_computation.8 | async-start | bytes 2211840 | tf_op jit(solution)/shard_map/all_gather | solution.py:84
  49.8 5.9 %copy-start.35 = (s32[24,2]{0,1:T(2,128)S(1)}, s32[24,2]{0,1:T(2,128)}, u32[]{:S(2)}) copy-start(s32[24,2]{0,1:T(2,128)} %param.9) | copy-start | bytes 580
  49.8 6.2 %copy-start.36 = (f32[24,2]{0,1:T(2,128)S(1)}, f32[24,2]{0,1:T(2,128)}, u32[]{:S(2)}) copy-start(f32[24,2]{0,1:T(2,128)} %param.10) | copy-start | bytes 580
  49.8 27.1 %all-to-all-start.1 = ((bf16[4,2,80,1536]{3,2,1,0:T(8,128)(2,1)}), bf16[4,2,80,1536]{3,2,1,0:T(8,128)(2,1)}, u32[]{:S(2)}, u32[]{:S(2)}) async-start(bf16[4,2,80,1536]{3,2,1,0:T(8,128)(2,1)} %broadcast_in_dim.21), calls=%async_computation.1 | async-start | bytes 3932160 | tf_op jit(solution)/shard_map/all_to_all | solution.py:15
  55.7 116.7 %reduce-scatter.2.cloned.1.call-start = ((), (), s32[]{:S(2)}) async-start(), calls=%async_computation.9 | async-start | bytes 2211840 | tf_op jit(solution)/shard_map/reduce_scatter | solution.py:139
  56.0 24.5 %copy-start.2 = (bf16[1,128,3072]{2,1,0:T(8,128)(2,1)S(1)}, bf16[1,128,3072]{2,1,0:T(8,128)(2,1)}, u32[]{:S(2)}) copy-start(bf16[1,128,3072]{2,1,0:T(8,128)(2,1)} %param.11) | copy-start | bytes 2359300
  56.0 25.5 %copy-start.15 = (bf16[1,128,3072]{2,1,0:T(8,128)(2,1)S(1)}, bf16[1,128,3072]{2,1,0:T(8,128)(2,1)}, u32[]{:S(2)}) copy-start(bf16[1,128,3072]{2,1,0:T(8,128)(2,1)} %param.12) | copy-start | bytes 2359300
  76.9 17.9 %collective-permute-start = (bf16[4,2,80,1536]{3,2,1,0:T(8,128)(2,1)}, bf16[4,2,80,1536]{3,2,1,0:T(8,128)(2,1)}, u32[]{:S(2)}, u32[]{:S(2)}) collective-permute-start(bf16[4,2,80,1536]{3,2,1,0:T(8,128)(2,1)} %all-to-all-done.1), channel_id=1, source_target_pairs={{0,32},{32,0},{1,33},{33,1},{2,34},{34,2},{3,35},{35,3},{4,36},{36... | collective-permute-start | bytes 5898248 | tf_op jit(solution)/shard_map/ppermute | solution.py:19
  83.8 4.4 %copy-start.13 = (bf16[8,2,40,1536]{3,2,1,0:T(8,128)(2,1)S(1)}, bf16[8,2,40,1536]{3,2,1,0:T(8,128)(2,1)}, u32[]{:S(2)}) copy-start(bf16[8,2,40,1536]{3,2,1,0:T(8,128)(2,1)} %all-gather.2.cloned.1.call-done) | copy-start | bytes 5898244
  85.6 10.9 %collective-permute-start.1 = (bf16[8,2,40,1536]{3,2,0,1:T(8,128)(2,1)S(1)}, bf16[8,2,40,1536]{3,2,0,1:T(8,128)(2,1)S(1)}, u32[]{:S(2)}, u32[]{:S(2)}) collective-permute-start(bf16[8,2,40,1536]{3,2,0,1:T(8,128)(2,1)S(1)} %copy.106), channel_id=1, source_target_pairs={{0,32},{32,0},{1,33},{33,1},{2,34},{34,2},{3,35},{35,3},{4,36},{36... | collective-permute-start | bytes 5898248 | tf_op jit(solution)/shard_map/ppermute | solution.py:19
  91.5 13.6 %copy-start.28 = (bf16[320,128]{1,0:T(8,128)(2,1)}, bf16[320,128]{1,0:T(8,128)(2,1)S(1)}, u32[]{:S(2)}) copy-start(bf16[320,128]{1,0:T(8,128)(2,1)S(1)} %get-tuple-element.16) | copy-start | bytes 245764
  91.5 14.9 %copy-start.30 = (bf16[320,128]{1,0:T(8,128)(2,1)}, bf16[320,128]{1,0:T(8,128)(2,1)S(1)}, u32[]{:S(2)}) copy-start(bf16[320,128]{1,0:T(8,128)(2,1)S(1)} %get-tuple-element.18) | copy-start | bytes 245764
  91.5 16.1 %copy-start.26 = (bf16[320,128]{1,0:T(8,128)(2,1)}, bf16[320,128]{1,0:T(8,128)(2,1)S(1)}, u32[]{:S(2)}) copy-start(bf16[320,128]{1,0:T(8,128)(2,1)S(1)} %get-tuple-element.17) | copy-start | bytes 245764
  96.5 4.3 %copy-start.11 = (bf16[4,1,80,1536]{3,2,1,0:T(8,128)(2,1)}, bf16[4,1,80,1536]{3,2,1,0:T(8,128)(2,1)S(1)}, u32[]{:S(2)}) copy-start(bf16[4,1,80,1536]{3,2,1,0:T(8,128)(2,1)S(1)} %get-tuple-element.5) | copy-start | bytes 2949124
  103.1 11.5 %collective-permute-start.3 = (bf16[1,2,320,1536]{3,2,1,0:T(8,128)(2,1)S(1)}, bf16[1,2,320,1536]{3,2,1,0:T(8,128)(2,1)S(1)}, u32[]{:S(2)}, u32[]{:S(2)}) collective-permute-start(bf16[1,2,320,1536]{3,2,1,0:T(8,128)(2,1)S(1)} %pad_maximum_fusion.1), channel_id=1, source_target_pairs={{0,32},{32,0},{1,33},{33,1},{2,34},{34,2},{3,35},{35,3},{4,36},{36... | collective-permute-start | bytes 5898248 | tf_op jit(solution)/shard_map/ppermute | solution.py:19
  112.1 10.6 %collective-permute-start.2 = (bf16[4,2,80,1536]{3,2,1,0:T(8,128)(2,1)}, bf16[4,2,80,1536]{3,2,1,0:T(8,128)(2,1)}, u32[]{:S(2)}, u32[]{:S(2)}) collective-permute-start(bf16[4,2,80,1536]{3,2,1,0:T(8,128)(2,1)} %pad_maximum_fusion), channel_id=1, source_target_pairs={{0,32},{32,0},{1,33},{33,1},{2,34},{34,2},{3,35},{35,3},{4,36},{36... | collective-permute-start | bytes 5898248 | tf_op jit(solution)/shard_map/ppermute | solution.py:19
  126.2 6.0 %copy-start.27 = (bf16[320,128]{1,0:T(8,128)(2,1)S(1)}, bf16[320,128]{1,0:T(8,128)(2,1)}, u32[]{:S(2)}) copy-start(bf16[320,128]{1,0:T(8,128)(2,1)} %copy-done.26) | copy-start | bytes 245764
  126.2 30.0 %all-to-all-start.3 = ((bf16[4,2,80,1536]{3,2,1,0:T(8,128)(2,1)}), bf16[4,2,80,1536]{3,2,1,0:T(8,128)(2,1)}, u32[]{:S(2)}, u32[]{:S(2)}) async-start(bf16[4,2,80,1536]{3,2,1,0:T(8,128)(2,1)} %fusion), calls=%async_computation.3 | async-start | bytes 3932160 | tf_op jit(solution)/shard_map/all_to_all | solution.py:131
  163.6 20.5 %all-to-all-start.4 = ((bf16[8,40,768]{2,1,0:T(8,128)(2,1)}), bf16[8,40,768]{2,1,0:T(8,128)(2,1)}, u32[]{:S(2)}, u32[]{:S(2)}) async-start(bf16[8,40,768]{2,1,0:T(8,128)(2,1)} %reshape.133), calls=%async_computation.4 | async-start | bytes 983040 | tf_op jit(solution)/shard_map/all_to_all | solution.py:131
  184.2 9.9 %all-to-all-start.5 = ((bf16[4,40,768]{2,1,0:T(8,128)(2,1)}), bf16[4,40,768]{2,1,0:T(8,128)(2,1)S(1)}, u32[]{:S(2)}, u32[]{:S(2)}) async-start(bf16[4,40,768]{2,1,0:T(8,128)(2,1)} %reshape.134), calls=%async_computation.6 | async-start | bytes 491520 | tf_op jit(solution)/shard_map/all_to_all | solution.py:131
  189.4 23.6 %copy-start.1 = (bf16[24,3072]{1,0:T(8,128)(2,1)S(1)}, bf16[24,3072]{1,0:T(8,128)(2,1)}, u32[]{:S(2)}) copy-start(bf16[24,3072]{1,0:T(8,128)(2,1)} %param.7) | copy-start | bytes 442372
  195.0 16.3 %all-to-all-start.6 = ((bf16[8,20,384]{2,1,0:T(8,128)(2,1)}), bf16[8,20,384]{2,1,0:T(8,128)(2,1)S(1)}, u32[]{:S(2)}, u32[]{:S(2)}) async-start(bf16[8,20,384]{2,1,0:T(8,128)(2,1)} %copy.120), calls=%async_computation.7 | async-start | bytes 294912 | tf_op jit(solution)/shard_map/all_to_all | solution.py:146
  (26 other events, 51.9 us)
Sparse Core Ops, SparseCore 0:
  35.6 44.4 all-gather.1
  118.4 42.8 reduce-scatter.1

commit v3 on v1

--- a/solution.py
+++ b/solution.py
@@ -35,10 +35,41 @@
     return lax.dot_general(a, b, (dims, ((), ())), preferred_element_type=F32)
 
 
-def forward_backward(rows_tok, rows_grad, w_gate, w_up, w_down):
+def shift(a, step):
+    count = lax.axis_size("z")
+    return lax.ppermute(a, "z", [(i, (i + step) % count) for i in range(count)])
+
+
+def ring_gather(block, ahead):
+    up, down, from_below, from_above = block, block, [], []
+    for step in range(ahead):
+        up = shift(up, 1)
+        from_below.append(up)
+        if step < lax.axis_size("z") - 1 - ahead:
+            down = shift(down, -1)
+            from_above.append(down)
+    return jnp.concatenate([block] + from_below + from_above[::-1], axis=0)
+
+
+def ring_sum(parts, ahead):
+    count = len(parts)
+    down, up = parts[ahead], parts[ahead + 1]
+    for step in range(ahead):
+        down = shift(down, -1)
+        if step < ahead - 1:
+            down = (down.astype(F32) + parts[ahead - 1 - step].astype(F32)).astype(BF16)
+        if step < count - 1 - ahead:
+            up = shift(up, 1)
+            if step < count - 2 - ahead:
+                up = (up.astype(F32) + parts[ahead + 2 + step].astype(F32)).astype(BF16)
+    return (parts[0].astype(F32) + down.astype(F32) + up.astype(F32)).astype(BF16)
+
+
+def forward_backward(rows_tok, rows_grad, w_gate, w_up, w_down, turn):
     pre_gate = dot(rows_tok, w_gate, ((1,), (1,)))
     pre_up = dot(rows_tok, w_up, ((1,), (1,)))
     grad_hidden = dot(rows_grad, w_down, ((1,), (1,)))
+    grad_hidden = jnp.dot(turn, grad_hidden, precision=HIGH)
     sigmoid_gate = jax.nn.sigmoid(pre_gate)
     activated = pre_gate * sigmoid_gate
     hidden = (activated * pre_up).astype(BF16)
@@ -47,8 +78,11 @@
     ).astype(BF16)
     grad_up = (grad_hidden * activated).astype(BF16)
     out_part = dot(hidden, w_down, ((1,), (0,)))
-    din_part = dot(grad_gate, w_gate, ((1,), (0,))) + dot(grad_up, w_up, ((1,), (0,)))
-    return hidden, grad_gate, grad_up, out_part, din_part
+    turned = [
+        dot(turn.astype(BF16), a, ((0,), (0,))).astype(BF16) for a in (hidden, grad_gate, grad_up)
+    ]
+    din_part = dot(turned[1], w_gate, ((1,), (0,))) + dot(turned[2], w_up, ((1,), (0,)))
+    return turned[0], grad_gate, grad_up, out_part, din_part
 
 
 def on_device(tokens, cotangent, experts, gate_weights, w_gate, w_up, w_down):
@@ -64,31 +98,30 @@
     picked_grad = dot(picks, cotangent, ((1,), (0,)))
     scaled_grad = (picked_grad * slot_gate[:, None]).astype(BF16)
 
-    block = jnp.concatenate([slot_tokens, scaled_grad], axis=0).reshape(4 * C, width // 2)
-    by_z = spread(block, "z").reshape(n_z, 2, C, width)
-    by_z = by_z.transpose(1, 0, 2, 3).reshape(2, n_z * C, width)
-    own = spread(by_z, "x")
-    other = swap(own)
+    n_rows = n_x * n_z * C
+    quarter = (4 * C, width // 4)
+    tok_own = spread(slot_tokens.reshape(quarter), "z").reshape(n_z * C, width)
+    grad_own = spread(scaled_grad.reshape(quarter), "x").reshape(n_x * C, width)
+    tok_own = spread(tok_own, "x").reshape(n_rows, width)
+    ahead = n_z // 2
+    grad_own = ring_gather(grad_own, ahead)
+    tok_other, grad_other = swap(tok_own), swap(grad_own)
 
-    def rows(a, which):
-        return a[:, which].reshape(n_x * n_z * C, width)
+    at_tok = lax.broadcasted_iota(jnp.int32, (n_rows, n_rows), 0)
+    at_grad = lax.broadcasted_iota(jnp.int32, (n_rows, n_rows), 1)
+    of_z = (lax.axis_index("z") - at_grad // (n_x * C) + n_z) % n_z
+    of_x, of_slot = at_grad // C % n_x, at_grad % C
+    turn = (at_tok == of_x * (n_z * C) + of_z * C + of_slot).astype(F32)
 
-    tok_own, grad_own = rows(own, 0), rows(own, 1)
-    tok_other, grad_other = rows(other, 0), rows(other, 1)
-    hid_b, gg_b, gu_b, out_b, din_b = forward_backward(tok_other, grad_other, w_gate, w_up, w_down)
-    hid_a, gg_a, gu_a, out_a, din_a = forward_backward(tok_own, grad_own, w_gate, w_up, w_down)
+    weights = (w_gate, w_up, w_down, turn)
+    hid_b, gg_b, gu_b, out_b, din_b = forward_backward(tok_other, grad_other, *weights)
+    hid_a, gg_a, gu_a, out_a, din_a = forward_backward(tok_own, grad_own, *weights)
 
-    def pack(out_part, din_part):
-        return jnp.stack(
-            [
-                out_part.reshape(n_x, n_z * C, width),
-                din_part.reshape(n_x, n_z * C, width),
-            ],
-            axis=1,
-        )
+    def chip_sum(mine, partner):
+        return (mine + swap(partner.astype(BF16)).astype(F32)).astype(BF16)
 
-    from_partner = swap(pack(out_b.astype(BF16), din_b.astype(BF16)))
-    chip_sum = (pack(out_a, din_a) + from_partner.astype(F32)).astype(BF16)
+    sum_out = chip_sum(out_a, out_b).reshape(n_x, n_z * C, width)
+    sum_din = chip_sum(din_a, din_b).reshape(n_z, n_x * C, width)
 
     def weight_grad(left_a, right_a, left_b, right_b):
         total = dot(left_a, right_a, ((0,), (0,))) + dot(left_b, right_b, ((0,), (0,)))
@@ -98,11 +131,15 @@
     grad_w_up = weight_grad(gu_a, tok_own, gu_b, tok_other)
     grad_w_down = weight_grad(hid_a, grad_own, hid_b, grad_other)
 
-    sum_x = lax.all_to_all(chip_sum, "x", split_axis=0, concat_axis=0, tiled=True)
-    sum_x = jnp.sum(sum_x.astype(F32), axis=0).astype(BF16)
-    sum_x = sum_x.reshape(2, n_z, C, width).transpose(1, 0, 2, 3).reshape(n_z, 4 * C, width // 2)
-    sum_z = lax.all_to_all(sum_x, "z", split_axis=0, concat_axis=0, tiled=True)
-    sum_z = jnp.sum(sum_z.astype(F32), axis=0).astype(BF16)
+    def exchange_sum(a, axis):
+        a = lax.all_to_all(a, axis, split_axis=0, concat_axis=0, tiled=True)
+        return jnp.sum(a.astype(F32), axis=0).astype(BF16)
+
+    sum_out = exchange_sum(sum_out, "x")
+    sum_din = ring_sum([sum_din[j] for j in range(n_z)], ahead)
+    sum_out = exchange_sum(sum_out.reshape((n_z,) + quarter), "z").reshape(C, width)
+    sum_din = exchange_sum(sum_din.reshape((n_x,) + quarter), "x").reshape(C, width)
+    sum_z = jnp.concatenate([sum_out, sum_din], axis=0)
     part = width // n_y
     to_y = sum_z.reshape(2 * C, n_y, part).transpose(1, 0, 2)
     by_y = lax.all_to_all(to_y, "y", split_axis=0, concat_axis=0, tiled=True)

time: 233 us -> 247 us (1.060)
  blocking collectives: 85 us -> 0 us
  starting transfers between devices: 21.9 us -> 104 us
  matrix products: 22.5 us -> 55.4 us
  waiting for transfers between devices: 79 us -> 50.5 us
  local copies, waits for them, and re-layouts: 13.9 us -> 19.5 us
  other arithmetic: 8.93 us -> 13.8 us
    all_to_all x2 -> x0, blocking collectives: 85 us -> none  [spread(): return lax.all_to_all(copies, axis, split_axis=0, concat_axis=0, tiled=True)]
    ppermute x0 -> x14, starting transfers between devices: none -> 50.3 us  [shift(): return lax.ppermute(a, 'z', [(i, (i + step) % count) for i in range(count)])]
    all_to_all x2 -> x6, waiting for transfers between devices: 64.3 us -> 17.9 us  [the longest x3 9 us: exchange_sum(): a = lax.all_to_all(a, axis, split_axis=0, concat_axis=0, tiled=True)]
    dot_general x20, matrix products: 20.9 us -> 53 us  [dot(): return lax.dot_general(a, b, (dims, ((), ())), preferred_element_type=F32)]
    all_to_all x2 -> x6, starting transfers between devices: 10.6 us -> 38.9 us  [the longest x3 20.1 us: spread(): return lax.all_to_all(copies, axis, split_axis=0, concat_axis=0, tiled=True)]
    ppermute x0 -> x14, waiting for transfers between devices: none -> 25.1 us  [shift(): return lax.ppermute(a, 'z', [(i, (i + step) % count) for i in range(count)])]
    unnamed x22 -> x81, local copies, waits for them, and re-layouts: 1.74 us -> 9.68 us
    ppermute x2 -> x4, waiting for transfers between devices: 8.06 us -> 1.21 us  [swap(): return lax.ppermute(a, 'c', [(0, 1), (1, 0)])]
  transfers between devices with their start and end apart: 5 -> 25, of which waited for: 5 -> 13; matrix products, arithmetic and copies ran while one was open for 7% -> 27% of each run, Pallas kernels for 0% -> 0%
where the time goes in v3:
time: 247 us; the launch traced here: 245 us
  starting transfers between devices  104 us (42%)
  matrix products  55.4 us (22%)
  waiting for transfers between devices  50.5 us (20%)
  local copies, waits for them, and re-layouts  19.5 us (8%)
  other arithmetic  13.8 us (6%)
    dot_general x20, matrix products, dot(): return lax.dot_general(a, b, (dims, ((), ())), preferred_element_type=F32)  53 us
    ppermute x14, starting transfers between devices, shift(): return lax.ppermute(a, 'z', [(i, (i + step) % count) for i in range(count)])  50.3 us
    ppermute x14, waiting for transfers between devices, shift(): return lax.ppermute(a, 'z', [(i, (i + step) % count) for i in range(count)])  25.1 us
    all_to_all x3, starting transfers between devices, spread(): return lax.all_to_all(copies, axis, split_axis=0, concat_axis=0, tiled=True)  20.1 us
    all_to_all x3, starting transfers between devices, exchange_sum(): a = lax.all_to_all(a, axis, split_axis=0, concat_axis=0, tiled=True)  18.8 us
    unnamed x81, local copies, waits for them, and re-layouts  9.68 us
    all_to_all x3, waiting for transfers between devices, exchange_sum(): a = lax.all_to_all(a, axis, split_axis=0, concat_axis=0, tiled=True)  9 us
    all_to_all x3, waiting for transfers between devices, spread(): return lax.all_to_all(copies, axis, split_axis=0, concat_axis=0, tiled=True)  8.9 us
  transfers between devices with their start and end apart: 25, of which 13 were waited for; matrix products, arithmetic and copies ran while one was open for 27% of the time, Pallas kernels for 0%

profile of v3, /device:TPU:2, one launch (start us, length us, event | category | flops | bytes accessed | tf_op | source)
XLA Modules:
  0.0 245.0 jit_solution(8147438520494195442)
XLA Ops:
  4.4 9.2 %all-to-all-start.4 = ((bf16[4,40,768]{2,1,0:T(8,128)(2,1)}), bf16[4,40,768]{2,1,0:T(8,128)(2,1)S(1)}, u32[]{:S(2)}, u32[]{:S(2)}) async-start(bf16[4,40,768]{2,1,0:T(8,128)(2,1)} %broadcast_in_dim.46), calls=%async_computation.4 | async-start | bytes 491520 | tf_op jit(solution)/shard_map/all_to_all | solution.py:15
  14.7 4.0 %all-to-all-done.4 = bf16[4,40,768]{2,1,0:T(8,128)(2,1)S(1)} async-done(((bf16[4,40,768]{2,1,0:T(8,128)(2,1)}), bf16[4,40,768]{2,1,0:T(8,128)(2,1)S(1)}, u32[]{:S(2)}, u32[]{:S(2)}) %all-to-all-start.4) | async-done | bytes 245792 | tf_op jit(solution)/shard_map/all_to_all | solution.py:15
  19.6 5.9 %all-to-all-start = ((bf16[8,40,768]{2,1,0:T(8,128)(2,1)}), bf16[8,40,768]{2,1,0:T(8,128)(2,1)S(1)}, u32[]{:S(2)}, u32[]{:S(2)}) async-start(bf16[8,40,768]{2,1,0:T(8,128)(2,1)} %broadcast_in_dim.19), calls=%async_computation | async-start | bytes 983040 | tf_op jit(solution)/shard_map/all_to_all | solution.py:15
  25.6 5.1 %collective-permute-start.6 = (bf16[40,3072]{1,0:T(8,128)(2,1)S(1)}, bf16[40,3072]{1,0:T(8,128)(2,1)S(1)}, u32[]{:S(2)}, u32[]{:S(2)}) collective-permute-start(bf16[40,3072]{1,0:T(8,128)(2,1)S(1)} %reshape.146), channel_id=1, source_target_pairs={{0,448},{64,0},{128,64},{192,128},{256,192},{320,256},{384,320},{4... | collective-permute-start | bytes 737288 | tf_op jit(solution)/shard_map/ppermute | solution.py:40
  33.4 8.8 %collective-permute-done.6 = bf16[40,3072]{1,0:T(8,128)(2,1)S(1)} collective-permute-done((bf16[40,3072]{1,0:T(8,128)(2,1)S(1)}, bf16[40,3072]{1,0:T(8,128)(2,1)S(1)}, u32[]{:S(2)}, u32[]{:S(2)}) %collective-permute-start.6) | collective-permute-done | bytes 245792 | tf_op jit(solution)/shard_map/ppermute | solution.py:40
  50.4 4.7 %collective-permute-start.8 = (bf16[40,3072]{1,0:T(8,128)(2,1)}, bf16[40,3072]{1,0:T(8,128)(2,1)}, u32[]{:S(2)}, u32[]{:S(2)}) collective-permute-start(bf16[40,3072]{1,0:T(8,128)(2,1)} %collective-permute-done.7), channel_id=1, source_target_pairs={{0,448},{64,0},{128,64},{192,128},{256,192},{320,256},{384,320},{4... | collective-permute-start | bytes 737288 | tf_op jit(solution)/shard_map/ppermute | solution.py:40
  60.6 4.9 %all-to-all-start.1 = ((bf16[4,80,3072]{2,1,0:T(8,128)(2,1)}), bf16[4,80,3072]{2,1,0:T(8,128)(2,1)S(1)}, u32[]{:S(2)}, u32[]{:S(2)}) async-start(bf16[4,80,3072]{2,1,0:T(8,128)(2,1)} %broadcast_in_dim.21), calls=%async_computation.1 | async-start | bytes 3932160 | tf_op jit(solution)/shard_map/all_to_all | solution.py:15
  70.9 4.4 %collective-permute-done.5 = bf16[40,3072]{1,0:T(8,128)(2,1)S(1)} collective-permute-done((bf16[40,3072]{1,0:T(8,128)(2,1)}, bf16[40,3072]{1,0:T(8,128)(2,1)S(1)}, u32[]{:S(2)}, u32[]{:S(2)}) %collective-permute-start.5) | collective-permute-done | bytes 245792 | tf_op jit(solution)/shard_map/ppermute | solution.py:40
  81.9 4.9 %all-to-all-done.1 = bf16[4,80,3072]{2,1,0:T(8,128)(2,1)S(1)} async-done(((bf16[4,80,3072]{2,1,0:T(8,128)(2,1)}), bf16[4,80,3072]{2,1,0:T(8,128)(2,1)S(1)}, u32[]{:S(2)}, u32[]{:S(2)}) %all-to-all-start.1) | async-done | bytes 1966112 | tf_op jit(solution)/shard_map/all_to_all | solution.py:15
  101.9 4.4 %fusion = bf16[320,3072]{1,0:T(8,128)(2,1)} fusion(f32[320,3072]{1,0:T(8,128)} %fusion.9, bf16[320,128]{1,0:T(8,128)(2,1)} %get-tuple-element.16, bf16[1,128,3072]{2,1,0:T(8,128)(2,1)S(1)} %copy-done, s32[320]{0:T(512)} %copy-done.25, s32[320]{0:T(512)S(1)} %get-tuple-element.22, s32[320]{0:T(512)S(1)} %get-tuple-element.21, s32[320]{0:T(512)S(1)} %get-tuple-element.25, ...), kind=kOutput, calls=%fused_computation.2 | convolution fusion | flops 283361280 | bytes 6775236 | tf_op jit(solution)/shard_map/dot_general | solution.py:35
  113.9 4.0 %fusion.8 = f32[320,3072]{1,0:T(8,128)} fusion(bf16[320,128]{1,0:T(8,128)(2,1)} %get-tuple-element.12, bf16[1,128,3072]{2,1,0:T(8,128)(2,1)} %param.11, s32[320]{0:T(512)} %copy-done.25, s32[320]{0:T(512)S(1)} %get-tuple-element.22, s32[320]{0:T(512)S(1)} %get-tuple-element.21, s32[320]{0:T(512)S(1)} %get-tuple-element.25, s32[]{:T(128)S(6)} %axis_index.28, ...), kind=kOutput, calls=%fused_computation.24 | convolution fusion | flops 281395200 | bytes 4809156 | tf_op jit(solution)/shard_map/dot_general | solution.py:35
  123.1 5.0 %add_convert_fusion = bf16[320,3072]{1,0:T(8,128)(2,1)} fusion(bf16[320,3072]{1,0:T(8,128)(2,1)} %collective-permute-done.10, f32[320,3072]{1,0:T(8,128)} %fusion.8, bf16[320,128]{1,0:T(8,128)(2,1)} %get-tuple-element.13, bf16[1,128,3072]{2,1,0:T(8,128)(2,1)S(1)} %copy-done, s32[320]{0:T(512)} %copy-done.25, s32[320]{0:T(512)S(1)} %get-tuple-element.22, ...), kind=kOutput, calls=%fused_computation.4 | convolution fusion | flops 285327360 | bytes 8741316 | tf_op jit(solution)/shard_map/dot_general | solution.py:35
  130.0 4.8 %collective-permute-start.11 = (bf16[40,3072]{1,0:T(8,128)(2,1)}, bf16[40,3072]{1,0:T(8,128)(2,1)}, u32[]{:S(2)}, u32[]{:S(2)}) collective-permute-start(bf16[40,3072]{1,0:T(8,128)(2,1)} %get-tuple-element.9), channel_id=1, source_target_pairs={{0,448},{64,0},{128,64},{192,128},{256,192},{320,256},{384,320},{4... | collective-permute-start | bytes 737288 | tf_op jit(solution)/shard_map/ppermute | solution.py:40
  142.5 5.6 %collective-permute-start.12 = (bf16[40,3072]{1,0:T(8,128)(2,1)}, bf16[40,3072]{1,0:T(8,128)(2,1)}, u32[]{:S(2)}, u32[]{:S(2)}) collective-permute-start(bf16[40,3072]{1,0:T(8,128)(2,1)} %add_convert_fusion.7), channel_id=1, source_target_pairs={{0,448},{64,0},{128,64},{192,128},{256,192},{320,256},{384,320},{4... | collective-permute-start | bytes 737288 | tf_op jit(solution)/shard_map/ppermute | solution.py:40
  155.3 5.5 %collective-permute-start.13 = (bf16[40,3072]{1,0:T(8,128)(2,1)}, bf16[40,3072]{1,0:T(8,128)(2,1)}, u32[]{:S(2)}, u32[]{:S(2)}) collective-permute-start(bf16[40,3072]{1,0:T(8,128)(2,1)} %get-tuple-element.7), channel_id=1, source_target_pairs={{0,448},{64,0},{128,64},{192,128},{256,192},{320,256},{384,320},{4... | collective-permute-start | bytes 737288 | tf_op jit(solution)/shard_map/ppermute | solution.py:40
  166.5 6.0 %all-to-all-start.2 = ((bf16[4,80,3072]{2,1,0:T(8,128)(2,1)}), bf16[4,80,3072]{2,1,0:T(8,128)(2,1)}, u32[]{:S(2)}, u32[]{:S(2)}) async-start(bf16[4,80,3072]{2,1,0:T(8,128)(2,1)} %bitcast.97), calls=%async_computation.2 | async-start | bytes 3932160 | tf_op jit(solution)/shard_map/all_to_all | solution.py:135
  173.9 5.1 %collective-permute-start.14 = (bf16[40,3072]{1,0:T(8,128)(2,1)S(1)}, bf16[40,3072]{1,0:T(8,128)(2,1)S(1)}, u32[]{:S(2)}, u32[]{:S(2)}) collective-permute-start(bf16[40,3072]{1,0:T(8,128)(2,1)S(1)} %get-tuple-element.5), channel_id=1, source_target_pairs={{0,448},{64,0},{128,64},{192,128},{256,192},{320,256},{384,320},{4... | collective-permute-start | bytes 737288 | tf_op jit(solution)/shard_map/ppermute | solution.py:40
  182.9 5.6 %collective-permute-done.17 = bf16[40,3072]{1,0:T(8,128)(2,1)S(1)} collective-permute-done((bf16[40,3072]{1,0:T(8,128)(2,1)S(1)}, bf16[40,3072]{1,0:T(8,128)(2,1)S(1)}, u32[]{:S(2)}, u32[]{:S(2)}) %collective-permute-start.17) | collective-permute-done | bytes 245792 | tf_op jit(solution)/shard_map/ppermute | solution.py:40
  190.3 4.3 %all-to-all-done.2 = bf16[4,80,3072]{2,1,0:T(8,128)(2,1)} async-done(((bf16[4,80,3072]{2,1,0:T(8,128)(2,1)}), bf16[4,80,3072]{2,1,0:T(8,128)(2,1)}, u32[]{:S(2)}, u32[]{:S(2)}) %all-to-all-start.2) | async-done | bytes 1966112 | tf_op jit(solution)/shard_map/all_to_all | solution.py:135
  194.6 4.8 %all-to-all-start.5 = ((bf16[4,40,768]{2,1,0:T(8,128)(2,1)}), bf16[4,40,768]{2,1,0:T(8,128)(2,1)S(1)}, u32[]{:S(2)}, u32[]{:S(2)}) async-start(bf16[4,40,768]{2,1,0:T(8,128)(2,1)} %reshape.147), calls=%async_computation.5 | async-start | bytes 491520 | tf_op jit(solution)/shard_map/all_to_all | solution.py:135
  204.6 8.0 %all-to-all-start.3 = ((bf16[8,40,768]{2,1,0:T(8,128)(2,1)}), bf16[8,40,768]{2,1,0:T(8,128)(2,1)S(1)}, u32[]{:S(2)}, u32[]{:S(2)}) async-start(bf16[8,40,768]{2,1,0:T(8,128)(2,1)} %reshape.145), calls=%async_computation.3 | async-start | bytes 983040 | tf_op jit(solution)/shard_map/all_to_all | solution.py:135
  221.7 4.5 %all-to-all-done.3 = bf16[8,40,768]{2,1,0:T(8,128)(2,1)S(1)} async-done(((bf16[8,40,768]{2,1,0:T(8,128)(2,1)}), bf16[8,40,768]{2,1,0:T(8,128)(2,1)S(1)}, u32[]{:S(2)}, u32[]{:S(2)}) %all-to-all-start.3) | async-done | bytes 491552 | tf_op jit(solution)/shard_map/all_to_all | solution.py:135
  226.9 7.1 %all-to-all-start.6 = ((bf16[8,20,384]{2,1,0:T(8,128)(2,1)}), bf16[8,20,384]{2,1,0:T(8,128)(2,1)S(1)}, u32[]{:S(2)}, u32[]{:S(2)}) async-start(bf16[8,20,384]{2,1,0:T(8,128)(2,1)} %copy.45), calls=%async_computation.6 | async-start | bytes 294912 | tf_op jit(solution)/shard_map/all_to_all | solution.py:145
  237.1 6.2 %all-to-all-done.6 = bf16[8,20,384]{2,1,0:T(8,128)(2,1)S(1)} async-done(((bf16[8,20,384]{2,1,0:T(8,128)(2,1)}), bf16[8,20,384]{2,1,0:T(8,128)(2,1)S(1)}, u32[]{:S(2)}, u32[]{:S(2)}) %all-to-all-start.6) | async-done | bytes 122912 | tf_op jit(solution)/shard_map/all_to_all | solution.py:145
  (175 shorter events, 110.5 us)
Async XLA Ops:
  4.4 14.4 %all-to-all-start.4 = ((bf16[4,40,768]{2,1,0:T(8,128)(2,1)}), bf16[4,40,768]{2,1,0:T(8,128)(2,1)S(1)}, u32[]{:S(2)}, u32[]{:S(2)}) async-start(bf16[4,40,768]{2,1,0:T(8,128)(2,1)} %broadcast_in_dim.46), calls=%async_computation.4 | async-start | bytes 491520 | tf_op jit(solution)/shard_map/all_to_all | solution.py:15
  19.6 39.2 %all-to-all-start = ((bf16[8,40,768]{2,1,0:T(8,128)(2,1)}), bf16[8,40,768]{2,1,0:T(8,128)(2,1)S(1)}, u32[]{:S(2)}, u32[]{:S(2)}) async-start(bf16[8,40,768]{2,1,0:T(8,128)(2,1)} %broadcast_in_dim.19), calls=%async_computation | async-start | bytes 983040 | tf_op jit(solution)/shard_map/all_to_all | solution.py:15
  25.6 16.6 %collective-permute-start.6 = (bf16[40,3072]{1,0:T(8,128)(2,1)S(1)}, bf16[40,3072]{1,0:T(8,128)(2,1)S(1)}, u32[]{:S(2)}, u32[]{:S(2)}) collective-permute-start(bf16[40,3072]{1,0:T(8,128)(2,1)S(1)} %reshape.146), channel_id=1, source_target_pairs={{0,448},{64,0},{128,64},{192,128},{256,192},{320,256},{384,320},{4... | collective-permute-start | bytes 737288 | tf_op jit(solution)/shard_map/ppermute | solution.py:40
  30.8 14.9 %collective-permute-start.2 = (bf16[40,3072]{1,0:T(8,128)(2,1)S(1)}, bf16[40,3072]{1,0:T(8,128)(2,1)S(1)}, u32[]{:S(2)}, u32[]{:S(2)}) collective-permute-start(bf16[40,3072]{1,0:T(8,128)(2,1)S(1)} %reshape.146), channel_id=1, source_target_pairs={{0,64},{64,128},{128,192},{192,256},{256,320},{320,384},{384,448},... | collective-permute-start | bytes 737288 | tf_op jit(solution)/shard_map/ppermute | solution.py:40
  42.2 8.2 %collective-permute-start.7 = (bf16[40,3072]{1,0:T(8,128)(2,1)S(1)}, bf16[40,3072]{1,0:T(8,128)(2,1)}, u32[]{:S(2)}, u32[]{:S(2)}) collective-permute-start(bf16[40,3072]{1,0:T(8,128)(2,1)S(1)} %collective-permute-done.6), channel_id=1, source_target_pairs={{0,448},{64,0},{128,64},{192,128},{256,192},{320,256},{384,320},{4... | collective-permute-start | bytes 737288 | tf_op jit(solution)/shard_map/ppermute | solution.py:40
  45.6 9.5 %collective-permute-start.3 = (bf16[40,3072]{1,0:T(8,128)(2,1)S(1)}, bf16[40,3072]{1,0:T(8,128)(2,1)}, u32[]{:S(2)}, u32[]{:S(2)}) collective-permute-start(bf16[40,3072]{1,0:T(8,128)(2,1)S(1)} %collective-permute-done.2), channel_id=1, source_target_pairs={{0,64},{64,128},{128,192},{192,256},{256,320},{320,384},{384,448},... | collective-permute-start | bytes 737288 | tf_op jit(solution)/shard_map/ppermute | solution.py:40
  50.4 25.5 %collective-permute-start.8 = (bf16[40,3072]{1,0:T(8,128)(2,1)}, bf16[40,3072]{1,0:T(8,128)(2,1)}, u32[]{:S(2)}, u32[]{:S(2)}) collective-permute-start(bf16[40,3072]{1,0:T(8,128)(2,1)} %collective-permute-done.7), channel_id=1, source_target_pairs={{0,448},{64,0},{128,64},{192,128},{256,192},{320,256},{384,320},{4... | collective-permute-start | bytes 737288 | tf_op jit(solution)/shard_map/ppermute | solution.py:40
  55.2 10.4 %collective-permute-start.4 = (bf16[40,3072]{1,0:T(8,128)(2,1)}, bf16[40,3072]{1,0:T(8,128)(2,1)}, u32[]{:S(2)}, u32[]{:S(2)}) collective-permute-start(bf16[40,3072]{1,0:T(8,128)(2,1)} %collective-permute-done.3), channel_id=1, source_target_pairs={{0,64},{64,128},{128,192},{192,256},{256,320},{320,384},{384,448},... | collective-permute-start | bytes 737288 | tf_op jit(solution)/shard_map/ppermute | solution.py:40
  60.6 26.1 %all-to-all-start.1 = ((bf16[4,80,3072]{2,1,0:T(8,128)(2,1)}), bf16[4,80,3072]{2,1,0:T(8,128)(2,1)S(1)}, u32[]{:S(2)}, u32[]{:S(2)}) async-start(bf16[4,80,3072]{2,1,0:T(8,128)(2,1)} %broadcast_in_dim.21), calls=%async_computation.1 | async-start | bytes 3932160 | tf_op jit(solution)/shard_map/all_to_all | solution.py:15
  65.6 9.6 %collective-permute-start.5 = (bf16[40,3072]{1,0:T(8,128)(2,1)}, bf16[40,3072]{1,0:T(8,128)(2,1)S(1)}, u32[]{:S(2)}, u32[]{:S(2)}) collective-permute-start(bf16[40,3072]{1,0:T(8,128)(2,1)} %collective-permute-done.4), channel_id=1, source_target_pairs={{0,64},{64,128},{128,192},{192,256},{256,320},{320,384},{384,448},... | collective-permute-start | bytes 737288 | tf_op jit(solution)/shard_map/ppermute | solution.py:40
  80.0 8.9 %collective-permute-start.9 = (bf16[320,3072]{1,0:T(8,128)(2,1)}, bf16[320,3072]{1,0:T(8,128)(2,1)}, u32[]{:S(2)}, u32[]{:S(2)}) collective-permute-start(bf16[320,3072]{1,0:T(8,128)(2,1)} %constant_dynamic-update-slice_fusion), channel_id=1, source_target_pairs={{0,32},{32,0},{1,33},{33,1},{2,34},{34,2},{3,35},{35,3},{4,36},{36... | collective-permute-start | bytes 5898248 | tf_op jit(solution)/shard_map/ppermute | solution.py:19
  106.4 16.7 %collective-permute-start.10 = (bf16[320,3072]{1,0:T(8,128)(2,1)}, bf16[320,3072]{1,0:T(8,128)(2,1)}, u32[]{:S(2)}, u32[]{:S(2)}) collective-permute-start(bf16[320,3072]{1,0:T(8,128)(2,1)} %fusion), channel_id=1, source_target_pairs={{0,32},{32,0},{1,33},{33,1},{2,34},{34,2},{3,35},{35,3},{4,36},{36... | collective-permute-start | bytes 5898248 | tf_op jit(solution)/shard_map/ppermute | solution.py:19
  120.8 42.2 %collective-permute-start.1 = (bf16[320,3072]{1,0:T(8,128)(2,1)}, bf16[320,3072]{1,0:T(8,128)(2,1)}, u32[]{:S(2)}, u32[]{:S(2)}) collective-permute-start(bf16[320,3072]{1,0:T(8,128)(2,1)} %convolution_convert_fusion), channel_id=1, source_target_pairs={{0,32},{32,0},{1,33},{33,1},{2,34},{34,2},{3,35},{35,3},{4,36},{36... | collective-permute-start | bytes 5898248 | tf_op jit(solution)/shard_map/ppermute | solution.py:19
  130.0 10.7 %collective-permute-start.11 = (bf16[40,3072]{1,0:T(8,128)(2,1)}, bf16[40,3072]{1,0:T(8,128)(2,1)}, u32[]{:S(2)}, u32[]{:S(2)}) collective-permute-start(bf16[40,3072]{1,0:T(8,128)(2,1)} %get-tuple-element.9), channel_id=1, source_target_pairs={{0,448},{64,0},{128,64},{192,128},{256,192},{320,256},{384,320},{4... | collective-permute-start | bytes 737288 | tf_op jit(solution)/shard_map/ppermute | solution.py:40
  137.6 12.0 %collective-permute-start.15 = (bf16[40,3072]{1,0:T(8,128)(2,1)}, bf16[40,3072]{1,0:T(8,128)(2,1)}, u32[]{:S(2)}, u32[]{:S(2)}) collective-permute-start(bf16[40,3072]{1,0:T(8,128)(2,1)} %get-tuple-element.10), channel_id=1, source_target_pairs={{0,64},{64,128},{128,192},{192,256},{256,320},{320,384},{384,448},... | collective-permute-start | bytes 737288 | tf_op jit(solution)/shard_map/ppermute | solution.py:40
  142.5 10.6 %collective-permute-start.12 = (bf16[40,3072]{1,0:T(8,128)(2,1)}, bf16[40,3072]{1,0:T(8,128)(2,1)}, u32[]{:S(2)}, u32[]{:S(2)}) collective-permute-start(bf16[40,3072]{1,0:T(8,128)(2,1)} %add_convert_fusion.7), channel_id=1, source_target_pairs={{0,448},{64,0},{128,64},{192,128},{256,192},{320,256},{384,320},{4... | collective-permute-start | bytes 737288 | tf_op jit(solution)/shard_map/ppermute | solution.py:40
  155.3 17.2 %collective-permute-start.13 = (bf16[40,3072]{1,0:T(8,128)(2,1)}, bf16[40,3072]{1,0:T(8,128)(2,1)}, u32[]{:S(2)}, u32[]{:S(2)}) collective-permute-start(bf16[40,3072]{1,0:T(8,128)(2,1)} %get-tuple-element.7), channel_id=1, source_target_pairs={{0,448},{64,0},{128,64},{192,128},{256,192},{320,256},{384,320},{4... | collective-permute-start | bytes 737288 | tf_op jit(solution)/shard_map/ppermute | solution.py:40
  160.8 11.6 %collective-permute-start.16 = (bf16[40,3072]{1,0:T(8,128)(2,1)}, bf16[40,3072]{1,0:T(8,128)(2,1)}, u32[]{:S(2)}, u32[]{:S(2)}) collective-permute-start(bf16[40,3072]{1,0:T(8,128)(2,1)} %get-tuple-element.8), channel_id=1, source_target_pairs={{0,64},{64,128},{128,192},{192,256},{256,320},{320,384},{384,448},... | collective-permute-start | bytes 737288 | tf_op jit(solution)/shard_map/ppermute | solution.py:40
  166.5 28.1 %all-to-all-start.2 = ((bf16[4,80,3072]{2,1,0:T(8,128)(2,1)}), bf16[4,80,3072]{2,1,0:T(8,128)(2,1)}, u32[]{:S(2)}, u32[]{:S(2)}) async-start(bf16[4,80,3072]{2,1,0:T(8,128)(2,1)} %bitcast.97), calls=%async_computation.2 | async-start | bytes 3932160 | tf_op jit(solution)/shard_map/all_to_all | solution.py:135
  173.9 9.0 %collective-permute-start.14 = (bf16[40,3072]{1,0:T(8,128)(2,1)S(1)}, bf16[40,3072]{1,0:T(8,128)(2,1)S(1)}, u32[]{:S(2)}, u32[]{:S(2)}) collective-permute-start(bf16[40,3072]{1,0:T(8,128)(2,1)S(1)} %get-tuple-element.5), channel_id=1, source_target_pairs={{0,448},{64,0},{128,64},{192,128},{256,192},{320,256},{384,320},{4... | collective-permute-start | bytes 737288 | tf_op jit(solution)/shard_map/ppermute | solution.py:40
  179.0 9.4 %collective-permute-start.17 = (bf16[40,3072]{1,0:T(8,128)(2,1)S(1)}, bf16[40,3072]{1,0:T(8,128)(2,1)S(1)}, u32[]{:S(2)}, u32[]{:S(2)}) collective-permute-start(bf16[40,3072]{1,0:T(8,128)(2,1)S(1)} %get-tuple-element.6), channel_id=1, source_target_pairs={{0,64},{64,128},{128,192},{192,256},{256,320},{320,384},{384,448},... | collective-permute-start | bytes 737288 | tf_op jit(solution)/shard_map/ppermute | solution.py:40
  194.6 10.0 %all-to-all-start.5 = ((bf16[4,40,768]{2,1,0:T(8,128)(2,1)}), bf16[4,40,768]{2,1,0:T(8,128)(2,1)S(1)}, u32[]{:S(2)}, u32[]{:S(2)}) async-start(bf16[4,40,768]{2,1,0:T(8,128)(2,1)} %reshape.147), calls=%async_computation.5 | async-start | bytes 491520 | tf_op jit(solution)/shard_map/all_to_all | solution.py:135
  204.6 21.6 %all-to-all-start.3 = ((bf16[8,40,768]{2,1,0:T(8,128)(2,1)}), bf16[8,40,768]{2,1,0:T(8,128)(2,1)S(1)}, u32[]{:S(2)}, u32[]{:S(2)}) async-start(bf16[8,40,768]{2,1,0:T(8,128)(2,1)} %reshape.145), calls=%async_computation.3 | async-start | bytes 983040 | tf_op jit(solution)/shard_map/all_to_all | solution.py:135
  226.9 16.3 %all-to-all-start.6 = ((bf16[8,20,384]{2,1,0:T(8,128)(2,1)}), bf16[8,20,384]{2,1,0:T(8,128)(2,1)S(1)}, u32[]{:S(2)}, u32[]{:S(2)}) async-start(bf16[8,20,384]{2,1,0:T(8,128)(2,1)} %copy.45), calls=%async_computation.6 | async-start | bytes 294912 | tf_op jit(solution)/shard_map/all_to_all | solution.py:145
  (38 other events, 441.9 us)

commit v4 on v3

--- a/solution.py
+++ b/solution.py
@@ -1,6 +1,8 @@
 import jax
 import jax.numpy as jnp
 from jax import lax
+from jax.experimental import pallas as pl
+from jax.experimental.pallas import tpu as pltpu
 from jax.sharding import Mesh, PartitionSpec as P
 
 C = 10
@@ -35,41 +37,23 @@
     return lax.dot_general(a, b, (dims, ((), ())), preferred_element_type=F32)
 
 
-def shift(a, step):
-    count = lax.axis_size("z")
-    return lax.ppermute(a, "z", [(i, (i + step) % count) for i in range(count)])
-
-
-def ring_gather(block, ahead):
-    up, down, from_below, from_above = block, block, [], []
-    for step in range(ahead):
-        up = shift(up, 1)
-        from_below.append(up)
-        if step < lax.axis_size("z") - 1 - ahead:
-            down = shift(down, -1)
-            from_above.append(down)
-    return jnp.concatenate([block] + from_below + from_above[::-1], axis=0)
-
-
-def ring_sum(parts, ahead):
-    count = len(parts)
-    down, up = parts[ahead], parts[ahead + 1]
-    for step in range(ahead):
-        down = shift(down, -1)
-        if step < ahead - 1:
-            down = (down.astype(F32) + parts[ahead - 1 - step].astype(F32)).astype(BF16)
-        if step < count - 1 - ahead:
-            up = shift(up, 1)
-            if step < count - 2 - ahead:
-                up = (up.astype(F32) + parts[ahead + 2 + step].astype(F32)).astype(BF16)
-    return (parts[0].astype(F32) + down.astype(F32) + up.astype(F32)).astype(BF16)
-
-
-def forward_backward(rows_tok, rows_grad, w_gate, w_up, w_down, turn):
+def layer_kernel(tok_ref, grad_ref, wg_ref, wu_ref, wd_ref, turn_ref, *outs):
+    turned_hidden_ref, grad_gate_ref, grad_up_ref, out_ref, din_ref = outs
+    w_gate, w_up, w_down = wg_ref[...], wu_ref[...], wd_ref[...]
+    turn = turn_ref[...]
+    units = w_gate.shape[0]
+    rows_tok = tok_ref[...]
+    grad_hidden = dot(grad_ref[...], w_down, ((1,), (1,)))
+    high = grad_hidden.astype(BF16)
+    rest = grad_hidden - high.astype(F32)
+    middle = rest.astype(BF16)
+    low = (rest - middle.astype(F32)).astype(BF16)
+    pieces = dot(turn, jnp.concatenate([high, middle, low], axis=1), ((1,), (0,)))
+    grad_hidden = (
+        pieces[:, :units] + pieces[:, units : 2 * units] + pieces[:, 2 * units :]
+    )
     pre_gate = dot(rows_tok, w_gate, ((1,), (1,)))
     pre_up = dot(rows_tok, w_up, ((1,), (1,)))
-    grad_hidden = dot(rows_grad, w_down, ((1,), (1,)))
-    grad_hidden = jnp.dot(turn, grad_hidden, precision=HIGH)
     sigmoid_gate = jax.nn.sigmoid(pre_gate)
     activated = pre_gate * sigmoid_gate
     hidden = (activated * pre_up).astype(BF16)
@@ -77,12 +61,27 @@
         grad_hidden * pre_up * sigmoid_gate * (1.0 + pre_gate * (1.0 - sigmoid_gate))
     ).astype(BF16)
     grad_up = (grad_hidden * activated).astype(BF16)
-    out_part = dot(hidden, w_down, ((1,), (0,)))
-    turned = [
-        dot(turn.astype(BF16), a, ((0,), (0,))).astype(BF16) for a in (hidden, grad_gate, grad_up)
-    ]
-    din_part = dot(turned[1], w_gate, ((1,), (0,))) + dot(turned[2], w_up, ((1,), (0,)))
-    return turned[0], grad_gate, grad_up, out_part, din_part
+    grad_gate_ref[...] = grad_gate
+    grad_up_ref[...] = grad_up
+    turned = dot(turn, jnp.concatenate([hidden, grad_gate, grad_up], axis=1), ((0,), (0,)))
+    turned = turned.astype(BF16)
+    turned_hidden_ref[...] = turned[:, :units]
+    din_part = dot(turned[:, units : 2 * units], w_gate, ((1,), (0,)))
+    din_part += dot(turned[:, 2 * units :], w_up, ((1,), (0,)))
+    din_ref[...] = din_part.astype(BF16)
+    out_ref[...] = dot(hidden, w_down, ((1,), (0,))).astype(BF16)
+
+
+def forward_backward(rows_tok, rows_grad, w_gate, w_up, w_down, turn):
+    n_rows, width = rows_tok.shape
+    narrow = jax.ShapeDtypeStruct((n_rows, w_gate.shape[0]), BF16)
+    wide = jax.ShapeDtypeStruct((n_rows, width), BF16)
+    return pl.pallas_call(
+        layer_kernel,
+        out_shape=(narrow, narrow, narrow, wide, wide),
+        compiler_params=pltpu.CompilerParams(vmem_limit_bytes=40 * 1024 * 1024),
+        name="layer",
+    )(rows_tok, rows_grad, w_gate, w_up, w_down, turn)
 
 
 def on_device(tokens, cotangent, experts, gate_weights, w_gate, w_up, w_down):
@@ -100,28 +99,26 @@
 
     n_rows = n_x * n_z * C
     quarter = (4 * C, width // 4)
+    grad_own = spread(scaled_grad.reshape(quarter), "x").reshape(n_x * C, width)
+    grad_own = lax.all_gather(grad_own, "z", axis=0, tiled=True)
     tok_own = spread(slot_tokens.reshape(quarter), "z").reshape(n_z * C, width)
-    grad_own = spread(scaled_grad.reshape(quarter), "x").reshape(n_x * C, width)
     tok_own = spread(tok_own, "x").reshape(n_rows, width)
-    ahead = n_z // 2
-    grad_own = ring_gather(grad_own, ahead)
     tok_other, grad_other = swap(tok_own), swap(grad_own)
 
     at_tok = lax.broadcasted_iota(jnp.int32, (n_rows, n_rows), 0)
     at_grad = lax.broadcasted_iota(jnp.int32, (n_rows, n_rows), 1)
-    of_z = (lax.axis_index("z") - at_grad // (n_x * C) + n_z) % n_z
-    of_x, of_slot = at_grad // C % n_x, at_grad % C
-    turn = (at_tok == of_x * (n_z * C) + of_z * C + of_slot).astype(F32)
+    of_z, of_x, of_slot = at_grad // (n_x * C), at_grad // C % n_x, at_grad % C
+    turn = (at_tok == of_x * (n_z * C) + of_z * C + of_slot).astype(BF16)
 
     weights = (w_gate, w_up, w_down, turn)
     hid_b, gg_b, gu_b, out_b, din_b = forward_backward(tok_other, grad_other, *weights)
     hid_a, gg_a, gu_a, out_a, din_a = forward_backward(tok_own, grad_own, *weights)
 
     def chip_sum(mine, partner):
-        return (mine + swap(partner.astype(BF16)).astype(F32)).astype(BF16)
+        return (mine.astype(F32) + swap(partner).astype(F32)).astype(BF16)
 
+    sum_din = chip_sum(din_a, din_b)
     sum_out = chip_sum(out_a, out_b).reshape(n_x, n_z * C, width)
-    sum_din = chip_sum(din_a, din_b).reshape(n_z, n_x * C, width)
 
     def weight_grad(left_a, right_a, left_b, right_b):
         total = dot(left_a, right_a, ((0,), (0,))) + dot(left_b, right_b, ((0,), (0,)))
@@ -135,8 +132,8 @@
         a = lax.all_to_all(a, axis, split_axis=0, concat_axis=0, tiled=True)
         return jnp.sum(a.astype(F32), axis=0).astype(BF16)
 
+    sum_din = lax.psum_scatter(sum_din, "z", scatter_dimension=0, tiled=True)
     sum_out = exchange_sum(sum_out, "x")
-    sum_din = ring_sum([sum_din[j] for j in range(n_z)], ahead)
     sum_out = exchange_sum(sum_out.reshape((n_z,) + quarter), "z").reshape(C, width)
     sum_din = exchange_sum(sum_din.reshape((n_x,) + quarter), "x").reshape(C, width)
     sum_z = jnp.concatenate([sum_out, sum_din], axis=0)

time: 247 us -> 197 us (0.80)
  starting transfers between devices: 104 us -> 30.9 us
  blocking collectives: 0 us -> 59.5 us
  matrix products: 55.4 us -> 13.7 us
  between operations: 1.47 us -> 14.3 us
  Pallas kernels: 0 us -> 12.6 us
  local copies, waits for them, and re-layouts: 19.5 us -> 10.5 us
  waiting for transfers between devices: 50.5 us -> 44.1 us
  other arithmetic: 13.8 us -> 10.2 us
    all_to_all x0 -> x3, blocking collectives: none -> 59.5 us  [spread(): return lax.all_to_all(copies, axis, split_axis=0, concat_axis=0, tiled=True)]
    ppermute x14 -> x0, starting transfers between devices: 50.3 us -> none  [shift(): return lax.ppermute(a, 'z', [(i, (i + step) % count) for i in range(count)])]
    dot_general x20 -> x8, matrix products: 53 us -> 12.1 us  [dot(): return lax.dot_general(a, b, (dims, ((), ())), preferred_element_type=F32)]
    ppermute x14 -> x0, waiting for transfers between devices: 25.1 us -> none  [shift(): return lax.ppermute(a, 'z', [(i, (i + step) % count) for i in range(count)])]
    all_to_all x3, waiting for transfers between devices: 9 us -> 33.7 us  [exchange_sum(): a = lax.all_to_all(a, axis, split_axis=0, concat_axis=0, tiled=True)]
    all_to_all x3 -> x0, starting transfers between devices: 20.1 us -> none  [spread(): return lax.all_to_all(copies, axis, split_axis=0, concat_axis=0, tiled=True)]
    pallas_call x0 -> x2, Pallas kernels: none -> 12.6 us  [forward_backward(): pl.pallas_call(layer_kernel, out_shape=(narrow, narrow, narrow, wide, wid...]
    all_to_all x3 -> x0, waiting for transfers between devices: 8.9 us -> none  [spread(): return lax.all_to_all(copies, axis, split_axis=0, concat_axis=0, tiled=True)]
  transfers between devices with their start and end apart: 25 -> 10, of which waited for: 13 -> 6; matrix products, arithmetic and copies ran while one was open for 27% -> 12% of each run, Pallas kernels for 0% -> 2%
where the time goes in v4:
time: 197 us; the launch traced here: 196 us
  blocking collectives  59.5 us (30%)
  waiting for transfers between devices  44.1 us (22%)
  starting transfers between devices  30.9 us (16%)
  between operations  14.3 us (7%)
  matrix products  13.7 us (7%)
  Pallas kernels  12.6 us (6%)
  local copies, waits for them, and re-layouts  10.5 us (5%)
  other arithmetic  10.2 us (5%)
    all_to_all x3, blocking collectives, spread(): return lax.all_to_all(copies, axis, split_axis=0, concat_axis=0, tiled=True)  59.5 us
    all_to_all x3, waiting for transfers between devices, exchange_sum(): a = lax.all_to_all(a, axis, split_axis=0, concat_axis=0, tiled=True)  33.7 us
    all_to_all x3, starting transfers between devices, exchange_sum(): a = lax.all_to_all(a, axis, split_axis=0, concat_axis=0, tiled=True)  14.8 us
    pallas_call x2, Pallas kernels, forward_backward(): pl.pallas_call(layer_kernel, out_shape=(narrow, narrow, narrow, wide, wid...  12.6 us
    dot_general x8, matrix products, dot(): return lax.dot_general(a, b, (dims, ((), ())), preferred_element_type=F32)  12.1 us
    ppermute x4, starting transfers between devices, swap(): return lax.ppermute(a, 'c', [(0, 1), (1, 0)])  8.63 us
    all_to_all x1, starting transfers between devices, on_device(): by_y = lax.all_to_all(to_y, 'y', split_axis=0, concat_axis=0, tiled=True)  7.34 us
    convert_element_type x2, other arithmetic, chip_sum(): return (mine.astype(F32) + swap(partner).astype(F32)).astype(BF16)  6.23 us
  transfers between devices with their start and end apart: 10, of which 6 were waited for; matrix products, arithmetic and copies ran while one was open for 12% of the time, Pallas kernels for 2%

profile of v4, /device:TPU:2, one launch (start us, length us, event | category | flops | bytes accessed | tf_op | source)
XLA Modules:
  0.0 195.9 jit_solution(15766577099429241302)
XLA Ops:
  9.4 13.4 %all_to_all.35 = bf16[4,40,768]{2,1,0:T(8,128)(2,1)S(1)} all-to-all(bf16[4,40,768]{2,1,0:T(8,128)(2,1)S(1)} %broadcast_in_dim.46), channel_id=1, replica_groups=mesh['z'=8,'c'=2,'y'=8,'x'=4] {'x'}, dimensions={0} | all-to-all | bytes 491520 | tf_op jit(solution)/shard_map/all_to_all | solution.py:17
  24.0 22.8 %all_to_all.36 = bf16[8,40,768]{2,1,0:T(8,128)(2,1)S(1)} all-to-all(bf16[8,40,768]{2,1,0:T(8,128)(2,1)S(1)} %broadcast_in_dim.19), channel_id=1, replica_groups=mesh['z'=8,'c'=2,'y'=8,'x'=4] {'z'}, dimensions={0} | all-to-all | bytes 983040 | tf_op jit(solution)/shard_map/all_to_all | solution.py:17
  47.3 23.3 %all_to_all.37 = bf16[4,80,3072]{2,1,0:T(8,128)(2,1)S(1)} all-to-all(bf16[4,80,3072]{2,1,0:T(8,128)(2,1)S(1)} %broadcast_in_dim.21), channel_id=1, replica_groups=mesh['z'=8,'c'=2,'y'=8,'x'=4] {'x'}, dimensions={0} | all-to-all | bytes 3932160 | tf_op jit(solution)/shard_map/all_to_all | solution.py:17
  70.6 1.9 collective-permute-start
  72.5 2.4 %collective-permute-start.1 = (bf16[320,3072]{1,0:T(8,128)(2,1)}, bf16[320,3072]{1,0:T(8,128)(2,1)S(1)}, u32[]{:S(2)}, u32[]{:S(2)}) collective-permute-start(bf16[320,3072]{1,0:T(8,128)(2,1)} %all-gather.2.cloned.1.call-done.grad_ref), channel_id=1, source_target_pairs={{0,32},{32,0},{1,33},{33,1},{2,34},{34,2},{3,35},{35,3},{4,36},{36... | collective-permute-start | bytes 5898248 | tf_op jit(solution)/shard_map/ppermute | solution.py:21
  76.6 2.7 %collective-permute-done.1.grad_ref = bf16[320,3072]{1,0:T(8,128)(2,1)S(1)} collective-permute-done((bf16[320,3072]{1,0:T(8,128)(2,1)}, bf16[320,3072]{1,0:T(8,128)(2,1)S(1)}, u32[]{:S(2)}, u32[]{:S(2)}) %collective-permute-start.1) | collective-permute-done | bytes 1966112 | tf_op jit(solution)/shard_map/ppermute | solution.py:21
  82.1 7.8 %layer.3 = (bf16[320,128]{1,0:T(8,128)(2,1)S(1)}, bf16[320,128]{1,0:T(8,128)(2,1)S(1)}, bf16[320,128]{1,0:T(8,128)(2,1)S(1)}, bf16[320,3072]{1,0:T(8,128)(2,1)}, bf16[320,3072]{1,0:T(8,128)(2,1)S(1)}) custom-call(bf16[320,3072]{1,0:T(8,128)(2,1)} %collective-permute-done.tok_ref, bf16[320,3072]{1,0:T(8,128)(2,1)S(1)} %collective-permute-done.1.grad_ref, ...), custom_call_target="tpu_custom_call" | custom-call | tf_op jit(solution)/shard_map/layer/pallas_call | solution.py:79
  90.0 2.0 %collective-permute-start.3 = (bf16[320,3072]{1,0:T(8,128)(2,1)S(1)}, bf16[320,3072]{1,0:T(8,128)(2,1)S(1)}, u32[]{:S(2)}, u32[]{:S(2)}) collective-permute-start(bf16[320,3072]{1,0:T(8,128)(2,1)S(1)} %get-tuple-element.18), channel_id=1, source_target_pairs={{0,32},{32,0},{1,33},{33,1},{2,34},{34,2},{3,35},{35,3},{4,36},{36... | collective-permute-start | bytes 5898248 | tf_op jit(solution)/shard_map/ppermute | solution.py:21
  92.0 2.3 %collective-permute-start.2 = (bf16[320,3072]{1,0:T(8,128)(2,1)}, bf16[320,3072]{1,0:T(8,128)(2,1)}, u32[]{:S(2)}, u32[]{:S(2)}) collective-permute-start(bf16[320,3072]{1,0:T(8,128)(2,1)} %get-tuple-element.16), channel_id=1, source_target_pairs={{0,32},{32,0},{1,33},{33,1},{2,34},{34,2},{3,35},{35,3},{4,36},{36... | collective-permute-start | bytes 5898248 | tf_op jit(solution)/shard_map/ppermute | solution.py:21
  94.3 4.7 %layer.2 = (bf16[320,128]{1,0:T(8,128)(2,1)S(1)}, bf16[320,128]{1,0:T(8,128)(2,1)S(1)}, bf16[320,128]{1,0:T(8,128)(2,1)S(1)}, bf16[320,3072]{1,0:T(8,128)(2,1)S(1)}, bf16[320,3072]{1,0:T(8,128)(2,1)S(1)}) custom-call(bf16[320,3072]{1,0:T(8,128)(2,1)S(1)} %bitcast.49, bf16[320,3072]{1,0:T(8,128)(2,1)S(1)} %copy-done.1, bf16[128,3072]{1,0:T(8,128)(2,1)S(1)} %bitcast.53, ...), custom_call_target="tpu_custom_call" | custom-call | tf_op jit(solution)/shard_map/layer/pallas_call | solution.py:79
  100.3 2.0 %add_convert_fusion = bf16[320,3072]{1,0:T(8,128)(2,1)} fusion(bf16[320,3072]{1,0:T(8,128)(2,1)S(1)} %collective-permute-done.3, bf16[320,3072]{1,0:T(8,128)(2,1)S(1)} %get-tuple-element.17), kind=kLoop, calls=%fused_computation | loop fusion | flops 3932160 | bytes 5898240 | tf_op jit(solution)/shard_map/convert_element_type | solution.py:118
  102.4 4.2 %add_convert_fusion.1 = bf16[320,3072]{1,0:T(8,128)(2,1)} fusion(bf16[320,3072]{1,0:T(8,128)(2,1)} %collective-permute-done.2, bf16[320,3072]{1,0:T(8,128)(2,1)} %copy-done.10), kind=kLoop, calls=%fused_computation.1 | loop fusion | flops 3932160 | bytes 5898240 | tf_op jit(solution)/shard_map/convert_element_type | solution.py:118
  106.6 6.0 %all-to-all-start.3 = ((bf16[4,80,3072]{2,1,0:T(8,128)(2,1)}), bf16[4,80,3072]{2,1,0:T(8,128)(2,1)}, u32[]{:S(2)}, u32[]{:S(2)}) async-start(bf16[4,80,3072]{2,1,0:T(8,128)(2,1)} %bitcast.58), calls=%async_computation.3 | async-start | bytes 3932160 | tf_op jit(solution)/shard_map/all_to_all | solution.py:132
  114.6 22.2 %all-to-all-done.3 = bf16[4,80,3072]{2,1,0:T(8,128)(2,1)} async-done(((bf16[4,80,3072]{2,1,0:T(8,128)(2,1)}), bf16[4,80,3072]{2,1,0:T(8,128)(2,1)}, u32[]{:S(2)}, u32[]{:S(2)}) %all-to-all-start.3) | async-done | bytes 1966112 | tf_op jit(solution)/shard_map/all_to_all | solution.py:132
  136.8 1.9 reduce_sum.86
  139.8 4.0 %all-to-all-start.4 = ((bf16[8,40,768]{2,1,0:T(8,128)(2,1)}), bf16[8,40,768]{2,1,0:T(8,128)(2,1)S(1)}, u32[]{:S(2)}, u32[]{:S(2)}) async-start(bf16[8,40,768]{2,1,0:T(8,128)(2,1)} %reshape.129), calls=%async_computation.4 | async-start | bytes 983040 | tf_op jit(solution)/shard_map/all_to_all | solution.py:132
  143.8 1.8 fusion.44
  150.5 9.5 %all-to-all-done.4 = bf16[8,40,768]{2,1,0:T(8,128)(2,1)S(1)} async-done(((bf16[8,40,768]{2,1,0:T(8,128)(2,1)}), bf16[8,40,768]{2,1,0:T(8,128)(2,1)S(1)}, u32[]{:S(2)}, u32[]{:S(2)}) %all-to-all-start.4) | async-done | bytes 491552 | tf_op jit(solution)/shard_map/all_to_all | solution.py:132
  160.0 4.8 %all-to-all-start.5 = ((bf16[4,40,768]{2,1,0:T(8,128)(2,1)}), bf16[4,40,768]{2,1,0:T(8,128)(2,1)S(1)}, u32[]{:S(2)}, u32[]{:S(2)}) async-start(bf16[4,40,768]{2,1,0:T(8,128)(2,1)} %reshape.130), calls=%async_computation.6 | async-start | bytes 491520 | tf_op jit(solution)/shard_map/all_to_all | solution.py:132
  164.8 3.0 %fusion.5 = bf16[1,128,3072]{2,1,0:T(8,128)(2,1)} fusion(f32[128,3072]{1,0:T(8,128)S(1)} %copy-done.12, bf16[320,128]{1,0:T(8,128)(2,1)S(1)} %get-tuple-element.20, bf16[320,3072]{1,0:T(8,128)(2,1)} %collective-permute-done.tok_ref), kind=kOutput, calls=%fused_computation.10 | convolution fusion | flops 252444672 | bytes 4407296 | tf_op jit(solution)/shard_map/dot_general | solution.py:37
  168.0 2.0 %all-to-all-done.5 = bf16[4,40,768]{2,1,0:T(8,128)(2,1)S(1)} async-done(((bf16[4,40,768]{2,1,0:T(8,128)(2,1)}), bf16[4,40,768]{2,1,0:T(8,128)(2,1)S(1)}, u32[]{:S(2)}, u32[]{:S(2)}) %all-to-all-start.5) | async-done | bytes 245792 | tf_op jit(solution)/shard_map/all_to_all | solution.py:132
  170.8 7.3 %all-to-all-start.6 = ((bf16[8,20,384]{2,1,0:T(8,128)(2,1)}), bf16[8,20,384]{2,1,0:T(8,128)(2,1)S(1)}, u32[]{:S(2)}, u32[]{:S(2)}) async-start(bf16[8,20,384]{2,1,0:T(8,128)(2,1)} %copy.45), calls=%async_computation.7 | async-start | bytes 294912 | tf_op jit(solution)/shard_map/all_to_all | solution.py:142
  178.1 3.0 %fusion.4 = bf16[1,128,3072]{2,1,0:T(8,128)(2,1)} fusion(f32[128,3072]{1,0:T(8,128)S(1)} %copy-done.11, bf16[320,128]{1,0:T(8,128)(2,1)S(1)} %get-tuple-element.22, bf16[320,3072]{1,0:T(8,128)(2,1)} %collective-permute-done.tok_ref), kind=kOutput, calls=%fused_computation.9 | convolution fusion | flops 252444672 | bytes 4407296 | tf_op jit(solution)/shard_map/dot_general | solution.py:37
  181.1 6.2 %all-to-all-done.6 = bf16[8,20,384]{2,1,0:T(8,128)(2,1)S(1)} async-done(((bf16[8,20,384]{2,1,0:T(8,128)(2,1)}), bf16[8,20,384]{2,1,0:T(8,128)(2,1)S(1)}, u32[]{:S(2)}, u32[]{:S(2)}) %all-to-all-start.6) | async-done | bytes 122912 | tf_op jit(solution)/shard_map/all_to_all | solution.py:142
  (86 shorter events, 20.0 us)
Async XLA Ops:
  7.2 1.9 copy-start
  7.2 16.5 %copy-start.13 = (bf16[24,3072]{1,0:T(8,128)(2,1)S(1)}, bf16[24,3072]{1,0:T(8,128)(2,1)}, u32[]{:S(2)}) copy-start(bf16[24,3072]{1,0:T(8,128)(2,1)} %param.7) | copy-start | bytes 442372
  7.2 65.3 %all-gather.2.cloned.1.call-start = ((), (), s32[]{:S(2)}) async-start(), calls=%async_computation.8 | async-start | bytes 2211840 | tf_op jit(solution)/shard_map/all_gather | solution.py:103
  23.6 125.0 %reduce-scatter.2.cloned.1.call-start = ((), (), s32[]{:S(2)}) async-start(), calls=%async_computation.9 | async-start | bytes 2211840 | tf_op jit(solution)/shard_map/reduce_scatter | solution.py:135
  47.3 32.0 %copy-start.5 = (bf16[1,128,3072]{2,1,0:T(8,128)(2,1)S(1)}, bf16[1,128,3072]{2,1,0:T(8,128)(2,1)}, u32[]{:S(2)}) copy-start(bf16[1,128,3072]{2,1,0:T(8,128)(2,1)} %param.11) | copy-start | bytes 2359300
  70.6 6.0 %collective-permute-start = (bf16[320,3072]{1,0:T(8,128)(2,1)S(1)}, bf16[320,3072]{1,0:T(8,128)(2,1)}, u32[]{:S(2)}, u32[]{:S(2)}) collective-permute-start(bf16[320,3072]{1,0:T(8,128)(2,1)S(1)} %bitcast.48), channel_id=1, source_target_pairs={{0,32},{32,0},{1,33},{33,1},{2,34},{34,2},{3,35},{35,3},{4,36},{36... | collective-permute-start | bytes 5898248 | tf_op jit(solution)/shard_map/ppermute | solution.py:21
  72.5 6.7 %collective-permute-start.1 = (bf16[320,3072]{1,0:T(8,128)(2,1)}, bf16[320,3072]{1,0:T(8,128)(2,1)S(1)}, u32[]{:S(2)}, u32[]{:S(2)}) collective-permute-start(bf16[320,3072]{1,0:T(8,128)(2,1)} %all-gather.2.cloned.1.call-done.grad_ref), channel_id=1, source_target_pairs={{0,32},{32,0},{1,33},{33,1},{2,34},{34,2},{3,35},{35,3},{4,36},{36... | collective-permute-start | bytes 5898248 | tf_op jit(solution)/shard_map/ppermute | solution.py:21
  79.3 10.7 %copy-start.3 = (bf16[320,3072]{1,0:T(8,128)(2,1)}, bf16[320,3072]{1,0:T(8,128)(2,1)S(1)}, u32[]{:S(2)}) copy-start(bf16[320,3072]{1,0:T(8,128)(2,1)S(1)} %collective-permute-done.1.grad_ref) | copy-start | bytes 5898244
  79.3 1.7 copy-start.6
  82.1 12.2 %copy-start.1 = (bf16[320,3072]{1,0:T(8,128)(2,1)S(1)}, bf16[320,3072]{1,0:T(8,128)(2,1)}, u32[]{:S(2)}) copy-start(bf16[320,3072]{1,0:T(8,128)(2,1)} %all-gather.2.cloned.1.call-done.grad_ref) | copy-start | bytes 5898244
  82.1 12.2 %copy-start.7 = (bf16[1,128,3072]{2,1,0:T(8,128)(2,1)S(1)}, bf16[1,128,3072]{2,1,0:T(8,128)(2,1)}, u32[]{:S(2)}) copy-start(bf16[1,128,3072]{2,1,0:T(8,128)(2,1)} %param.12) | copy-start | bytes 2359300
  82.1 12.2 %copy-start.9 = (bf16[1,128,3072]{2,1,0:T(8,128)(2,1)S(1)}, bf16[1,128,3072]{2,1,0:T(8,128)(2,1)}, u32[]{:S(2)}) copy-start(bf16[1,128,3072]{2,1,0:T(8,128)(2,1)} %param.13) | copy-start | bytes 2359300
  90.0 10.4 %collective-permute-start.3 = (bf16[320,3072]{1,0:T(8,128)(2,1)S(1)}, bf16[320,3072]{1,0:T(8,128)(2,1)S(1)}, u32[]{:S(2)}, u32[]{:S(2)}) collective-permute-start(bf16[320,3072]{1,0:T(8,128)(2,1)S(1)} %get-tuple-element.18), channel_id=1, source_target_pairs={{0,32},{32,0},{1,33},{33,1},{2,34},{34,2},{3,35},{35,3},{4,36},{36... | collective-permute-start | bytes 5898248 | tf_op jit(solution)/shard_map/ppermute | solution.py:21
  92.0 10.4 %collective-permute-start.2 = (bf16[320,3072]{1,0:T(8,128)(2,1)}, bf16[320,3072]{1,0:T(8,128)(2,1)}, u32[]{:S(2)}, u32[]{:S(2)}) collective-permute-start(bf16[320,3072]{1,0:T(8,128)(2,1)} %get-tuple-element.16), channel_id=1, source_target_pairs={{0,32},{32,0},{1,33},{33,1},{2,34},{34,2},{3,35},{35,3},{4,36},{36... | collective-permute-start | bytes 5898248 | tf_op jit(solution)/shard_map/ppermute | solution.py:21
  106.6 6.0 %copy-start.14 = (s32[24,2]{0,1:T(2,128)S(1)}, s32[24,2]{0,1:T(2,128)}, u32[]{:S(2)}) copy-start(s32[24,2]{0,1:T(2,128)} %param.9) | copy-start | bytes 580
  106.6 6.2 %copy-start.15 = (f32[24,2]{0,1:T(2,128)S(1)}, f32[24,2]{0,1:T(2,128)}, u32[]{:S(2)}) copy-start(f32[24,2]{0,1:T(2,128)} %param.10) | copy-start | bytes 580
  106.6 30.2 %all-to-all-start.3 = ((bf16[4,80,3072]{2,1,0:T(8,128)(2,1)}), bf16[4,80,3072]{2,1,0:T(8,128)(2,1)}, u32[]{:S(2)}, u32[]{:S(2)}) async-start(bf16[4,80,3072]{2,1,0:T(8,128)(2,1)} %bitcast.58), calls=%async_computation.3 | async-start | bytes 3932160 | tf_op jit(solution)/shard_map/all_to_all | solution.py:132
  139.8 20.2 %all-to-all-start.4 = ((bf16[8,40,768]{2,1,0:T(8,128)(2,1)}), bf16[8,40,768]{2,1,0:T(8,128)(2,1)S(1)}, u32[]{:S(2)}, u32[]{:S(2)}) async-start(bf16[8,40,768]{2,1,0:T(8,128)(2,1)} %reshape.129), calls=%async_computation.4 | async-start | bytes 983040 | tf_op jit(solution)/shard_map/all_to_all | solution.py:132
  143.8 1.8 copy-start.2
  145.6 1.6 copy-start.4
  147.2 17.7 %copy-start.12 = (f32[128,3072]{1,0:T(8,128)S(1)}, f32[128,3072]{1,0:T(8,128)}, u32[]{:S(2)}) copy-start(f32[128,3072]{1,0:T(8,128)} %fusion.43) | copy-start | bytes 4718596
  160.0 10.0 %all-to-all-start.5 = ((bf16[4,40,768]{2,1,0:T(8,128)(2,1)}), bf16[4,40,768]{2,1,0:T(8,128)(2,1)S(1)}, u32[]{:S(2)}, u32[]{:S(2)}) async-start(bf16[4,40,768]{2,1,0:T(8,128)(2,1)} %reshape.130), calls=%async_computation.6 | async-start | bytes 491520 | tf_op jit(solution)/shard_map/all_to_all | solution.py:132
  167.9 10.2 %copy-start.11 = (f32[128,3072]{1,0:T(8,128)S(1)}, f32[128,3072]{1,0:T(8,128)}, u32[]{:S(2)}) copy-start(f32[128,3072]{1,0:T(8,128)} %fusion.44) | copy-start | bytes 4718596
  170.8 16.6 %all-to-all-start.6 = ((bf16[8,20,384]{2,1,0:T(8,128)(2,1)}), bf16[8,20,384]{2,1,0:T(8,128)(2,1)S(1)}, u32[]{:S(2)}, u32[]{:S(2)}) async-start(bf16[8,20,384]{2,1,0:T(8,128)(2,1)} %copy.45), calls=%async_computation.7 | async-start | bytes 294912 | tf_op jit(solution)/shard_map/all_to_all | solution.py:142
  (2 other events, 2.4 us)
Sparse Core Ops, SparseCore 0:
  23.8 44.5 all-gather.1
  102.5 43.3 reduce-scatter.1

commit v5 on v4

--- a/solution.py
+++ b/solution.py
@@ -79,7 +79,7 @@
     return pl.pallas_call(
         layer_kernel,
         out_shape=(narrow, narrow, narrow, wide, wide),
-        compiler_params=pltpu.CompilerParams(vmem_limit_bytes=40 * 1024 * 1024),
+        compiler_params=pltpu.CompilerParams(vmem_limit_bytes=26 * 1024 * 1024),
         name="layer",
     )(rows_tok, rows_grad, w_gate, w_up, w_down, turn)
 
@@ -111,8 +111,9 @@
     turn = (at_tok == of_x * (n_z * C) + of_z * C + of_slot).astype(BF16)
 
     weights = (w_gate, w_up, w_down, turn)
+    hid_a, gg_a, gu_a, out_a, din_a = forward_backward(tok_own, grad_own, *weights)
+    tok_other, grad_other, out_a = lax.optimization_barrier((tok_other, grad_other, out_a))
     hid_b, gg_b, gu_b, out_b, din_b = forward_backward(tok_other, grad_other, *weights)
-    hid_a, gg_a, gu_a, out_a, din_a = forward_backward(tok_own, grad_own, *weights)
 
     def chip_sum(mine, partner):
         return (mine.astype(F32) + swap(partner).astype(F32)).astype(BF16)
@@ -132,10 +133,20 @@
         a = lax.all_to_all(a, axis, split_axis=0, concat_axis=0, tiled=True)
         return jnp.sum(a.astype(F32), axis=0).astype(BF16)
 
+    def turn_sum(a, axis):
+        here = lax.axis_index(axis)
+        count = a.shape[0]
+        total = lax.dynamic_index_in_dim(a, here, keepdims=False).astype(F32)
+        for step in (1, count - 1, *range(2, count - 1)):
+            theirs = lax.dynamic_index_in_dim(a, (here + step) % count, keepdims=False)
+            pairs = [(i, (i + step) % count) for i in range(count)]
+            total += lax.ppermute(theirs, axis, pairs).astype(F32)
+        return total.astype(BF16)
+
     sum_din = lax.psum_scatter(sum_din, "z", scatter_dimension=0, tiled=True)
     sum_out = exchange_sum(sum_out, "x")
     sum_out = exchange_sum(sum_out.reshape((n_z,) + quarter), "z").reshape(C, width)
-    sum_din = exchange_sum(sum_din.reshape((n_x,) + quarter), "x").reshape(C, width)
+    sum_din = turn_sum(sum_din.reshape((n_x,) + quarter), "x").reshape(C, width)
     sum_z = jnp.concatenate([sum_out, sum_din], axis=0)
     part = width // n_y
     to_y = sum_z.reshape(2 * C, n_y, part).transpose(1, 0, 2)

time: 197 us -> 188 us (0.954)
  waiting for transfers between devices: 44.1 us -> 29.5 us
  starting transfers between devices: 30.9 us -> 35.9 us
    all_to_all x3 -> x2, waiting for transfers between devices: 33.7 us -> 20.4 us  [exchange_sum(): a = lax.all_to_all(a, axis, split_axis=0, concat_axis=0, tiled=True)]
    ppermute x0 -> x3, starting transfers between devices: none -> 9.81 us  [turn_sum(): total += lax.ppermute(theirs, axis, pairs).astype(F32)]
    all_to_all x3 -> x2, starting transfers between devices: 14.8 us -> 10 us  [exchange_sum(): a = lax.all_to_all(a, axis, split_axis=0, concat_axis=0, tiled=True)]
  transfers between devices with their start and end apart: 10 -> 12, of which waited for: 6 -> 5; matrix products, arithmetic and copies ran while one was open for 12% -> 12% of each run, Pallas kernels for 2% -> 3%
where the time goes in v5:
time: 188 us; the launch traced here: 187 us
  blocking collectives  59.5 us (32%)
  starting transfers between devices  35.9 us (19%)
  waiting for transfers between devices  29.5 us (16%)
  between operations  14.4 us (8%)
  matrix products  13.7 us (7%)
  Pallas kernels  13.1 us (7%)
  local copies, waits for them, and re-layouts  10.9 us (6%)
  other arithmetic  10.3 us (5%)
    all_to_all x3, blocking collectives, spread(): return lax.all_to_all(copies, axis, split_axis=0, concat_axis=0, tiled=True)  59.5 us
    all_to_all x2, waiting for transfers between devices, exchange_sum(): a = lax.all_to_all(a, axis, split_axis=0, concat_axis=0, tiled=True)  20.4 us
    pallas_call x2, Pallas kernels, forward_backward(): pl.pallas_call(layer_kernel, out_shape=(narrow, narrow, narrow, wide, wid...  13.1 us
    dot_general x8, matrix products, dot(): return lax.dot_general(a, b, (dims, ((), ())), preferred_element_type=F32)  12 us
    all_to_all x2, starting transfers between devices, exchange_sum(): a = lax.all_to_all(a, axis, split_axis=0, concat_axis=0, tiled=True)  10 us
    ppermute x3, starting transfers between devices, turn_sum(): total += lax.ppermute(theirs, axis, pairs).astype(F32)  9.81 us
    ppermute x4, starting transfers between devices, swap(): return lax.ppermute(a, 'c', [(0, 1), (1, 0)])  8.63 us
    all_to_all x1, starting transfers between devices, on_device(): by_y = lax.all_to_all(to_y, 'y', split_axis=0, concat_axis=0, tiled=True)  7.33 us
  transfers between devices with their start and end apart: 12, of which 5 were waited for; matrix products, arithmetic and copies ran while one was open for 12% of the time, Pallas kernels for 3%

profile of v5, /device:TPU:2, one launch (start us, length us, event | category | flops | bytes accessed | tf_op | source)
XLA Modules:
  0.0 187.3 jit_solution(17977036870944532873)
XLA Ops:
  9.4 13.4 %all_to_all.30 = bf16[4,40,768]{2,1,0:T(8,128)(2,1)S(1)} all-to-all(bf16[4,40,768]{2,1,0:T(8,128)(2,1)S(1)} %broadcast_in_dim.46), channel_id=1, replica_groups=mesh['z'=8,'c'=2,'y'=8,'x'=4] {'x'}, dimensions={0} | all-to-all | bytes 491520 | tf_op jit(solution)/shard_map/all_to_all | solution.py:17
  24.0 22.8 %all_to_all.31 = bf16[8,40,768]{2,1,0:T(8,128)(2,1)S(1)} all-to-all(bf16[8,40,768]{2,1,0:T(8,128)(2,1)S(1)} %broadcast_in_dim.19), channel_id=1, replica_groups=mesh['z'=8,'c'=2,'y'=8,'x'=4] {'z'}, dimensions={0} | all-to-all | bytes 983040 | tf_op jit(solution)/shard_map/all_to_all | solution.py:17
  47.3 23.3 %all_to_all.32 = bf16[4,80,3072]{2,1,0:T(8,128)(2,1)S(1)} all-to-all(bf16[4,80,3072]{2,1,0:T(8,128)(2,1)S(1)} %broadcast_in_dim.21), channel_id=1, replica_groups=mesh['z'=8,'c'=2,'y'=8,'x'=4] {'x'}, dimensions={0} | all-to-all | bytes 3932160 | tf_op jit(solution)/shard_map/all_to_all | solution.py:17
  70.6 1.9 %collective-permute-start = (bf16[320,3072]{1,0:T(8,128)(2,1)S(1)}, bf16[320,3072]{1,0:T(8,128)(2,1)}, u32[]{:S(2)}, u32[]{:S(2)}) collective-permute-start(bf16[320,3072]{1,0:T(8,128)(2,1)S(1)} %bitcast.57), channel_id=1, source_target_pairs={{0,32},{32,0},{1,33},{33,1},{2,34},{34,2},{3,35},{35,3},{4,36},{36... | collective-permute-start | bytes 5898248 | tf_op jit(solution)/shard_map/ppermute | solution.py:21
  72.6 2.4 %collective-permute-start.1 = (bf16[320,3072]{1,0:T(8,128)(2,1)}, bf16[320,3072]{1,0:T(8,128)(2,1)S(1)}, u32[]{:S(2)}, u32[]{:S(2)}) collective-permute-start(bf16[320,3072]{1,0:T(8,128)(2,1)} %all-gather.2.cloned.1.call-done.grad_ref), channel_id=1, source_target_pairs={{0,32},{32,0},{1,33},{33,1},{2,34},{34,2},{3,35},{35,3},{4,36},{36... | collective-permute-start | bytes 5898248 | tf_op jit(solution)/shard_map/ppermute | solution.py:21
  78.9 4.7 %layer.2 = (bf16[320,128]{1,0:T(8,128)(2,1)S(1)}, bf16[320,128]{1,0:T(8,128)(2,1)S(1)}, bf16[320,128]{1,0:T(8,128)(2,1)S(1)}, bf16[320,3072]{1,0:T(8,128)(2,1)S(1)}, bf16[320,3072]{1,0:T(8,128)(2,1)S(1)}) custom-call(bf16[320,3072]{1,0:T(8,128)(2,1)S(1)} %bitcast.58, bf16[320,3072]{1,0:T(8,128)(2,1)S(1)} %copy-done.1, bf16[128,3072]{1,0:T(8,128)(2,1)S(1)} %bitcast.61, ...), custom_call_target="tpu_custom_call" | custom-call | tf_op jit(solution)/shard_map/layer/pallas_call | solution.py:79
  85.1 8.4 %layer.3 = (bf16[320,128]{1,0:T(8,128)(2,1)S(1)}, bf16[320,128]{1,0:T(8,128)(2,1)S(1)}, bf16[320,128]{1,0:T(8,128)(2,1)S(1)}, bf16[320,3072]{1,0:T(8,128)(2,1)}, bf16[320,3072]{1,0:T(8,128)(2,1)S(1)}) custom-call(bf16[320,3072]{1,0:T(8,128)(2,1)} %collective-permute-done.tok_ref, bf16[320,3072]{1,0:T(8,128)(2,1)S(1)} %collective-permute-done.1.grad_ref, ...), custom_call_target="tpu_custom_call" | custom-call | tf_op jit(solution)/shard_map/layer/pallas_call | solution.py:79
  93.5 1.9 %collective-permute-start.3 = (bf16[320,3072]{1,0:T(8,128)(2,1)S(1)}, bf16[320,3072]{1,0:T(8,128)(2,1)S(1)}, u32[]{:S(2)}, u32[]{:S(2)}) collective-permute-start(bf16[320,3072]{1,0:T(8,128)(2,1)S(1)} %get-tuple-element.24), channel_id=1, source_target_pairs={{0,32},{32,0},{1,33},{33,1},{2,34},{34,2},{3,35},{35,3},{4,36},{36... | collective-permute-start | bytes 5898248 | tf_op jit(solution)/shard_map/ppermute | solution.py:21
  95.4 2.4 %collective-permute-start.2 = (bf16[320,3072]{1,0:T(8,128)(2,1)}, bf16[320,3072]{1,0:T(8,128)(2,1)}, u32[]{:S(2)}, u32[]{:S(2)}) collective-permute-start(bf16[320,3072]{1,0:T(8,128)(2,1)} %get-tuple-element.22), channel_id=1, source_target_pairs={{0,32},{32,0},{1,33},{33,1},{2,34},{34,2},{3,35},{35,3},{4,36},{36... | collective-permute-start | bytes 5898248 | tf_op jit(solution)/shard_map/ppermute | solution.py:21
  99.3 2.0 %add_convert_fusion = bf16[320,3072]{1,0:T(8,128)(2,1)} fusion(bf16[320,3072]{1,0:T(8,128)(2,1)S(1)} %collective-permute-done.3, bf16[320,3072]{1,0:T(8,128)(2,1)S(1)} %get-tuple-element.23), kind=kLoop, calls=%fused_computation | loop fusion | flops 3932160 | bytes 5898240 | tf_op jit(solution)/shard_map/convert_element_type | solution.py:119
  102.3 4.2 %add_convert_fusion.1 = bf16[320,3072]{1,0:T(8,128)(2,1)} fusion(bf16[320,3072]{1,0:T(8,128)(2,1)} %collective-permute-done.2, bf16[320,3072]{1,0:T(8,128)(2,1)} %copy-done.10), kind=kLoop, calls=%fused_computation.1 | loop fusion | flops 3932160 | bytes 5898240 | tf_op jit(solution)/shard_map/convert_element_type | solution.py:119
  106.5 6.0 %all-to-all-start.3 = ((bf16[4,80,3072]{2,1,0:T(8,128)(2,1)}), bf16[4,80,3072]{2,1,0:T(8,128)(2,1)}, u32[]{:S(2)}, u32[]{:S(2)}) async-start(bf16[4,80,3072]{2,1,0:T(8,128)(2,1)} %bitcast.67), calls=%async_computation.3 | async-start | bytes 3932160 | tf_op jit(solution)/shard_map/all_to_all | solution.py:133
  112.8 1.8 fusion.46
  114.6 1.8 fusion.47
  116.3 20.4 %all-to-all-done.3 = bf16[4,80,3072]{2,1,0:T(8,128)(2,1)} async-done(((bf16[4,80,3072]{2,1,0:T(8,128)(2,1)}), bf16[4,80,3072]{2,1,0:T(8,128)(2,1)}, u32[]{:S(2)}, u32[]{:S(2)}) %all-to-all-start.3) | async-done | bytes 1966112 | tf_op jit(solution)/shard_map/all_to_all | solution.py:133
  136.7 1.9 %reduce_sum.74 = bf16[80,3072]{1,0:T(8,128)(2,1)S(1)} reduce(bf16[4,80,3072]{2,1,0:T(8,128)(2,1)} %all-to-all-done.3, bf16[]{:T(256)} %constant.90.clone.1), dimensions={0}, to_apply=%region_7.8 | reduce | flops 737280 | bytes 2457602 | tf_op jit(solution)/shard_map/reduce_sum | solution.py:134
  139.7 4.0 %all-to-all-start.4 = ((bf16[8,40,768]{2,1,0:T(8,128)(2,1)}), bf16[8,40,768]{2,1,0:T(8,128)(2,1)S(1)}, u32[]{:S(2)}, u32[]{:S(2)}) async-start(bf16[8,40,768]{2,1,0:T(8,128)(2,1)} %reshape.131), calls=%async_computation.4 | async-start | bytes 983040 | tf_op jit(solution)/shard_map/all_to_all | solution.py:133
  147.9 1.9 %collective-permute-start.4 = (bf16[40,768]{1,0:T(8,128)(2,1)S(1)}, bf16[40,768]{1,0:T(8,128)(2,1)S(1)}, u32[]{:S(2)}, u32[]{:S(2)}) collective-permute-start(bf16[40,768]{1,0:T(8,128)(2,1)S(1)} %get-tuple-element.31), channel_id=1, source_target_pairs={{0,1},{1,2},{2,3},{3,0},{4,5},{5,6},{6,7},{7,4},{8,9},{9,10},{10,1... | collective-permute-start | bytes 184328 | tf_op jit(solution)/shard_map/ppermute | solution.py:143
  149.9 5.4 %collective-permute-start.6 = (bf16[40,768]{1,0:T(8,128)(2,1)S(1)}, bf16[40,768]{1,0:T(8,128)(2,1)S(1)}, u32[]{:S(2)}, u32[]{:S(2)}) collective-permute-start(bf16[40,768]{1,0:T(8,128)(2,1)S(1)} %get-tuple-element.32), channel_id=1, source_target_pairs={{0,2},{1,3},{2,0},{3,1},{4,6},{5,7},{6,4},{7,5},{8,10},{9,11},{10,... | collective-permute-start | bytes 184328 | tf_op jit(solution)/shard_map/ppermute | solution.py:143
  155.3 2.5 %collective-permute-start.5 = (bf16[40,768]{1,0:T(8,128)(2,1)S(1)}, bf16[40,768]{1,0:T(8,128)(2,1)S(1)}, u32[]{:S(2)}, u32[]{:S(2)}) collective-permute-start(bf16[40,768]{1,0:T(8,128)(2,1)S(1)} %get-tuple-element.33), channel_id=1, source_target_pairs={{0,3},{1,0},{2,1},{3,2},{4,7},{5,4},{6,5},{7,6},{8,11},{9,8},{10,9... | collective-permute-start | bytes 184328 | tf_op jit(solution)/shard_map/ppermute | solution.py:143
  157.8 3.0 %fusion.4 = bf16[1,128,3072]{2,1,0:T(8,128)(2,1)} fusion(f32[128,3072]{1,0:T(8,128)S(1)} %copy-done.12, bf16[320,128]{1,0:T(8,128)(2,1)S(1)} %get-tuple-element.28, bf16[320,3072]{1,0:T(8,128)(2,1)} %collective-permute-done.tok_ref), kind=kOutput, calls=%fused_computation.9 | convolution fusion | flops 252444672 | bytes 4407296 | tf_op jit(solution)/shard_map/dot_general | solution.py:37
  162.2 7.3 %all-to-all-start.5 = ((bf16[8,20,384]{2,1,0:T(8,128)(2,1)}), bf16[8,20,384]{2,1,0:T(8,128)(2,1)S(1)}, u32[]{:S(2)}, u32[]{:S(2)}) async-start(bf16[8,20,384]{2,1,0:T(8,128)(2,1)} %copy.45), calls=%async_computation.6 | async-start | bytes 294912 | tf_op jit(solution)/shard_map/all_to_all | solution.py:153
  169.5 3.0 %fusion.5 = bf16[1,128,3072]{2,1,0:T(8,128)(2,1)} fusion(f32[128,3072]{1,0:T(8,128)S(1)} %copy-done.11, bf16[320,128]{1,0:T(8,128)(2,1)S(1)} %get-tuple-element.26, bf16[320,3072]{1,0:T(8,128)(2,1)} %collective-permute-done.tok_ref), kind=kOutput, calls=%fused_computation.10 | convolution fusion | flops 252444672 | bytes 4407296 | tf_op jit(solution)/shard_map/dot_general | solution.py:37
  172.5 6.2 %all-to-all-done.5 = bf16[8,20,384]{2,1,0:T(8,128)(2,1)S(1)} async-done(((bf16[8,20,384]{2,1,0:T(8,128)(2,1)}), bf16[8,20,384]{2,1,0:T(8,128)(2,1)S(1)}, u32[]{:S(2)}, u32[]{:S(2)}) %all-to-all-start.5) | async-done | bytes 122912 | tf_op jit(solution)/shard_map/all_to_all | solution.py:153
  (91 shorter events, 20.1 us)
Async XLA Ops:
  7.2 1.9 %copy-start = (bf16[24,3072]{1,0:T(8,128)(2,1)S(1)}, bf16[24,3072]{1,0:T(8,128)(2,1)}, u32[]{:S(2)}) copy-start(bf16[24,3072]{1,0:T(8,128)(2,1)} %param.8) | copy-start | bytes 442372
  7.2 16.5 %copy-start.13 = (bf16[24,3072]{1,0:T(8,128)(2,1)S(1)}, bf16[24,3072]{1,0:T(8,128)(2,1)}, u32[]{:S(2)}) copy-start(bf16[24,3072]{1,0:T(8,128)(2,1)} %param.7) | copy-start | bytes 442372
  7.2 65.4 %all-gather.2.cloned.1.call-start = ((), (), s32[]{:S(2)}) async-start(), calls=%async_computation.7 | async-start | bytes 2211840 | tf_op jit(solution)/shard_map/all_gather | solution.py:103
  23.6 123.2 %reduce-scatter.2.cloned.1.call-start = ((), (), s32[]{:S(2)}) async-start(), calls=%async_computation.8 | async-start | bytes 2211840 | tf_op jit(solution)/shard_map/reduce_scatter | solution.py:146
  47.3 27.8 %copy-start.5 = (bf16[1,128,3072]{2,1,0:T(8,128)(2,1)S(1)}, bf16[1,128,3072]{2,1,0:T(8,128)(2,1)}, u32[]{:S(2)}) copy-start(bf16[1,128,3072]{2,1,0:T(8,128)(2,1)} %param.11) | copy-start | bytes 2359300
  70.6 14.5 %collective-permute-start = (bf16[320,3072]{1,0:T(8,128)(2,1)S(1)}, bf16[320,3072]{1,0:T(8,128)(2,1)}, u32[]{:S(2)}, u32[]{:S(2)}) collective-permute-start(bf16[320,3072]{1,0:T(8,128)(2,1)S(1)} %bitcast.57), channel_id=1, source_target_pairs={{0,32},{32,0},{1,33},{33,1},{2,34},{34,2},{3,35},{35,3},{4,36},{36... | collective-permute-start | bytes 5898248 | tf_op jit(solution)/shard_map/ppermute | solution.py:21
  72.6 12.5 %collective-permute-start.1 = (bf16[320,3072]{1,0:T(8,128)(2,1)}, bf16[320,3072]{1,0:T(8,128)(2,1)S(1)}, u32[]{:S(2)}, u32[]{:S(2)}) collective-permute-start(bf16[320,3072]{1,0:T(8,128)(2,1)} %all-gather.2.cloned.1.call-done.grad_ref), channel_id=1, source_target_pairs={{0,32},{32,0},{1,33},{33,1},{2,34},{34,2},{3,35},{35,3},{4,36},{36... | collective-permute-start | bytes 5898248 | tf_op jit(solution)/shard_map/ppermute | solution.py:21
  78.9 6.1 %copy-start.7 = (bf16[1,128,3072]{2,1,0:T(8,128)(2,1)S(1)}, bf16[1,128,3072]{2,1,0:T(8,128)(2,1)}, u32[]{:S(2)}) copy-start(bf16[1,128,3072]{2,1,0:T(8,128)(2,1)} %param.12) | copy-start | bytes 2359300
  78.9 6.1 %copy-start.9 = (bf16[1,128,3072]{2,1,0:T(8,128)(2,1)S(1)}, bf16[1,128,3072]{2,1,0:T(8,128)(2,1)}, u32[]{:S(2)}) copy-start(bf16[1,128,3072]{2,1,0:T(8,128)(2,1)} %param.13) | copy-start | bytes 2359300
  85.1 8.4 %copy-start.3 = (bf16[320,3072]{1,0:T(8,128)(2,1)}, bf16[320,3072]{1,0:T(8,128)(2,1)S(1)}, u32[]{:S(2)}) copy-start(bf16[320,3072]{1,0:T(8,128)(2,1)S(1)} %collective-permute-done.1.grad_ref) | copy-start | bytes 5898244
  93.5 5.9 %collective-permute-start.3 = (bf16[320,3072]{1,0:T(8,128)(2,1)S(1)}, bf16[320,3072]{1,0:T(8,128)(2,1)S(1)}, u32[]{:S(2)}, u32[]{:S(2)}) collective-permute-start(bf16[320,3072]{1,0:T(8,128)(2,1)S(1)} %get-tuple-element.24), channel_id=1, source_target_pairs={{0,32},{32,0},{1,33},{33,1},{2,34},{34,2},{3,35},{35,3},{4,36},{36... | collective-permute-start | bytes 5898248 | tf_op jit(solution)/shard_map/ppermute | solution.py:21
  95.4 6.9 %collective-permute-start.2 = (bf16[320,3072]{1,0:T(8,128)(2,1)}, bf16[320,3072]{1,0:T(8,128)(2,1)}, u32[]{:S(2)}, u32[]{:S(2)}) collective-permute-start(bf16[320,3072]{1,0:T(8,128)(2,1)} %get-tuple-element.22), channel_id=1, source_target_pairs={{0,32},{32,0},{1,33},{33,1},{2,34},{34,2},{3,35},{35,3},{4,36},{36... | collective-permute-start | bytes 5898248 | tf_op jit(solution)/shard_map/ppermute | solution.py:21
  106.5 6.0 %copy-start.14 = (s32[24,2]{0,1:T(2,128)S(1)}, s32[24,2]{0,1:T(2,128)}, u32[]{:S(2)}) copy-start(s32[24,2]{0,1:T(2,128)} %param.9) | copy-start | bytes 580
  106.5 6.2 %copy-start.15 = (f32[24,2]{0,1:T(2,128)S(1)}, f32[24,2]{0,1:T(2,128)}, u32[]{:S(2)}) copy-start(f32[24,2]{0,1:T(2,128)} %param.10) | copy-start | bytes 580
  106.5 30.2 %all-to-all-start.3 = ((bf16[4,80,3072]{2,1,0:T(8,128)(2,1)}), bf16[4,80,3072]{2,1,0:T(8,128)(2,1)}, u32[]{:S(2)}, u32[]{:S(2)}) async-start(bf16[4,80,3072]{2,1,0:T(8,128)(2,1)} %bitcast.67), calls=%async_computation.3 | async-start | bytes 3932160 | tf_op jit(solution)/shard_map/all_to_all | solution.py:133
  116.3 27.4 %copy-start.2 = (bf16[320,3072]{1,0:T(8,128)(2,1)S(1)}, bf16[320,3072]{1,0:T(8,128)(2,1)}, u32[]{:S(2)}) copy-start(bf16[320,3072]{1,0:T(8,128)(2,1)} %all-gather.2.cloned.1.call-done.grad_ref) | copy-start | bytes 5898244
  139.7 21.1 %all-to-all-start.4 = ((bf16[8,40,768]{2,1,0:T(8,128)(2,1)}), bf16[8,40,768]{2,1,0:T(8,128)(2,1)S(1)}, u32[]{:S(2)}, u32[]{:S(2)}) async-start(bf16[8,40,768]{2,1,0:T(8,128)(2,1)} %reshape.131), calls=%async_computation.4 | async-start | bytes 983040 | tf_op jit(solution)/shard_map/all_to_all | solution.py:133
  143.7 1.6 copy-start.4
  145.3 12.5 %copy-start.12 = (f32[128,3072]{1,0:T(8,128)S(1)}, f32[128,3072]{1,0:T(8,128)}, u32[]{:S(2)}) copy-start(f32[128,3072]{1,0:T(8,128)} %fusion.47) | copy-start | bytes 4718596
  147.9 13.0 %collective-permute-start.4 = (bf16[40,768]{1,0:T(8,128)(2,1)S(1)}, bf16[40,768]{1,0:T(8,128)(2,1)S(1)}, u32[]{:S(2)}, u32[]{:S(2)}) collective-permute-start(bf16[40,768]{1,0:T(8,128)(2,1)S(1)} %get-tuple-element.31), channel_id=1, source_target_pairs={{0,1},{1,2},{2,3},{3,0},{4,5},{5,6},{6,7},{7,4},{8,9},{9,10},{10,1... | collective-permute-start | bytes 184328 | tf_op jit(solution)/shard_map/ppermute | solution.py:143
  149.9 11.1 %collective-permute-start.6 = (bf16[40,768]{1,0:T(8,128)(2,1)S(1)}, bf16[40,768]{1,0:T(8,128)(2,1)S(1)}, u32[]{:S(2)}, u32[]{:S(2)}) collective-permute-start(bf16[40,768]{1,0:T(8,128)(2,1)S(1)} %get-tuple-element.32), channel_id=1, source_target_pairs={{0,2},{1,3},{2,0},{3,1},{4,6},{5,7},{6,4},{7,5},{8,10},{9,11},{10,... | collective-permute-start | bytes 184328 | tf_op jit(solution)/shard_map/ppermute | solution.py:143
  155.3 6.1 %collective-permute-start.5 = (bf16[40,768]{1,0:T(8,128)(2,1)S(1)}, bf16[40,768]{1,0:T(8,128)(2,1)S(1)}, u32[]{:S(2)}, u32[]{:S(2)}) collective-permute-start(bf16[40,768]{1,0:T(8,128)(2,1)S(1)} %get-tuple-element.33), channel_id=1, source_target_pairs={{0,3},{1,0},{2,1},{3,2},{4,7},{5,4},{6,5},{7,6},{8,11},{9,8},{10,9... | collective-permute-start | bytes 184328 | tf_op jit(solution)/shard_map/ppermute | solution.py:143
  160.8 8.7 %copy-start.11 = (f32[128,3072]{1,0:T(8,128)S(1)}, f32[128,3072]{1,0:T(8,128)}, u32[]{:S(2)}) copy-start(f32[128,3072]{1,0:T(8,128)} %fusion.46) | copy-start | bytes 4718596
  162.2 16.6 %all-to-all-start.5 = ((bf16[8,20,384]{2,1,0:T(8,128)(2,1)}), bf16[8,20,384]{2,1,0:T(8,128)(2,1)S(1)}, u32[]{:S(2)}, u32[]{:S(2)}) async-start(bf16[8,20,384]{2,1,0:T(8,128)(2,1)} %copy.45), calls=%async_computation.6 | async-start | bytes 294912 | tf_op jit(solution)/shard_map/all_to_all | solution.py:153
  (4 other events, 5.2 us)
Sparse Core Ops, SparseCore 0:
  23.8 44.5 all-gather.1
  101.5 43.2 reduce-scatter.1

commit v6 on v5

--- a/solution.py
+++ b/solution.py
@@ -37,23 +37,36 @@
     return lax.dot_general(a, b, (dims, ((), ())), preferred_element_type=F32)
 
 
-def layer_kernel(tok_ref, grad_ref, wg_ref, wu_ref, wd_ref, turn_ref, *outs):
-    turned_hidden_ref, grad_gate_ref, grad_up_ref, out_ref, din_ref = outs
-    w_gate, w_up, w_down = wg_ref[...], wu_ref[...], wd_ref[...]
-    turn = turn_ref[...]
+def layer_kernel(*refs):
+    sources, outs, scratch = refs[:6], refs[6:11], refs[11:]
+    turned_hidden_ref, grad_gate_ref, grad_up_ref, out_hbm, din_hbm = outs
+    tok, grad, w_gate, w_up, w_down, turn_ref, out_ref, din_ref, sems = scratch
+    buffers = (tok, grad, w_gate, w_up, w_down, turn_ref)
+    loads = [
+        pltpu.make_async_copy(source, buffer, sems.at[i])
+        for i, (source, buffer) in enumerate(zip(sources, buffers))
+    ]
+    for i in (1, 4, 5, 0, 2, 3):
+        loads[i].start()
     units = w_gate.shape[0]
-    rows_tok = tok_ref[...]
-    grad_hidden = dot(grad_ref[...], w_down, ((1,), (1,)))
+    loads[1].wait()
+    loads[4].wait()
+    grad_hidden = dot(grad[...], w_down[...], ((1,), (1,)))
     high = grad_hidden.astype(BF16)
     rest = grad_hidden - high.astype(F32)
     middle = rest.astype(BF16)
     low = (rest - middle.astype(F32)).astype(BF16)
+    loads[5].wait()
+    turn = turn_ref[...]
     pieces = dot(turn, jnp.concatenate([high, middle, low], axis=1), ((1,), (0,)))
     grad_hidden = (
         pieces[:, :units] + pieces[:, units : 2 * units] + pieces[:, 2 * units :]
     )
-    pre_gate = dot(rows_tok, w_gate, ((1,), (1,)))
-    pre_up = dot(rows_tok, w_up, ((1,), (1,)))
+    loads[0].wait()
+    loads[2].wait()
+    pre_gate = dot(tok[...], w_gate[...], ((1,), (1,)))
+    loads[3].wait()
+    pre_up = dot(tok[...], w_up[...], ((1,), (1,)))
     sigmoid_gate = jax.nn.sigmoid(pre_gate)
     activated = pre_gate * sigmoid_gate
     hidden = (activated * pre_up).astype(BF16)
@@ -66,22 +79,40 @@
     turned = dot(turn, jnp.concatenate([hidden, grad_gate, grad_up], axis=1), ((0,), (0,)))
     turned = turned.astype(BF16)
     turned_hidden_ref[...] = turned[:, :units]
-    din_part = dot(turned[:, units : 2 * units], w_gate, ((1,), (0,)))
-    din_part += dot(turned[:, 2 * units :], w_up, ((1,), (0,)))
+    din_part = dot(turned[:, units : 2 * units], w_gate[...], ((1,), (0,)))
+    din_part += dot(turned[:, 2 * units :], w_up[...], ((1,), (0,)))
     din_ref[...] = din_part.astype(BF16)
-    out_ref[...] = dot(hidden, w_down, ((1,), (0,))).astype(BF16)
+    store_din = pltpu.make_async_copy(din_ref, din_hbm, sems.at[6])
+    store_din.start()
+    out_ref[...] = dot(hidden, w_down[...], ((1,), (0,))).astype(BF16)
+    store_out = pltpu.make_async_copy(out_ref, out_hbm, sems.at[7])
+    store_out.start()
+    store_din.wait()
+    store_out.wait()
 
 
 def forward_backward(rows_tok, rows_grad, w_gate, w_up, w_down, turn):
     n_rows, width = rows_tok.shape
+    operands = (rows_tok, rows_grad, w_gate, w_up, w_down, turn)
+    operands = [pltpu.with_memory_space_constraint(a, pltpu.HBM) for a in operands]
     narrow = jax.ShapeDtypeStruct((n_rows, w_gate.shape[0]), BF16)
-    wide = jax.ShapeDtypeStruct((n_rows, width), BF16)
+    wide = pltpu.HBM((n_rows, width), BF16)
+    in_hbm = pl.BlockSpec(memory_space=pltpu.HBM)
+    in_vmem = pl.BlockSpec(memory_space=pltpu.VMEM)
     return pl.pallas_call(
         layer_kernel,
         out_shape=(narrow, narrow, narrow, wide, wide),
+        in_specs=[in_hbm] * 6,
+        out_specs=(in_vmem, in_vmem, in_vmem, in_hbm, in_hbm),
+        scratch_shapes=[
+            *(pltpu.VMEM(a.shape, BF16) for a in operands),
+            pltpu.VMEM((n_rows, width), BF16),
+            pltpu.VMEM((n_rows, width), BF16),
+            pltpu.SemaphoreType.DMA((8,)),
+        ],
         compiler_params=pltpu.CompilerParams(vmem_limit_bytes=26 * 1024 * 1024),
         name="layer",
-    )(rows_tok, rows_grad, w_gate, w_up, w_down, turn)
+    )(*operands)
 
 
 def on_device(tokens, cotangent, experts, gate_weights, w_gate, w_up, w_down):
@@ -145,6 +176,9 @@
 
     sum_din = lax.psum_scatter(sum_din, "z", scatter_dimension=0, tiled=True)
     sum_out = exchange_sum(sum_out, "x")
+    sum_out, grad_w_gate, grad_w_up, grad_w_down = lax.optimization_barrier(
+        (sum_out, grad_w_gate, grad_w_up, grad_w_down)
+    )
     sum_out = exchange_sum(sum_out.reshape((n_z,) + quarter), "z").reshape(C, width)
     sum_din = turn_sum(sum_din.reshape((n_x,) + quarter), "x").reshape(C, width)
     sum_z = jnp.concatenate([sum_out, sum_din], axis=0)

time: 188 us -> 190 us (1.011)
  Pallas kernels: 13.1 us -> 19.1 us
  local copies, waits for them, and re-layouts: 10.9 us -> 7.78 us
  matrix products: 13.7 us -> 11.4 us
    pallas_call x2, Pallas kernels: 13.1 us -> 19.1 us  [forward_backward(): pl.pallas_call(layer_kernel, out_shape=(narrow, narrow, narrow, wide, wid...]
    all_to_all x2, waiting for transfers between devices: 20.4 us -> 17.1 us  [exchange_sum(): a = lax.all_to_all(a, axis, split_axis=0, concat_axis=0, tiled=True)]
    unnamed x32 -> x22, local copies, waits for them, and re-layouts: 6.17 us -> 3.07 us
    all_to_all x1, waiting for transfers between devices: 6.21 us -> 9.25 us  [on_device(): by_y = lax.all_to_all(to_y, 'y', split_axis=0, concat_axis=0, tiled=True)]
    dot_general x8, matrix products: 12 us -> 9.74 us  [dot(): return lax.dot_general(a, b, (dims, ((), ())), preferred_element_type=F32)]
  transfers between devices with their start and end apart: 12 -> 12, of which waited for: 5 -> 6; matrix products, arithmetic and copies ran while one was open for 12% -> 11% of each run, Pallas kernels for 3% -> 5%
where the time goes in v6:
time: 190 us; the launch traced here: 189 us
  blocking collectives  59.4 us (31%)
  starting transfers between devices  36.2 us (19%)
  waiting for transfers between devices  30.1 us (16%)
  Pallas kernels  19.1 us (10%)
  between operations  14.4 us (8%)
  matrix products  11.4 us (6%)
  other arithmetic  10.3 us (5%)
  local copies, waits for them, and re-layouts  7.78 us (4%)
    all_to_all x3, blocking collectives, spread(): return lax.all_to_all(copies, axis, split_axis=0, concat_axis=0, tiled=True)  59.4 us
    pallas_call x2, Pallas kernels, forward_backward(): pl.pallas_call(layer_kernel, out_shape=(narrow, narrow, narrow, wide, wid...  19.1 us
    all_to_all x2, waiting for transfers between devices, exchange_sum(): a = lax.all_to_all(a, axis, split_axis=0, concat_axis=0, tiled=True)  17.1 us
    ppermute x3, starting transfers between devices, turn_sum(): total += lax.ppermute(theirs, axis, pairs).astype(F32)  10.3 us
    all_to_all x2, starting transfers between devices, exchange_sum(): a = lax.all_to_all(a, axis, split_axis=0, concat_axis=0, tiled=True)  9.95 us
    dot_general x8, matrix products, dot(): return lax.dot_general(a, b, (dims, ((), ())), preferred_element_type=F32)  9.74 us
    all_to_all x1, waiting for transfers between devices, on_device(): by_y = lax.all_to_all(to_y, 'y', split_axis=0, concat_axis=0, tiled=True)  9.25 us
    ppermute x4, starting transfers between devices, swap(): return lax.ppermute(a, 'c', [(0, 1), (1, 0)])  8.64 us
  transfers between devices with their start and end apart: 12, of which 6 were waited for; matrix products, arithmetic and copies ran while one was open for 11% of the time, Pallas kernels for 5%

profile of v6, /device:TPU:2, one launch (start us, length us, event | category | flops | bytes accessed | tf_op | source)
XLA Modules:
  0.0 188.7 jit_solution(16892088474366666430)
XLA Ops:
  9.4 13.4 %all_to_all.30 = bf16[4,40,768]{2,1,0:T(8,128)(2,1)S(1)} all-to-all(bf16[4,40,768]{2,1,0:T(8,128)(2,1)S(1)} %broadcast_in_dim.46), channel_id=1, replica_groups=mesh['z'=8,'c'=2,'y'=8,'x'=4] {'x'}, dimensions={0} | all-to-all | bytes 491520 | tf_op jit(solution)/shard_map/all_to_all | solution.py:17
  24.0 22.8 %all_to_all.31 = bf16[8,40,768]{2,1,0:T(8,128)(2,1)S(1)} all-to-all(bf16[8,40,768]{2,1,0:T(8,128)(2,1)S(1)} %broadcast_in_dim.19), channel_id=1, replica_groups=mesh['z'=8,'c'=2,'y'=8,'x'=4] {'z'}, dimensions={0} | all-to-all | bytes 983040 | tf_op jit(solution)/shard_map/all_to_all | solution.py:17
  47.3 23.2 %all_to_all.32 = bf16[4,80,3072]{2,1,0:T(8,128)(2,1)S(1)} all-to-all(bf16[4,80,3072]{2,1,0:T(8,128)(2,1)S(1)} %broadcast_in_dim.21), channel_id=1, replica_groups=mesh['z'=8,'c'=2,'y'=8,'x'=4] {'x'}, dimensions={0} | all-to-all | bytes 3932160 | tf_op jit(solution)/shard_map/all_to_all | solution.py:17
  70.5 1.9 %collective-permute-start = (bf16[320,3072]{1,0:T(8,128)(2,1)S(1)}, bf16[320,3072]{1,0:T(8,128)(2,1)}, u32[]{:S(2)}, u32[]{:S(2)}) collective-permute-start(bf16[320,3072]{1,0:T(8,128)(2,1)S(1)} %bitcast.57), channel_id=1, source_target_pairs={{0,32},{32,0},{1,33},{33,1},{2,34},{34,2},{3,35},{35,3},{4,36},{36... | collective-permute-start | bytes 5898248 | tf_op jit(solution)/shard_map/ppermute | solution.py:21
  72.4 2.4 %collective-permute-start.1 = (bf16[320,3072]{1,0:T(8,128)(2,1)}, bf16[320,3072]{1,0:T(8,128)(2,1)S(1)}, u32[]{:S(2)}, u32[]{:S(2)}) collective-permute-start(bf16[320,3072]{1,0:T(8,128)(2,1)} %all-gather.2.cloned.1.call-done.refs_1_), channel_id=1, source_target_pairs={{0,32},{32,0},{1,33},{33,1},{2,34},{34,2},{3,35},{35,3},{4,36},{36... | collective-permute-start | bytes 5898248 | tf_op jit(solution)/shard_map/ppermute | solution.py:21
  75.6 9.5 %layer.2 = (bf16[320,128]{1,0:T(8,128)(2,1)S(1)}, bf16[320,128]{1,0:T(8,128)(2,1)S(1)}, bf16[320,128]{1,0:T(8,128)(2,1)S(1)}, bf16[320,3072]{1,0:T(8,128)(2,1)}, bf16[320,3072]{1,0:T(8,128)(2,1)}) custom-call(bf16[320,3072]{1,0:T(8,128)(2,1)} %bitcast.58, bf16[320,3072]{1,0:T(8,128)(2,1)} %all-gather.2.cloned.1.call-done.refs_1_, ...), custom_call_target="tpu_custom_call" | custom-call | tf_op jit(solution)/shard_map/layer/pallas_call | solution.py:102
  86.5 9.6 %layer.3 = (bf16[320,128]{1,0:T(8,128)(2,1)S(1)}, bf16[320,128]{1,0:T(8,128)(2,1)S(1)}, bf16[320,128]{1,0:T(8,128)(2,1)S(1)}, bf16[320,3072]{1,0:T(8,128)(2,1)}, bf16[320,3072]{1,0:T(8,128)(2,1)}) custom-call(bf16[320,3072]{1,0:T(8,128)(2,1)} %collective-permute-done.refs_0_, bf16[320,3072]{1,0:T(8,128)(2,1)} %copy-done.4, bf16[128,3072]{1,0:T(8,128)(2,1)} %bitcast.63, ...), custom_call_target="tpu_custom_call" | custom-call | tf_op jit(solution)/shard_map/layer/pallas_call | solution.py:102
  96.0 1.9 %collective-permute-start.3 = (bf16[320,3072]{1,0:T(8,128)(2,1)}, bf16[320,3072]{1,0:T(8,128)(2,1)S(1)}, u32[]{:S(2)}, u32[]{:S(2)}) collective-permute-start(bf16[320,3072]{1,0:T(8,128)(2,1)} %get-tuple-element.35), channel_id=1, source_target_pairs={{0,32},{32,0},{1,33},{33,1},{2,34},{34,2},{3,35},{35,3},{4,36},{36... | collective-permute-start | bytes 5898248 | tf_op jit(solution)/shard_map/ppermute | solution.py:21
  98.0 2.4 %collective-permute-start.2 = (bf16[320,3072]{1,0:T(8,128)(2,1)}, bf16[320,3072]{1,0:T(8,128)(2,1)}, u32[]{:S(2)}, u32[]{:S(2)}) collective-permute-start(bf16[320,3072]{1,0:T(8,128)(2,1)} %get-tuple-element.26), channel_id=1, source_target_pairs={{0,32},{32,0},{1,33},{33,1},{2,34},{34,2},{3,35},{35,3},{4,36},{36... | collective-permute-start | bytes 5898248 | tf_op jit(solution)/shard_map/ppermute | solution.py:21
  100.4 1.7 collective-permute-done.3
  102.1 2.1 %add_convert_fusion = bf16[320,3072]{1,0:T(8,128)(2,1)} fusion(bf16[320,3072]{1,0:T(8,128)(2,1)S(1)} %collective-permute-done.3, bf16[320,3072]{1,0:T(8,128)(2,1)S(1)} %copy-done.7), kind=kLoop, calls=%fused_computation | loop fusion | flops 3932160 | bytes 5898240 | tf_op jit(solution)/shard_map/convert_element_type | solution.py:150
  105.7 3.5 %add_convert_fusion.1 = bf16[320,3072]{1,0:T(8,128)(2,1)} fusion(bf16[320,3072]{1,0:T(8,128)(2,1)} %collective-permute-done.2, bf16[320,3072]{1,0:T(8,128)(2,1)S(1)} %copy-done.6), kind=kLoop, calls=%fused_computation.1 | loop fusion | flops 3932160 | bytes 5898240 | tf_op jit(solution)/shard_map/convert_element_type | solution.py:150
  109.3 6.0 %all-to-all-start.3 = ((bf16[4,80,3072]{2,1,0:T(8,128)(2,1)}), bf16[4,80,3072]{2,1,0:T(8,128)(2,1)}, u32[]{:S(2)}, u32[]{:S(2)}) async-start(bf16[4,80,3072]{2,1,0:T(8,128)(2,1)} %bitcast.61), calls=%async_computation.3 | async-start | bytes 3932160 | tf_op jit(solution)/shard_map/all_to_all | solution.py:164
  119.7 3.0 %fusion.4 = bf16[1,128,3072]{2,1,0:T(8,128)(2,1)} fusion(f32[128,3072]{1,0:T(8,128)S(1)} %fusion.47, bf16[320,128]{1,0:T(8,128)(2,1)S(1)} %get-tuple-element.30, bf16[320,3072]{1,0:T(8,128)(2,1)} %collective-permute-done.refs_0_), kind=kOutput, calls=%fused_computation.9 | convolution fusion | flops 252444672 | bytes 4407296 | tf_op jit(solution)/shard_map/dot_general | solution.py:37
  122.7 3.1 %fusion.5 = bf16[1,128,3072]{2,1,0:T(8,128)(2,1)} fusion(f32[128,3072]{1,0:T(8,128)S(1)} %fusion.46, bf16[320,128]{1,0:T(8,128)(2,1)S(1)} %get-tuple-element.28, bf16[320,3072]{1,0:T(8,128)(2,1)} %collective-permute-done.refs_0_), kind=kOutput, calls=%fused_computation.10 | convolution fusion | flops 252444672 | bytes 4407296 | tf_op jit(solution)/shard_map/dot_general | solution.py:37
  125.8 13.6 %all-to-all-done.3 = bf16[4,80,3072]{2,1,0:T(8,128)(2,1)} async-done(((bf16[4,80,3072]{2,1,0:T(8,128)(2,1)}), bf16[4,80,3072]{2,1,0:T(8,128)(2,1)}, u32[]{:S(2)}, u32[]{:S(2)}) %all-to-all-start.3) | async-done | bytes 1966112 | tf_op jit(solution)/shard_map/all_to_all | solution.py:164
  139.4 1.9 %reduce_sum.74 = bf16[80,3072]{1,0:T(8,128)(2,1)S(1)} reduce(bf16[4,80,3072]{2,1,0:T(8,128)(2,1)} %all-to-all-done.3, bf16[]{:T(256)} %constant.90.clone.1), dimensions={0}, to_apply=%region_7.8 | reduce | flops 737280 | bytes 2457602 | tf_op jit(solution)/shard_map/reduce_sum | solution.py:165
  142.4 4.0 %all-to-all-start.4 = ((bf16[8,40,768]{2,1,0:T(8,128)(2,1)}), bf16[8,40,768]{2,1,0:T(8,128)(2,1)S(1)}, u32[]{:S(2)}, u32[]{:S(2)}) async-start(bf16[8,40,768]{2,1,0:T(8,128)(2,1)} %reshape.131), calls=%async_computation.4 | async-start | bytes 983040 | tf_op jit(solution)/shard_map/all_to_all | solution.py:164
  148.8 3.5 %collective-permute-start.4 = (bf16[40,768]{1,0:T(8,128)(2,1)S(1)}, bf16[40,768]{1,0:T(8,128)(2,1)S(1)}, u32[]{:S(2)}, u32[]{:S(2)}) collective-permute-start(bf16[40,768]{1,0:T(8,128)(2,1)S(1)} %get-tuple-element.39), channel_id=1, source_target_pairs={{0,1},{1,2},{2,3},{3,0},{4,5},{5,6},{6,7},{7,4},{8,9},{9,10},{10,1... | collective-permute-start | bytes 184328 | tf_op jit(solution)/shard_map/ppermute | solution.py:174
  152.3 2.8 %collective-permute-start.6 = (bf16[40,768]{1,0:T(8,128)(2,1)S(1)}, bf16[40,768]{1,0:T(8,128)(2,1)S(1)}, u32[]{:S(2)}, u32[]{:S(2)}) collective-permute-start(bf16[40,768]{1,0:T(8,128)(2,1)S(1)} %get-tuple-element.40), channel_id=1, source_target_pairs={{0,2},{1,3},{2,0},{3,1},{4,6},{5,7},{6,4},{7,5},{8,10},{9,11},{10,... | collective-permute-start | bytes 184328 | tf_op jit(solution)/shard_map/ppermute | solution.py:174
  155.1 4.0 %collective-permute-start.5 = (bf16[40,768]{1,0:T(8,128)(2,1)S(1)}, bf16[40,768]{1,0:T(8,128)(2,1)S(1)}, u32[]{:S(2)}, u32[]{:S(2)}) collective-permute-start(bf16[40,768]{1,0:T(8,128)(2,1)S(1)} %get-tuple-element.41), channel_id=1, source_target_pairs={{0,3},{1,0},{2,1},{3,2},{4,7},{5,4},{6,5},{7,6},{8,11},{9,8},{10,9... | collective-permute-start | bytes 184328 | tf_op jit(solution)/shard_map/ppermute | solution.py:174
  159.1 3.5 %all-to-all-done.4 = bf16[8,40,768]{2,1,0:T(8,128)(2,1)S(1)} async-done(((bf16[8,40,768]{2,1,0:T(8,128)(2,1)}), bf16[8,40,768]{2,1,0:T(8,128)(2,1)S(1)}, u32[]{:S(2)}, u32[]{:S(2)}) %all-to-all-start.4) | async-done | bytes 491552 | tf_op jit(solution)/shard_map/all_to_all | solution.py:164
  163.6 7.3 %all-to-all-start.5 = ((bf16[8,20,384]{2,1,0:T(8,128)(2,1)}), bf16[8,20,384]{2,1,0:T(8,128)(2,1)S(1)}, u32[]{:S(2)}, u32[]{:S(2)}) async-start(bf16[8,20,384]{2,1,0:T(8,128)(2,1)} %copy.45), calls=%async_computation.6 | async-start | bytes 294912 | tf_op jit(solution)/shard_map/all_to_all | solution.py:187
  170.9 9.2 %all-to-all-done.5 = bf16[8,20,384]{2,1,0:T(8,128)(2,1)S(1)} async-done(((bf16[8,20,384]{2,1,0:T(8,128)(2,1)}), bf16[8,20,384]{2,1,0:T(8,128)(2,1)S(1)}, u32[]{:S(2)}, u32[]{:S(2)}) %all-to-all-start.5) | async-done | bytes 122912 | tf_op jit(solution)/shard_map/all_to_all | solution.py:187
  (81 shorter events, 17.9 us)
Async XLA Ops:
  7.2 1.9 %copy-start = (bf16[24,3072]{1,0:T(8,128)(2,1)S(1)}, bf16[24,3072]{1,0:T(8,128)(2,1)}, u32[]{:S(2)}) copy-start(bf16[24,3072]{1,0:T(8,128)(2,1)} %param.8) | copy-start | bytes 442372
  7.2 16.5 %copy-start.8 = (bf16[24,3072]{1,0:T(8,128)(2,1)S(1)}, bf16[24,3072]{1,0:T(8,128)(2,1)}, u32[]{:S(2)}) copy-start(bf16[24,3072]{1,0:T(8,128)(2,1)} %param.7) | copy-start | bytes 442372
  7.2 65.2 %all-gather.2.cloned.1.call-start = ((), (), s32[]{:S(2)}) async-start(), calls=%async_computation.7 | async-start | bytes 2211840 | tf_op jit(solution)/shard_map/all_gather | solution.py:134
  23.6 124.0 %reduce-scatter.2.cloned.1.call-start = ((), (), s32[]{:S(2)}) async-start(), calls=%async_computation.8 | async-start | bytes 2211840 | tf_op jit(solution)/shard_map/reduce_scatter | solution.py:177
  70.5 5.2 %copy-start.1 = (bf16[4,80,3072]{2,1,0:T(8,128)(2,1)}, bf16[4,80,3072]{2,1,0:T(8,128)(2,1)S(1)}, u32[]{:S(2)}) copy-start(bf16[4,80,3072]{2,1,0:T(8,128)(2,1)S(1)} %all_to_all.32) | copy-start | bytes 5898244
  70.5 14.7 %collective-permute-start = (bf16[320,3072]{1,0:T(8,128)(2,1)S(1)}, bf16[320,3072]{1,0:T(8,128)(2,1)}, u32[]{:S(2)}, u32[]{:S(2)}) collective-permute-start(bf16[320,3072]{1,0:T(8,128)(2,1)S(1)} %bitcast.57), channel_id=1, source_target_pairs={{0,32},{32,0},{1,33},{33,1},{2,34},{34,2},{3,35},{35,3},{4,36},{36... | collective-permute-start | bytes 5898248 | tf_op jit(solution)/shard_map/ppermute | solution.py:21
  72.4 12.8 %collective-permute-start.1 = (bf16[320,3072]{1,0:T(8,128)(2,1)}, bf16[320,3072]{1,0:T(8,128)(2,1)S(1)}, u32[]{:S(2)}, u32[]{:S(2)}) collective-permute-start(bf16[320,3072]{1,0:T(8,128)(2,1)} %all-gather.2.cloned.1.call-done.refs_1_), channel_id=1, source_target_pairs={{0,32},{32,0},{1,33},{33,1},{2,34},{34,2},{3,35},{35,3},{4,36},{36... | collective-permute-start | bytes 5898248 | tf_op jit(solution)/shard_map/ppermute | solution.py:21
  85.2 1.3 copy-start.4
  86.5 15.6 %copy-start.7 = (bf16[320,3072]{1,0:T(8,128)(2,1)S(1)}, bf16[320,3072]{1,0:T(8,128)(2,1)}, u32[]{:S(2)}) copy-start(bf16[320,3072]{1,0:T(8,128)(2,1)} %get-tuple-element.34) | copy-start | bytes 5898244
  96.0 6.1 %collective-permute-start.3 = (bf16[320,3072]{1,0:T(8,128)(2,1)}, bf16[320,3072]{1,0:T(8,128)(2,1)S(1)}, u32[]{:S(2)}, u32[]{:S(2)}) collective-permute-start(bf16[320,3072]{1,0:T(8,128)(2,1)} %get-tuple-element.35), channel_id=1, source_target_pairs={{0,32},{32,0},{1,33},{33,1},{2,34},{34,2},{3,35},{35,3},{4,36},{36... | collective-permute-start | bytes 5898248 | tf_op jit(solution)/shard_map/ppermute | solution.py:21
  98.0 7.1 %collective-permute-start.2 = (bf16[320,3072]{1,0:T(8,128)(2,1)}, bf16[320,3072]{1,0:T(8,128)(2,1)}, u32[]{:S(2)}, u32[]{:S(2)}) collective-permute-start(bf16[320,3072]{1,0:T(8,128)(2,1)} %get-tuple-element.26), channel_id=1, source_target_pairs={{0,32},{32,0},{1,33},{33,1},{2,34},{34,2},{3,35},{35,3},{4,36},{36... | collective-permute-start | bytes 5898248 | tf_op jit(solution)/shard_map/ppermute | solution.py:21
  104.2 1.5 copy-start.6
  109.3 6.0 %copy-start.2 = (bf16[4,80,3072]{2,1,0:T(8,128)(2,1)S(1)}, bf16[4,80,3072]{2,1,0:T(8,128)(2,1)}, u32[]{:S(2)}) copy-start(bf16[4,80,3072]{2,1,0:T(8,128)(2,1)} %copy-done.1) | copy-start | bytes 5898244
  109.3 30.1 %all-to-all-start.3 = ((bf16[4,80,3072]{2,1,0:T(8,128)(2,1)}), bf16[4,80,3072]{2,1,0:T(8,128)(2,1)}, u32[]{:S(2)}, u32[]{:S(2)}) async-start(bf16[4,80,3072]{2,1,0:T(8,128)(2,1)} %bitcast.61), calls=%async_computation.3 | async-start | bytes 3932160 | tf_op jit(solution)/shard_map/all_to_all | solution.py:164
  115.8 1.6 copy-start.3
  116.5 1.7 copy-start.5
  125.8 20.6 %copy-start.9 = (s32[24,2]{0,1:T(2,128)S(1)}, s32[24,2]{0,1:T(2,128)}, u32[]{:S(2)}) copy-start(s32[24,2]{0,1:T(2,128)} %param.9) | copy-start | bytes 580
  141.3 17.8 %copy-start.10 = (f32[24,2]{0,1:T(2,128)S(1)}, f32[24,2]{0,1:T(2,128)}, u32[]{:S(2)}) copy-start(f32[24,2]{0,1:T(2,128)} %param.10) | copy-start | bytes 580
  142.4 20.2 %all-to-all-start.4 = ((bf16[8,40,768]{2,1,0:T(8,128)(2,1)}), bf16[8,40,768]{2,1,0:T(8,128)(2,1)S(1)}, u32[]{:S(2)}, u32[]{:S(2)}) async-start(bf16[8,40,768]{2,1,0:T(8,128)(2,1)} %reshape.131), calls=%async_computation.4 | async-start | bytes 983040 | tf_op jit(solution)/shard_map/all_to_all | solution.py:164
  148.8 13.9 %collective-permute-start.4 = (bf16[40,768]{1,0:T(8,128)(2,1)S(1)}, bf16[40,768]{1,0:T(8,128)(2,1)S(1)}, u32[]{:S(2)}, u32[]{:S(2)}) collective-permute-start(bf16[40,768]{1,0:T(8,128)(2,1)S(1)} %get-tuple-element.39), channel_id=1, source_target_pairs={{0,1},{1,2},{2,3},{3,0},{4,5},{5,6},{6,7},{7,4},{8,9},{9,10},{10,1... | collective-permute-start | bytes 184328 | tf_op jit(solution)/shard_map/ppermute | solution.py:174
  152.3 10.5 %collective-permute-start.6 = (bf16[40,768]{1,0:T(8,128)(2,1)S(1)}, bf16[40,768]{1,0:T(8,128)(2,1)S(1)}, u32[]{:S(2)}, u32[]{:S(2)}) collective-permute-start(bf16[40,768]{1,0:T(8,128)(2,1)S(1)} %get-tuple-element.40), channel_id=1, source_target_pairs={{0,2},{1,3},{2,0},{3,1},{4,6},{5,7},{6,4},{7,5},{8,10},{9,11},{10,... | collective-permute-start | bytes 184328 | tf_op jit(solution)/shard_map/ppermute | solution.py:174
  155.1 7.7 %collective-permute-start.5 = (bf16[40,768]{1,0:T(8,128)(2,1)S(1)}, bf16[40,768]{1,0:T(8,128)(2,1)S(1)}, u32[]{:S(2)}, u32[]{:S(2)}) collective-permute-start(bf16[40,768]{1,0:T(8,128)(2,1)S(1)} %get-tuple-element.41), channel_id=1, source_target_pairs={{0,3},{1,0},{2,1},{3,2},{4,7},{5,4},{6,5},{7,6},{8,11},{9,8},{10,9... | collective-permute-start | bytes 184328 | tf_op jit(solution)/shard_map/ppermute | solution.py:174
  163.6 16.6 %all-to-all-start.5 = ((bf16[8,20,384]{2,1,0:T(8,128)(2,1)}), bf16[8,20,384]{2,1,0:T(8,128)(2,1)S(1)}, u32[]{:S(2)}, u32[]{:S(2)}) async-start(bf16[8,20,384]{2,1,0:T(8,128)(2,1)} %copy.45), calls=%async_computation.6 | async-start | bytes 294912 | tf_op jit(solution)/shard_map/all_to_all | solution.py:187
Sparse Core Ops, SparseCore 0:
  23.8 44.5 all-gather.1
  104.3 43.2 reduce-scatter.1

commit v7 on v5

--- a/solution.py
+++ b/solution.py
@@ -37,9 +37,12 @@
     return lax.dot_general(a, b, (dims, ((), ())), preferred_element_type=F32)
 
 
-def layer_kernel(tok_ref, grad_ref, wg_ref, wu_ref, wd_ref, turn_ref, *outs):
-    turned_hidden_ref, grad_gate_ref, grad_up_ref, out_ref, din_ref = outs
-    w_gate, w_up, w_down = wg_ref[...], wu_ref[...], wd_ref[...]
+def layer_kernel(tok_ref, grad_ref, turn_ref, *refs):
+    turned_hidden_ref, grad_gate_ref, grad_up_ref, out_ref, din_ref = refs[6:]
+    w_gate, w_up, w_down = [
+        jnp.concatenate([mine[...], theirs[...]], axis=0)
+        for mine, theirs in zip(refs[:3], refs[3:6])
+    ]
     turn = turn_ref[...]
     units = w_gate.shape[0]
     rows_tok = tok_ref[...]
@@ -72,16 +75,16 @@
     out_ref[...] = dot(hidden, w_down, ((1,), (0,))).astype(BF16)
 
 
-def forward_backward(rows_tok, rows_grad, w_gate, w_up, w_down, turn):
+def forward_backward(rows_tok, rows_grad, turn, mine, theirs):
     n_rows, width = rows_tok.shape
-    narrow = jax.ShapeDtypeStruct((n_rows, w_gate.shape[0]), BF16)
+    narrow = jax.ShapeDtypeStruct((n_rows, 2 * mine[0].shape[0]), BF16)
     wide = jax.ShapeDtypeStruct((n_rows, width), BF16)
     return pl.pallas_call(
         layer_kernel,
         out_shape=(narrow, narrow, narrow, wide, wide),
-        compiler_params=pltpu.CompilerParams(vmem_limit_bytes=26 * 1024 * 1024),
+        compiler_params=pltpu.CompilerParams(vmem_limit_bytes=32 * 1024 * 1024),
         name="layer",
-    )(rows_tok, rows_grad, w_gate, w_up, w_down, turn)
+    )(rows_tok, rows_grad, turn, *mine, *theirs)
 
 
 def on_device(tokens, cotangent, experts, gate_weights, w_gate, w_up, w_down):
@@ -103,31 +106,28 @@
     grad_own = lax.all_gather(grad_own, "z", axis=0, tiled=True)
     tok_own = spread(slot_tokens.reshape(quarter), "z").reshape(n_z * C, width)
     tok_own = spread(tok_own, "x").reshape(n_rows, width)
-    tok_other, grad_other = swap(tok_own), swap(grad_own)
 
     at_tok = lax.broadcasted_iota(jnp.int32, (n_rows, n_rows), 0)
     at_grad = lax.broadcasted_iota(jnp.int32, (n_rows, n_rows), 1)
     of_z, of_x, of_slot = at_grad // (n_x * C), at_grad // C % n_x, at_grad % C
     turn = (at_tok == of_x * (n_z * C) + of_z * C + of_slot).astype(BF16)
 
-    weights = (w_gate, w_up, w_down, turn)
-    hid_a, gg_a, gu_a, out_a, din_a = forward_backward(tok_own, grad_own, *weights)
-    tok_other, grad_other, out_a = lax.optimization_barrier((tok_other, grad_other, out_a))
-    hid_b, gg_b, gu_b, out_b, din_b = forward_backward(tok_other, grad_other, *weights)
+    mine = (w_gate, w_up, w_down)
+    theirs = tuple(swap(w) for w in mine)
+    hidden, grad_gate, grad_up, sum_out, sum_din = forward_backward(
+        tok_own, grad_own, turn, mine, theirs
+    )
+    sum_out = sum_out.reshape(n_x, n_z * C, width)
 
-    def chip_sum(mine, partner):
-        return (mine.astype(F32) + swap(partner).astype(F32)).astype(BF16)
+    def weight_grad(left, right):
+        units = left.shape[1] // 2
+        here = dot(left[:, :units], right, ((0,), (0,)))
+        there = swap(dot(left[:, units:], right, ((0,), (0,))))
+        return (here + there).astype(BF16)[None]
 
-    sum_din = chip_sum(din_a, din_b)
-    sum_out = chip_sum(out_a, out_b).reshape(n_x, n_z * C, width)
-
-    def weight_grad(left_a, right_a, left_b, right_b):
-        total = dot(left_a, right_a, ((0,), (0,))) + dot(left_b, right_b, ((0,), (0,)))
-        return total.astype(BF16)[None]
-
-    grad_w_gate = weight_grad(gg_a, tok_own, gg_b, tok_other)
-    grad_w_up = weight_grad(gu_a, tok_own, gu_b, tok_other)
-    grad_w_down = weight_grad(hid_a, grad_own, hid_b, grad_other)
+    grad_w_gate = weight_grad(grad_gate, tok_own)
+    grad_w_up = weight_grad(grad_up, tok_own)
+    grad_w_down = weight_grad(hidden, grad_own)
 
     def exchange_sum(a, axis):
         a = lax.all_to_all(a, axis, split_axis=0, concat_axis=0, tiled=True)

time: 188 us -> 182 us (0.968)
  the two profiles are of different devices: /device:TPU:2 before, /device:TPU:8 now
where the time goes in v7:
time: 182 us; the launch traced here: 181 us
  starting transfers between devices  45.8 us (25%)
  blocking collectives  38.2 us (21%)
  waiting for transfers between devices  37 us (20%)
  local copies, waits for them, and re-layouts  19.7 us (11%)
  matrix products  16.5 us (9%)
  between operations  14.5 us (8%)
  Pallas kernels  5.07 us (3%)
  other arithmetic  3.99 us (2%)
    all_to_all x2, blocking collectives, spread(): return lax.all_to_all(copies, axis, split_axis=0, concat_axis=0, tiled=True)  38.2 us
    dot_general x8, matrix products, dot(): return lax.dot_general(a, b, (dims, ((), ())), preferred_element_type=F32)  14.9 us
    reduce_scatter x1, waiting for transfers between devices, on_device(): sum_din = lax.psum_scatter(sum_din, 'z', scatter_dimension=0, tiled=True)  13.6 us
    unnamed x38, local copies, waits for them, and re-layouts  13.1 us
    ppermute x6, starting transfers between devices, swap(): return lax.ppermute(a, 'c', [(0, 1), (1, 0)])  12.7 us
    ppermute x3, starting transfers between devices, turn_sum(): total += lax.ppermute(theirs, axis, pairs).astype(F32)  11.1 us
    all_to_all x2, starting transfers between devices, exchange_sum(): a = lax.all_to_all(a, axis, split_axis=0, concat_axis=0, tiled=True)  10.5 us
    all_to_all x1, waiting for transfers between devices, spread(): return lax.all_to_all(copies, axis, split_axis=0, concat_axis=0, tiled=True)  9.89 us
  transfers between devices with their start and end apart: 15, of which 6 were waited for; matrix products, arithmetic and copies ran while one was open for 12% of the time, Pallas kernels for 0%

profile of v7, /device:TPU:8, one launch (start us, length us, event | category | flops | bytes accessed | tf_op | source)
XLA Modules:
  0.0 180.8 jit_solution(8108273902195596479)
XLA Ops:
  9.4 10.7 %all_to_all.30 = bf16[4,40,768]{2,1,0:T(8,128)(2,1)S(1)} all-to-all(bf16[4,40,768]{2,1,0:T(8,128)(2,1)S(1)} %broadcast_in_dim.46), channel_id=1, replica_groups=mesh['z'=8,'c'=2,'y'=8,'x'=4] {'x'}, dimensions={0} | all-to-all | bytes 491520 | tf_op jit(solution)/shard_map/all_to_all | solution.py:17
  21.2 27.6 %all_to_all.31 = bf16[8,40,768]{2,1,0:T(8,128)(2,1)S(1)} all-to-all(bf16[8,40,768]{2,1,0:T(8,128)(2,1)S(1)} %broadcast_in_dim.19), channel_id=1, replica_groups=mesh['z'=8,'c'=2,'y'=8,'x'=4] {'z'}, dimensions={0} | all-to-all | bytes 983040 | tf_op jit(solution)/shard_map/all_to_all | solution.py:17
  50.5 3.7 %all-to-all-start.1 = ((bf16[4,80,3072]{2,1,0:T(8,128)(2,1)}), bf16[4,80,3072]{2,1,0:T(8,128)(2,1)S(1)}, u32[]{:S(2)}, u32[]{:S(2)}) async-start(bf16[4,80,3072]{2,1,0:T(8,128)(2,1)} %broadcast_in_dim.21), calls=%async_computation.1 | async-start | bytes 3932160 | tf_op jit(solution)/shard_map/all_to_all | solution.py:17
  54.3 1.9 %collective-permute-start = (bf16[128,3072]{1,0:T(8,128)(2,1)S(1)}, bf16[128,3072]{1,0:T(8,128)(2,1)S(1)}, u32[]{:S(2)}, u32[]{:S(2)}) collective-permute-start(bf16[128,3072]{1,0:T(8,128)(2,1)S(1)} %bitcast.57), channel_id=1, source_target_pairs={{0,32},{32,0},{1,33},{33,1},{2,34},{34,2},{3,35},{35,3},{4,36},{36... | collective-permute-start | bytes 2359304 | tf_op jit(solution)/shard_map/ppermute | solution.py:21
  56.3 2.4 %collective-permute-start.1 = (bf16[128,3072]{1,0:T(8,128)(2,1)}, bf16[128,3072]{1,0:T(8,128)(2,1)S(1)}, u32[]{:S(2)}, u32[]{:S(2)}) collective-permute-start(bf16[128,3072]{1,0:T(8,128)(2,1)} %bitcast.59), channel_id=1, source_target_pairs={{0,32},{32,0},{1,33},{33,1},{2,34},{34,2},{3,35},{35,3},{4,36},{36... | collective-permute-start | bytes 2359304 | tf_op jit(solution)/shard_map/ppermute | solution.py:21
  58.7 1.9 %collective-permute-start.2 = (bf16[128,3072]{1,0:T(8,128)(2,1)}, bf16[128,3072]{1,0:T(8,128)(2,1)S(1)}, u32[]{:S(2)}, u32[]{:S(2)}) collective-permute-start(bf16[128,3072]{1,0:T(8,128)(2,1)} %bitcast.61), channel_id=1, source_target_pairs={{0,32},{32,0},{1,33},{33,1},{2,34},{34,2},{3,35},{35,3},{4,36},{36... | collective-permute-start | bytes 2359304 | tf_op jit(solution)/shard_map/ppermute | solution.py:21
  64.0 9.9 %all-to-all-done.1 = bf16[4,80,3072]{2,1,0:T(8,128)(2,1)S(1)} async-done(((bf16[4,80,3072]{2,1,0:T(8,128)(2,1)}), bf16[4,80,3072]{2,1,0:T(8,128)(2,1)S(1)}, u32[]{:S(2)}, u32[]{:S(2)}) %all-to-all-start.1) | async-done | bytes 1966112 | tf_op jit(solution)/shard_map/all_to_all | solution.py:17
  81.1 5.1 %layer.1 = (bf16[320,256]{1,0:T(8,128)(2,1)S(1)}, bf16[320,256]{1,0:T(8,128)(2,1)S(1)}, bf16[320,256]{1,0:T(8,128)(2,1)S(1)}, bf16[320,3072]{1,0:T(8,128)(2,1)S(1)}, bf16[320,3072]{1,0:T(8,128)(2,1)S(1)}) custom-call(bf16[320,3072]{1,0:T(8,128)(2,1)S(1)} %bitcast.51, bf16[320,3072]{1,0:T(8,128)(2,1)S(1)} %copy-done.1, bf16[320,320]{1,0:T(8,128)(2,1)S(1)} %fusion.14.turn_ref, ...), custom_call_target="tpu_custom_call" | custom-call | tf_op jit(solution)/shard_map/layer/pallas_call | solution.py:82
  89.4 4.6 %all-to-all-start.3 = ((bf16[4,80,3072]{2,1,0:T(8,128)(2,1)}), bf16[4,80,3072]{2,1,0:T(8,128)(2,1)}, u32[]{:S(2)}, u32[]{:S(2)}) async-start(bf16[4,80,3072]{2,1,0:T(8,128)(2,1)} %bitcast.56), calls=%async_computation.3 | async-start | bytes 3932160 | tf_op jit(solution)/shard_map/all_to_all | solution.py:133
  95.8 2.0 %collective-permute-start.6 = (f32[128,3072]{1,0:T(8,128)}, f32[128,3072]{1,0:T(8,128)}, u32[]{:S(2)}, u32[]{:S(2)}) collective-permute-start(f32[128,3072]{1,0:T(8,128)} %fusion.24), channel_id=1, source_target_pairs={{0,32},{32,0},{1,33},{33,1},{2,34},{34,2},{3,35},{35,3},{4,36},{36... | collective-permute-start | bytes 4718600 | tf_op jit(solution)/shard_map/ppermute | solution.py:21
  99.6 2.5 %collective-permute-start.7 = (f32[128,3072]{1,0:T(8,128)}, f32[128,3072]{1,0:T(8,128)}, u32[]{:S(2)}, u32[]{:S(2)}) collective-permute-start(f32[128,3072]{1,0:T(8,128)} %fusion.21), channel_id=1, source_target_pairs={{0,32},{32,0},{1,33},{33,1},{2,34},{34,2},{3,35},{35,3},{4,36},{36... | collective-permute-start | bytes 4718600 | tf_op jit(solution)/shard_map/ppermute | solution.py:21
  103.9 1.9 %collective-permute-start.8 = (f32[128,3072]{1,0:T(8,128)}, f32[128,3072]{1,0:T(8,128)}, u32[]{:S(2)}, u32[]{:S(2)}) collective-permute-start(f32[128,3072]{1,0:T(8,128)} %fusion.18), channel_id=1, source_target_pairs={{0,32},{32,0},{1,33},{33,1},{2,34},{34,2},{3,35},{35,3},{4,36},{36... | collective-permute-start | bytes 4718600 | tf_op jit(solution)/shard_map/ppermute | solution.py:21
  106.1 6.4 %all-to-all-done.3 = bf16[4,80,3072]{2,1,0:T(8,128)(2,1)} async-done(((bf16[4,80,3072]{2,1,0:T(8,128)(2,1)}), bf16[4,80,3072]{2,1,0:T(8,128)(2,1)}, u32[]{:S(2)}, u32[]{:S(2)}) %all-to-all-start.3) | async-done | bytes 1966112 | tf_op jit(solution)/shard_map/all_to_all | solution.py:133
  115.5 5.9 %all-to-all-start.4 = ((bf16[8,40,768]{2,1,0:T(8,128)(2,1)}), bf16[8,40,768]{2,1,0:T(8,128)(2,1)S(1)}, u32[]{:S(2)}, u32[]{:S(2)}) async-start(bf16[8,40,768]{2,1,0:T(8,128)(2,1)} %reshape.131), calls=%async_computation.4 | async-start | bytes 983040 | tf_op jit(solution)/shard_map/all_to_all | solution.py:133
  121.4 2.9 %fusion.5 = bf16[1,128,3072]{2,1,0:T(8,128)(2,1)} fusion(f32[128,3072]{1,0:T(8,128)} %collective-permute-done.6, bf16[320,3072]{1,0:T(8,128)(2,1)S(1)} %bitcast.54, bf16[320,256]{1,0:T(8,128)(2,1)S(1)} %copy-done.15), kind=kOutput, calls=%fused_computation.8 | convolution fusion | flops 252444672 | bytes 4407296 | tf_op jit(solution)/shard_map/dot_general | solution.py:37
  124.3 13.6 %reduce-scatter.2.cloned.1.call-done = bf16[40,3072]{1,0:T(8,128)(2,1)} async-done(((bf16[320,3072]{1,0:T(8,128)(2,1)}), bf16[40,3072]{1,0:T(8,128)(2,1)}) %reduce-scatter.2.cloned.1.call-update) | async-done | bytes 245776 | tf_op jit(solution)/shard_map/reduce_scatter | solution.py:146
  139.7 5.2 %collective-permute-start.5 = (bf16[40,768]{1,0:T(8,128)(2,1)}, bf16[40,768]{1,0:T(8,128)(2,1)S(1)}, u32[]{:S(2)}, u32[]{:S(2)}) collective-permute-start(bf16[40,768]{1,0:T(8,128)(2,1)} %get-tuple-element.16), channel_id=1, source_target_pairs={{0,2},{1,3},{2,0},{3,1},{4,6},{5,7},{6,4},{7,5},{8,10},{9,11},{10,... | collective-permute-start | bytes 184328 | tf_op jit(solution)/shard_map/ppermute | solution.py:143
  144.9 3.6 %collective-permute-start.4 = (bf16[40,768]{1,0:T(8,128)(2,1)}, bf16[40,768]{1,0:T(8,128)(2,1)S(1)}, u32[]{:S(2)}, u32[]{:S(2)}) collective-permute-start(bf16[40,768]{1,0:T(8,128)(2,1)} %get-tuple-element.17), channel_id=1, source_target_pairs={{0,3},{1,0},{2,1},{3,2},{4,7},{5,4},{6,5},{7,6},{8,11},{9,8},{10,9... | collective-permute-start | bytes 184328 | tf_op jit(solution)/shard_map/ppermute | solution.py:143
  148.6 2.2 %collective-permute-start.3 = (bf16[40,768]{1,0:T(8,128)(2,1)}, bf16[40,768]{1,0:T(8,128)(2,1)S(1)}, u32[]{:S(2)}, u32[]{:S(2)}) collective-permute-start(bf16[40,768]{1,0:T(8,128)(2,1)} %get-tuple-element.15), channel_id=1, source_target_pairs={{0,1},{1,2},{2,3},{3,0},{4,5},{5,6},{6,7},{7,4},{8,9},{9,10},{10,1... | collective-permute-start | bytes 184328 | tf_op jit(solution)/shard_map/ppermute | solution.py:143
  150.8 2.9 %fusion.4 = bf16[1,128,3072]{2,1,0:T(8,128)(2,1)} fusion(f32[128,3072]{1,0:T(8,128)} %collective-permute-done.7, bf16[320,3072]{1,0:T(8,128)(2,1)S(1)} %bitcast.55, bf16[320,256]{1,0:T(8,128)(2,1)S(1)} %get-tuple-element.13), kind=kOutput, calls=%fused_computation.7 | convolution fusion | flops 252444672 | bytes 4407296 | tf_op jit(solution)/shard_map/dot_general | solution.py:37
  153.8 2.3 %collective-permute-done.3 = bf16[40,768]{1,0:T(8,128)(2,1)S(1)} collective-permute-done((bf16[40,768]{1,0:T(8,128)(2,1)}, bf16[40,768]{1,0:T(8,128)(2,1)S(1)}, u32[]{:S(2)}, u32[]{:S(2)}) %collective-permute-start.3) | collective-permute-done | bytes 61472 | tf_op jit(solution)/shard_map/ppermute | solution.py:143
  156.9 7.6 %all-to-all-start.5 = ((bf16[8,20,384]{2,1,0:T(8,128)(2,1)}), bf16[8,20,384]{2,1,0:T(8,128)(2,1)S(1)}, u32[]{:S(2)}, u32[]{:S(2)}) async-start(bf16[8,20,384]{2,1,0:T(8,128)(2,1)} %copy.45), calls=%async_computation.6 | async-start | bytes 294912 | tf_op jit(solution)/shard_map/all_to_all | solution.py:153
  164.5 3.5 %fusion.3 = bf16[1,128,3072]{2,1,0:T(8,128)(2,1)} fusion(f32[128,3072]{1,0:T(8,128)} %collective-permute-done.8, bf16[320,3072]{1,0:T(8,128)(2,1)} %all-gather.2.cloned.1.call-done.grad_ref, bf16[320,256]{1,0:T(8,128)(2,1)S(1)} %get-tuple-element.14), kind=kOutput, calls=%fused_computation.6 | convolution fusion | flops 252444672 | bytes 4407296 | tf_op jit(solution)/shard_map/dot_general | solution.py:37
  168.0 4.3 %all-to-all-done.5 = bf16[8,20,384]{2,1,0:T(8,128)(2,1)S(1)} async-done(((bf16[8,20,384]{2,1,0:T(8,128)(2,1)}), bf16[8,20,384]{2,1,0:T(8,128)(2,1)S(1)}, u32[]{:S(2)}, u32[]{:S(2)}) %all-to-all-start.5) | async-done | bytes 122912 | tf_op jit(solution)/shard_map/all_to_all | solution.py:153
  (99 shorter events, 31.7 us)
Async XLA Ops:
  7.2 1.9 %copy-start = (bf16[24,3072]{1,0:T(8,128)(2,1)S(1)}, bf16[24,3072]{1,0:T(8,128)(2,1)}, u32[]{:S(2)}) copy-start(bf16[24,3072]{1,0:T(8,128)(2,1)} %param.8) | copy-start | bytes 442372
  7.2 13.7 %copy-start.16 = (bf16[24,3072]{1,0:T(8,128)(2,1)S(1)}, bf16[24,3072]{1,0:T(8,128)(2,1)}, u32[]{:S(2)}) copy-start(bf16[24,3072]{1,0:T(8,128)(2,1)} %param.7) | copy-start | bytes 442372
  7.2 66.7 %all-gather.2.cloned.1.call-start = ((), (), s32[]{:S(2)}) async-start(), calls=%async_computation.7 | async-start | bytes 2211840 | tf_op jit(solution)/shard_map/all_gather | solution.py:106
  50.5 3.8 %copy-start.5 = (bf16[1,128,3072]{2,1,0:T(8,128)(2,1)S(1)}, bf16[1,128,3072]{2,1,0:T(8,128)(2,1)}, u32[]{:S(2)}) copy-start(bf16[1,128,3072]{2,1,0:T(8,128)(2,1)} %param.11) | copy-start | bytes 2359300
  50.5 23.3 %all-to-all-start.1 = ((bf16[4,80,3072]{2,1,0:T(8,128)(2,1)}), bf16[4,80,3072]{2,1,0:T(8,128)(2,1)S(1)}, u32[]{:S(2)}, u32[]{:S(2)}) async-start(bf16[4,80,3072]{2,1,0:T(8,128)(2,1)} %broadcast_in_dim.21), calls=%async_computation.1 | async-start | bytes 3932160 | tf_op jit(solution)/shard_map/all_to_all | solution.py:17
  54.3 83.6 %reduce-scatter.2.cloned.1.call-start = ((), (), s32[]{:S(2)}) async-start(), calls=%async_computation.8 | async-start | bytes 2211840 | tf_op jit(solution)/shard_map/reduce_scatter | solution.py:146
  54.3 6.4 %collective-permute-start = (bf16[128,3072]{1,0:T(8,128)(2,1)S(1)}, bf16[128,3072]{1,0:T(8,128)(2,1)S(1)}, u32[]{:S(2)}, u32[]{:S(2)}) collective-permute-start(bf16[128,3072]{1,0:T(8,128)(2,1)S(1)} %bitcast.57), channel_id=1, source_target_pairs={{0,32},{32,0},{1,33},{33,1},{2,34},{34,2},{3,35},{35,3},{4,36},{36... | collective-permute-start | bytes 2359304 | tf_op jit(solution)/shard_map/ppermute | solution.py:21
  56.3 5.4 %collective-permute-start.1 = (bf16[128,3072]{1,0:T(8,128)(2,1)}, bf16[128,3072]{1,0:T(8,128)(2,1)S(1)}, u32[]{:S(2)}, u32[]{:S(2)}) collective-permute-start(bf16[128,3072]{1,0:T(8,128)(2,1)} %bitcast.59), channel_id=1, source_target_pairs={{0,32},{32,0},{1,33},{33,1},{2,34},{34,2},{3,35},{35,3},{4,36},{36... | collective-permute-start | bytes 2359304 | tf_op jit(solution)/shard_map/ppermute | solution.py:21
  58.7 4.4 %collective-permute-start.2 = (bf16[128,3072]{1,0:T(8,128)(2,1)}, bf16[128,3072]{1,0:T(8,128)(2,1)S(1)}, u32[]{:S(2)}, u32[]{:S(2)}) collective-permute-start(bf16[128,3072]{1,0:T(8,128)(2,1)} %bitcast.61), channel_id=1, source_target_pairs={{0,32},{32,0},{1,33},{33,1},{2,34},{34,2},{3,35},{35,3},{4,36},{36... | collective-permute-start | bytes 2359304 | tf_op jit(solution)/shard_map/ppermute | solution.py:21
  73.8 1.5 copy-start.1
  87.4 1.3 copy-start.4
  89.4 4.6 %copy-start.15 = (bf16[320,256]{1,0:T(8,128)(2,1)S(1)}, bf16[320,256]{1,0:T(8,128)(2,1)}, u32[]{:S(2)}) copy-start(bf16[320,256]{1,0:T(8,128)(2,1)} %copy-done.14) | copy-start | bytes 491524
  89.4 23.1 %all-to-all-start.3 = ((bf16[4,80,3072]{2,1,0:T(8,128)(2,1)}), bf16[4,80,3072]{2,1,0:T(8,128)(2,1)}, u32[]{:S(2)}, u32[]{:S(2)}) async-start(bf16[4,80,3072]{2,1,0:T(8,128)(2,1)} %bitcast.56), calls=%async_computation.3 | async-start | bytes 3932160 | tf_op jit(solution)/shard_map/all_to_all | solution.py:133
  95.8 6.4 %copy-start.2 = (bf16[320,3072]{1,0:T(8,128)(2,1)S(1)}, bf16[320,3072]{1,0:T(8,128)(2,1)}, u32[]{:S(2)}) copy-start(bf16[320,3072]{1,0:T(8,128)(2,1)} %all-gather.2.cloned.1.call-done.grad_ref) | copy-start | bytes 5898244
  95.8 25.7 %collective-permute-start.6 = (f32[128,3072]{1,0:T(8,128)}, f32[128,3072]{1,0:T(8,128)}, u32[]{:S(2)}, u32[]{:S(2)}) collective-permute-start(f32[128,3072]{1,0:T(8,128)} %fusion.24), channel_id=1, source_target_pairs={{0,32},{32,0},{1,33},{33,1},{2,34},{34,2},{3,35},{35,3},{4,36},{36... | collective-permute-start | bytes 4718600 | tf_op jit(solution)/shard_map/ppermute | solution.py:21
  99.6 6.2 %copy-start.17 = (s32[24,2]{0,1:T(2,128)S(1)}, s32[24,2]{0,1:T(2,128)}, u32[]{:S(2)}) copy-start(s32[24,2]{0,1:T(2,128)} %param.9) | copy-start | bytes 580
  99.6 6.5 %copy-start.18 = (f32[24,2]{0,1:T(2,128)S(1)}, f32[24,2]{0,1:T(2,128)}, u32[]{:S(2)}) copy-start(f32[24,2]{0,1:T(2,128)} %param.10) | copy-start | bytes 580
  99.6 51.2 %collective-permute-start.7 = (f32[128,3072]{1,0:T(8,128)}, f32[128,3072]{1,0:T(8,128)}, u32[]{:S(2)}, u32[]{:S(2)}) collective-permute-start(f32[128,3072]{1,0:T(8,128)} %fusion.21), channel_id=1, source_target_pairs={{0,32},{32,0},{1,33},{33,1},{2,34},{34,2},{3,35},{35,3},{4,36},{36... | collective-permute-start | bytes 4718600 | tf_op jit(solution)/shard_map/ppermute | solution.py:21
  103.9 60.6 %collective-permute-start.8 = (f32[128,3072]{1,0:T(8,128)}, f32[128,3072]{1,0:T(8,128)}, u32[]{:S(2)}, u32[]{:S(2)}) collective-permute-start(f32[128,3072]{1,0:T(8,128)} %fusion.18), channel_id=1, source_target_pairs={{0,32},{32,0},{1,33},{33,1},{2,34},{34,2},{3,35},{35,3},{4,36},{36... | collective-permute-start | bytes 4718600 | tf_op jit(solution)/shard_map/ppermute | solution.py:21
  115.5 38.2 %all-to-all-start.4 = ((bf16[8,40,768]{2,1,0:T(8,128)(2,1)}), bf16[8,40,768]{2,1,0:T(8,128)(2,1)S(1)}, u32[]{:S(2)}, u32[]{:S(2)}) async-start(bf16[8,40,768]{2,1,0:T(8,128)(2,1)} %reshape.131), calls=%async_computation.4 | async-start | bytes 983040 | tf_op jit(solution)/shard_map/all_to_all | solution.py:133
  139.7 14.1 %collective-permute-start.5 = (bf16[40,768]{1,0:T(8,128)(2,1)}, bf16[40,768]{1,0:T(8,128)(2,1)S(1)}, u32[]{:S(2)}, u32[]{:S(2)}) collective-permute-start(bf16[40,768]{1,0:T(8,128)(2,1)} %get-tuple-element.16), channel_id=1, source_target_pairs={{0,2},{1,3},{2,0},{3,1},{4,6},{5,7},{6,4},{7,5},{8,10},{9,11},{10,... | collective-permute-start | bytes 184328 | tf_op jit(solution)/shard_map/ppermute | solution.py:143
  144.9 8.9 %collective-permute-start.4 = (bf16[40,768]{1,0:T(8,128)(2,1)}, bf16[40,768]{1,0:T(8,128)(2,1)S(1)}, u32[]{:S(2)}, u32[]{:S(2)}) collective-permute-start(bf16[40,768]{1,0:T(8,128)(2,1)} %get-tuple-element.17), channel_id=1, source_target_pairs={{0,3},{1,0},{2,1},{3,2},{4,7},{5,4},{6,5},{7,6},{8,11},{9,8},{10,9... | collective-permute-start | bytes 184328 | tf_op jit(solution)/shard_map/ppermute | solution.py:143
  148.6 7.5 %collective-permute-start.3 = (bf16[40,768]{1,0:T(8,128)(2,1)}, bf16[40,768]{1,0:T(8,128)(2,1)S(1)}, u32[]{:S(2)}, u32[]{:S(2)}) collective-permute-start(bf16[40,768]{1,0:T(8,128)(2,1)} %get-tuple-element.15), channel_id=1, source_target_pairs={{0,1},{1,2},{2,3},{3,0},{4,5},{5,6},{6,7},{7,4},{8,9},{9,10},{10,1... | collective-permute-start | bytes 184328 | tf_op jit(solution)/shard_map/ppermute | solution.py:143
  156.9 15.4 %all-to-all-start.5 = ((bf16[8,20,384]{2,1,0:T(8,128)(2,1)}), bf16[8,20,384]{2,1,0:T(8,128)(2,1)S(1)}, u32[]{:S(2)}, u32[]{:S(2)}) async-start(bf16[8,20,384]{2,1,0:T(8,128)(2,1)} %copy.45), calls=%async_computation.6 | async-start | bytes 294912 | tf_op jit(solution)/shard_map/all_to_all | solution.py:153
  (10 other events, 10.2 us)
Sparse Core Ops, SparseCore 0:
  21.0 48.3 all-gather.1
  89.5 48.3 reduce-scatter.1

commit v8 on v7

--- a/solution.py
+++ b/solution.py
@@ -38,15 +38,23 @@
 
 
 def layer_kernel(tok_ref, grad_ref, turn_ref, *refs):
-    turned_hidden_ref, grad_gate_ref, grad_up_ref, out_ref, din_ref = refs[6:]
-    w_gate, w_up, w_down = [
-        jnp.concatenate([mine[...], theirs[...]], axis=0)
-        for mine, theirs in zip(refs[:3], refs[3:6])
+    sources, outs, scratch = refs[:6], refs[6:11], refs[11:]
+    turned_hidden_ref, grad_gate_ref, grad_up_ref, out_hbm, din_hbm = outs
+    w_gate, w_up, w_down, out_ref, din_ref, sems = scratch
+    half = w_gate.shape[0] // 2
+    loads = [
+        pltpu.make_async_copy(
+            source, (w_gate, w_up, w_down)[i % 3].at[pl.ds(i // 3 * half, half)], sems.at[i]
+        )
+        for i, source in enumerate(sources)
     ]
+    for i in (2, 5, 0, 3, 1, 4):
+        loads[i].start()
     turn = turn_ref[...]
-    units = w_gate.shape[0]
-    rows_tok = tok_ref[...]
-    grad_hidden = dot(grad_ref[...], w_down, ((1,), (1,)))
+    units = 2 * half
+    loads[2].wait()
+    loads[5].wait()
+    grad_hidden = dot(grad_ref[...], w_down[...], ((1,), (1,)))
     high = grad_hidden.astype(BF16)
     rest = grad_hidden - high.astype(F32)
     middle = rest.astype(BF16)
@@ -55,8 +63,12 @@
     grad_hidden = (
         pieces[:, :units] + pieces[:, units : 2 * units] + pieces[:, 2 * units :]
     )
-    pre_gate = dot(rows_tok, w_gate, ((1,), (1,)))
-    pre_up = dot(rows_tok, w_up, ((1,), (1,)))
+    loads[0].wait()
+    loads[3].wait()
+    pre_gate = dot(tok_ref[...], w_gate[...], ((1,), (1,)))
+    loads[1].wait()
+    loads[4].wait()
+    pre_up = dot(tok_ref[...], w_up[...], ((1,), (1,)))
     sigmoid_gate = jax.nn.sigmoid(pre_gate)
     activated = pre_gate * sigmoid_gate
     hidden = (activated * pre_up).astype(BF16)
@@ -69,22 +81,40 @@
     turned = dot(turn, jnp.concatenate([hidden, grad_gate, grad_up], axis=1), ((0,), (0,)))
     turned = turned.astype(BF16)
     turned_hidden_ref[...] = turned[:, :units]
-    din_part = dot(turned[:, units : 2 * units], w_gate, ((1,), (0,)))
-    din_part += dot(turned[:, 2 * units :], w_up, ((1,), (0,)))
+    din_part = dot(turned[:, units : 2 * units], w_gate[...], ((1,), (0,)))
+    din_part += dot(turned[:, 2 * units :], w_up[...], ((1,), (0,)))
     din_ref[...] = din_part.astype(BF16)
-    out_ref[...] = dot(hidden, w_down, ((1,), (0,))).astype(BF16)
+    store_din = pltpu.make_async_copy(din_ref, din_hbm, sems.at[6])
+    store_din.start()
+    out_ref[...] = dot(hidden, w_down[...], ((1,), (0,))).astype(BF16)
+    store_out = pltpu.make_async_copy(out_ref, out_hbm, sems.at[7])
+    store_out.start()
+    store_din.wait()
+    store_out.wait()
 
 
 def forward_backward(rows_tok, rows_grad, turn, mine, theirs):
     n_rows, width = rows_tok.shape
-    narrow = jax.ShapeDtypeStruct((n_rows, 2 * mine[0].shape[0]), BF16)
-    wide = jax.ShapeDtypeStruct((n_rows, width), BF16)
+    units = 2 * mine[0].shape[0]
+    weights = [pltpu.with_memory_space_constraint(w, pltpu.HBM) for w in (*mine, *theirs)]
+    narrow = jax.ShapeDtypeStruct((n_rows, units), BF16)
+    wide = pltpu.HBM((n_rows, width), BF16)
+    in_hbm = pl.BlockSpec(memory_space=pltpu.HBM)
+    in_vmem = pl.BlockSpec(memory_space=pltpu.VMEM)
     return pl.pallas_call(
         layer_kernel,
         out_shape=(narrow, narrow, narrow, wide, wide),
+        in_specs=[in_vmem] * 3 + [in_hbm] * 6,
+        out_specs=(in_vmem, in_vmem, in_vmem, in_hbm, in_hbm),
+        scratch_shapes=[
+            *(pltpu.VMEM((units, width), BF16) for _ in range(3)),
+            pltpu.VMEM((n_rows, width), BF16),
+            pltpu.VMEM((n_rows, width), BF16),
+            pltpu.SemaphoreType.DMA((8,)),
+        ],
         compiler_params=pltpu.CompilerParams(vmem_limit_bytes=32 * 1024 * 1024),
         name="layer",
-    )(rows_tok, rows_grad, turn, *mine, *theirs)
+    )(rows_tok, rows_grad, turn, *weights)
 
 
 def on_device(tokens, cotangent, experts, gate_weights, w_gate, w_up, w_down):

time: 182 us -> 177 us (0.973)
  local copies, waits for them, and re-layouts: 19.7 us -> 9.91 us
  Pallas kernels: 5.07 us -> 9.28 us
    unnamed x38 -> x16, local copies, waits for them, and re-layouts: 13.1 us -> 3.31 us
    pallas_call x1, Pallas kernels: 5.07 us -> 9.28 us  [forward_backward(): pl.pallas_call(layer_kernel, out_shape=(narrow, narrow, narrow, wide, wid...]
  transfers between devices with their start and end apart: 15 -> 15, of which waited for: 6 -> 6; matrix products, arithmetic and copies ran while one was open for 12% -> 13% of each run, Pallas kernels for 0% -> 0%
where the time goes in v8:
time: 177 us; the launch traced here: 176 us
  starting transfers between devices  45.2 us (26%)
  blocking collectives  38.2 us (22%)
  waiting for transfers between devices  38.1 us (22%)
  matrix products  16.6 us (9%)
  between operations  14.4 us (8%)
  local copies, waits for them, and re-layouts  9.91 us (6%)
  Pallas kernels  9.28 us (5%)
  other arithmetic  3.99 us (2%)
    all_to_all x2, blocking collectives, spread(): return lax.all_to_all(copies, axis, split_axis=0, concat_axis=0, tiled=True)  38.2 us
    dot_general x8, matrix products, dot(): return lax.dot_general(a, b, (dims, ((), ())), preferred_element_type=F32)  14.9 us
    reduce_scatter x1, waiting for transfers between devices, on_device(): sum_din = lax.psum_scatter(sum_din, 'z', scatter_dimension=0, tiled=True)  13.6 us
    ppermute x6, starting transfers between devices, swap(): return lax.ppermute(a, 'c', [(0, 1), (1, 0)])  12.7 us
    ppermute x3, starting transfers between devices, turn_sum(): total += lax.ppermute(theirs, axis, pairs).astype(F32)  11.2 us
    all_to_all x1, waiting for transfers between devices, spread(): return lax.all_to_all(copies, axis, split_axis=0, concat_axis=0, tiled=True)  10.6 us
    all_to_all x2, starting transfers between devices, exchange_sum(): a = lax.all_to_all(a, axis, split_axis=0, concat_axis=0, tiled=True)  10.4 us
    pallas_call x1, Pallas kernels, forward_backward(): pl.pallas_call(layer_kernel, out_shape=(narrow, narrow, narrow, wide, wid...  9.28 us
  transfers between devices with their start and end apart: 15, of which 6 were waited for; matrix products, arithmetic and copies ran while one was open for 13% of the time, Pallas kernels for 0%

profile of v8, /device:TPU:8, one launch (start us, length us, event | category | flops | bytes accessed | tf_op | source)
XLA Modules:
  0.0 175.7 jit_solution(1089690824784352911)
XLA Ops:
  9.4 10.7 %all_to_all.30 = bf16[4,40,768]{2,1,0:T(8,128)(2,1)S(1)} all-to-all(bf16[4,40,768]{2,1,0:T(8,128)(2,1)S(1)} %broadcast_in_dim.46), channel_id=1, replica_groups=mesh['z'=8,'c'=2,'y'=8,'x'=4] {'x'}, dimensions={0} | all-to-all | bytes 491520 | tf_op jit(solution)/shard_map/all_to_all | solution.py:17
  21.2 27.6 %all_to_all.31 = bf16[8,40,768]{2,1,0:T(8,128)(2,1)S(1)} all-to-all(bf16[8,40,768]{2,1,0:T(8,128)(2,1)S(1)} %broadcast_in_dim.19), channel_id=1, replica_groups=mesh['z'=8,'c'=2,'y'=8,'x'=4] {'z'}, dimensions={0} | all-to-all | bytes 983040 | tf_op jit(solution)/shard_map/all_to_all | solution.py:17
  50.5 3.6 %all-to-all-start.1 = ((bf16[4,80,3072]{2,1,0:T(8,128)(2,1)}), bf16[4,80,3072]{2,1,0:T(8,128)(2,1)S(1)}, u32[]{:S(2)}, u32[]{:S(2)}) async-start(bf16[4,80,3072]{2,1,0:T(8,128)(2,1)} %broadcast_in_dim.21), calls=%async_computation.1 | async-start | bytes 3932160 | tf_op jit(solution)/shard_map/all_to_all | solution.py:17
  54.2 1.9 %collective-permute-start = (bf16[128,3072]{1,0:T(8,128)(2,1)}, bf16[128,3072]{1,0:T(8,128)(2,1)S(1)}, u32[]{:S(2)}, u32[]{:S(2)}) collective-permute-start(bf16[128,3072]{1,0:T(8,128)(2,1)} %bitcast.5.refs_0_), channel_id=1, source_target_pairs={{0,32},{32,0},{1,33},{33,1},{2,34},{34,2},{3,35},{35,3},{4,36},{36... | collective-permute-start | bytes 2359304 | tf_op jit(solution)/shard_map/ppermute | solution.py:21
  56.1 2.4 %collective-permute-start.1 = (bf16[128,3072]{1,0:T(8,128)(2,1)}, bf16[128,3072]{1,0:T(8,128)(2,1)S(1)}, u32[]{:S(2)}, u32[]{:S(2)}) collective-permute-start(bf16[128,3072]{1,0:T(8,128)(2,1)} %bitcast.6.refs_1_), channel_id=1, source_target_pairs={{0,32},{32,0},{1,33},{33,1},{2,34},{34,2},{3,35},{35,3},{4,36},{36... | collective-permute-start | bytes 2359304 | tf_op jit(solution)/shard_map/ppermute | solution.py:21
  58.5 1.9 %collective-permute-start.2 = (bf16[128,3072]{1,0:T(8,128)(2,1)}, bf16[128,3072]{1,0:T(8,128)(2,1)}, u32[]{:S(2)}, u32[]{:S(2)}) collective-permute-start(bf16[128,3072]{1,0:T(8,128)(2,1)} %bitcast.7.refs_2_), channel_id=1, source_target_pairs={{0,32},{32,0},{1,33},{33,1},{2,34},{34,2},{3,35},{35,3},{4,36},{36... | collective-permute-start | bytes 2359304 | tf_op jit(solution)/shard_map/ppermute | solution.py:21
  63.1 10.6 %all-to-all-done.1 = bf16[4,80,3072]{2,1,0:T(8,128)(2,1)S(1)} async-done(((bf16[4,80,3072]{2,1,0:T(8,128)(2,1)}), bf16[4,80,3072]{2,1,0:T(8,128)(2,1)S(1)}, u32[]{:S(2)}, u32[]{:S(2)}) %all-to-all-start.1) | async-done | bytes 1966112 | tf_op jit(solution)/shard_map/all_to_all | solution.py:17
  75.2 9.3 %layer.1 = (bf16[320,256]{1,0:T(8,128)(2,1)S(1)}, bf16[320,256]{1,0:T(8,128)(2,1)S(1)}, bf16[320,256]{1,0:T(8,128)(2,1)S(1)}, bf16[320,3072]{1,0:T(8,128)(2,1)}, bf16[320,3072]{1,0:T(8,128)(2,1)}) custom-call(bf16[320,3072]{1,0:T(8,128)(2,1)S(1)} %bitcast.51, bf16[320,3072]{1,0:T(8,128)(2,1)S(1)} %copy-done.1, bf16[320,320]{1,0:T(8,128)(2,1)S(1)} %fusion.14.turn_ref, ...), custom_call_target="tpu_custom_call" | custom-call | tf_op jit(solution)/shard_map/layer/pallas_call | solution.py:104
  84.6 4.4 %all-to-all-start.3 = ((bf16[4,80,3072]{2,1,0:T(8,128)(2,1)}), bf16[4,80,3072]{2,1,0:T(8,128)(2,1)}, u32[]{:S(2)}, u32[]{:S(2)}) async-start(bf16[4,80,3072]{2,1,0:T(8,128)(2,1)} %bitcast.56), calls=%async_computation.3 | async-start | bytes 3932160 | tf_op jit(solution)/shard_map/all_to_all | solution.py:163
  90.8 2.0 %collective-permute-start.6 = (f32[128,3072]{1,0:T(8,128)}, f32[128,3072]{1,0:T(8,128)}, u32[]{:S(2)}, u32[]{:S(2)}) collective-permute-start(f32[128,3072]{1,0:T(8,128)} %fusion.24), channel_id=1, source_target_pairs={{0,32},{32,0},{1,33},{33,1},{2,34},{34,2},{3,35},{35,3},{4,36},{36... | collective-permute-start | bytes 4718600 | tf_op jit(solution)/shard_map/ppermute | solution.py:21
  94.6 2.5 %collective-permute-start.7 = (f32[128,3072]{1,0:T(8,128)}, f32[128,3072]{1,0:T(8,128)}, u32[]{:S(2)}, u32[]{:S(2)}) collective-permute-start(f32[128,3072]{1,0:T(8,128)} %fusion.21), channel_id=1, source_target_pairs={{0,32},{32,0},{1,33},{33,1},{2,34},{34,2},{3,35},{35,3},{4,36},{36... | collective-permute-start | bytes 4718600 | tf_op jit(solution)/shard_map/ppermute | solution.py:21
  98.9 1.9 %collective-permute-start.8 = (f32[128,3072]{1,0:T(8,128)}, f32[128,3072]{1,0:T(8,128)}, u32[]{:S(2)}, u32[]{:S(2)}) collective-permute-start(f32[128,3072]{1,0:T(8,128)} %fusion.18), channel_id=1, source_target_pairs={{0,32},{32,0},{1,33},{33,1},{2,34},{34,2},{3,35},{35,3},{4,36},{36... | collective-permute-start | bytes 4718600 | tf_op jit(solution)/shard_map/ppermute | solution.py:21
  101.1 6.4 %all-to-all-done.3 = bf16[4,80,3072]{2,1,0:T(8,128)(2,1)} async-done(((bf16[4,80,3072]{2,1,0:T(8,128)(2,1)}), bf16[4,80,3072]{2,1,0:T(8,128)(2,1)}, u32[]{:S(2)}, u32[]{:S(2)}) %all-to-all-start.3) | async-done | bytes 1966112 | tf_op jit(solution)/shard_map/all_to_all | solution.py:163
  110.5 6.0 %all-to-all-start.4 = ((bf16[8,40,768]{2,1,0:T(8,128)(2,1)}), bf16[8,40,768]{2,1,0:T(8,128)(2,1)S(1)}, u32[]{:S(2)}, u32[]{:S(2)}) async-start(bf16[8,40,768]{2,1,0:T(8,128)(2,1)} %reshape.131), calls=%async_computation.4 | async-start | bytes 983040 | tf_op jit(solution)/shard_map/all_to_all | solution.py:163
  116.5 2.9 %fusion.5 = bf16[1,128,3072]{2,1,0:T(8,128)(2,1)} fusion(f32[128,3072]{1,0:T(8,128)} %collective-permute-done.6, bf16[320,3072]{1,0:T(8,128)(2,1)S(1)} %bitcast.54, bf16[320,256]{1,0:T(8,128)(2,1)S(1)} %get-tuple-element.12), kind=kOutput, calls=%fused_computation.8 | convolution fusion | flops 252444672 | bytes 4407296 | tf_op jit(solution)/shard_map/dot_general | solution.py:37
  119.4 13.6 %reduce-scatter.2.cloned.1.call-done = bf16[40,3072]{1,0:T(8,128)(2,1)} async-done(((bf16[320,3072]{1,0:T(8,128)(2,1)}), bf16[40,3072]{1,0:T(8,128)(2,1)}) %reduce-scatter.2.cloned.1.call-update) | async-done | bytes 245776 | tf_op jit(solution)/shard_map/reduce_scatter | solution.py:176
  134.7 5.3 %collective-permute-start.5 = (bf16[40,768]{1,0:T(8,128)(2,1)}, bf16[40,768]{1,0:T(8,128)(2,1)S(1)}, u32[]{:S(2)}, u32[]{:S(2)}) collective-permute-start(bf16[40,768]{1,0:T(8,128)(2,1)} %get-tuple-element.16), channel_id=1, source_target_pairs={{0,2},{1,3},{2,0},{3,1},{4,6},{5,7},{6,4},{7,5},{8,10},{9,11},{10,... | collective-permute-start | bytes 184328 | tf_op jit(solution)/shard_map/ppermute | solution.py:173
  140.1 4.0 %collective-permute-start.4 = (bf16[40,768]{1,0:T(8,128)(2,1)S(1)}, bf16[40,768]{1,0:T(8,128)(2,1)S(1)}, u32[]{:S(2)}, u32[]{:S(2)}) collective-permute-start(bf16[40,768]{1,0:T(8,128)(2,1)S(1)} %get-tuple-element.17), channel_id=1, source_target_pairs={{0,3},{1,0},{2,1},{3,2},{4,7},{5,4},{6,5},{7,6},{8,11},{9,8},{10,9... | collective-permute-start | bytes 184328 | tf_op jit(solution)/shard_map/ppermute | solution.py:173
  144.1 1.9 %collective-permute-start.3 = (bf16[40,768]{1,0:T(8,128)(2,1)S(1)}, bf16[40,768]{1,0:T(8,128)(2,1)S(1)}, u32[]{:S(2)}, u32[]{:S(2)}) collective-permute-start(bf16[40,768]{1,0:T(8,128)(2,1)S(1)} %get-tuple-element.15), channel_id=1, source_target_pairs={{0,1},{1,2},{2,3},{3,0},{4,5},{5,6},{6,7},{7,4},{8,9},{9,10},{10,1... | collective-permute-start | bytes 184328 | tf_op jit(solution)/shard_map/ppermute | solution.py:173
  146.0 2.9 %fusion.4 = bf16[1,128,3072]{2,1,0:T(8,128)(2,1)} fusion(f32[128,3072]{1,0:T(8,128)} %collective-permute-done.7, bf16[320,3072]{1,0:T(8,128)(2,1)S(1)} %bitcast.55, bf16[320,256]{1,0:T(8,128)(2,1)S(1)} %get-tuple-element.13), kind=kOutput, calls=%fused_computation.7 | convolution fusion | flops 252444672 | bytes 4407296 | tf_op jit(solution)/shard_map/dot_general | solution.py:37
  149.0 2.4 %collective-permute-done.3 = bf16[40,768]{1,0:T(8,128)(2,1)S(1)} collective-permute-done((bf16[40,768]{1,0:T(8,128)(2,1)S(1)}, bf16[40,768]{1,0:T(8,128)(2,1)S(1)}, u32[]{:S(2)}, u32[]{:S(2)}) %collective-permute-start.3) | collective-permute-done | bytes 61472 | tf_op jit(solution)/shard_map/ppermute | solution.py:173
  152.2 7.2 %all-to-all-start.5 = ((bf16[8,20,384]{2,1,0:T(8,128)(2,1)}), bf16[8,20,384]{2,1,0:T(8,128)(2,1)S(1)}, u32[]{:S(2)}, u32[]{:S(2)}) async-start(bf16[8,20,384]{2,1,0:T(8,128)(2,1)} %copy.45), calls=%async_computation.6 | async-start | bytes 294912 | tf_op jit(solution)/shard_map/all_to_all | solution.py:183
  159.4 3.5 %fusion.3 = bf16[1,128,3072]{2,1,0:T(8,128)(2,1)} fusion(f32[128,3072]{1,0:T(8,128)} %collective-permute-done.8, bf16[320,3072]{1,0:T(8,128)(2,1)} %all-gather.2.cloned.1.call-done.grad_ref, bf16[320,256]{1,0:T(8,128)(2,1)S(1)} %get-tuple-element.14), kind=kOutput, calls=%fused_computation.6 | convolution fusion | flops 252444672 | bytes 4407296 | tf_op jit(solution)/shard_map/dot_general | solution.py:37
  162.9 4.3 %all-to-all-done.5 = bf16[8,20,384]{2,1,0:T(8,128)(2,1)S(1)} async-done(((bf16[8,20,384]{2,1,0:T(8,128)(2,1)}), bf16[8,20,384]{2,1,0:T(8,128)(2,1)S(1)}, u32[]{:S(2)}, u32[]{:S(2)}) %all-to-all-start.5) | async-done | bytes 122912 | tf_op jit(solution)/shard_map/all_to_all | solution.py:183
  (77 shorter events, 22.0 us)
Async XLA Ops:
  7.2 1.9 %copy-start = (bf16[24,3072]{1,0:T(8,128)(2,1)S(1)}, bf16[24,3072]{1,0:T(8,128)(2,1)}, u32[]{:S(2)}) copy-start(bf16[24,3072]{1,0:T(8,128)(2,1)} %param.8) | copy-start | bytes 442372
  7.2 13.7 %copy-start.5 = (bf16[24,3072]{1,0:T(8,128)(2,1)S(1)}, bf16[24,3072]{1,0:T(8,128)(2,1)}, u32[]{:S(2)}) copy-start(bf16[24,3072]{1,0:T(8,128)(2,1)} %param.7) | copy-start | bytes 442372
  7.2 66.5 %all-gather.2.cloned.1.call-start = ((), (), s32[]{:S(2)}) async-start(), calls=%async_computation.7 | async-start | bytes 2211840 | tf_op jit(solution)/shard_map/all_gather | solution.py:136
  50.5 23.2 %all-to-all-start.1 = ((bf16[4,80,3072]{2,1,0:T(8,128)(2,1)}), bf16[4,80,3072]{2,1,0:T(8,128)(2,1)S(1)}, u32[]{:S(2)}, u32[]{:S(2)}) async-start(bf16[4,80,3072]{2,1,0:T(8,128)(2,1)} %broadcast_in_dim.21), calls=%async_computation.1 | async-start | bytes 3932160 | tf_op jit(solution)/shard_map/all_to_all | solution.py:17
  54.1 78.8 %reduce-scatter.2.cloned.1.call-start = ((), (), s32[]{:S(2)}) async-start(), calls=%async_computation.8 | async-start | bytes 2211840 | tf_op jit(solution)/shard_map/reduce_scatter | solution.py:176
  54.2 6.4 %collective-permute-start = (bf16[128,3072]{1,0:T(8,128)(2,1)}, bf16[128,3072]{1,0:T(8,128)(2,1)S(1)}, u32[]{:S(2)}, u32[]{:S(2)}) collective-permute-start(bf16[128,3072]{1,0:T(8,128)(2,1)} %bitcast.5.refs_0_), channel_id=1, source_target_pairs={{0,32},{32,0},{1,33},{33,1},{2,34},{34,2},{3,35},{35,3},{4,36},{36... | collective-permute-start | bytes 2359304 | tf_op jit(solution)/shard_map/ppermute | solution.py:21
  56.1 4.5 %collective-permute-start.1 = (bf16[128,3072]{1,0:T(8,128)(2,1)}, bf16[128,3072]{1,0:T(8,128)(2,1)S(1)}, u32[]{:S(2)}, u32[]{:S(2)}) collective-permute-start(bf16[128,3072]{1,0:T(8,128)(2,1)} %bitcast.6.refs_1_), channel_id=1, source_target_pairs={{0,32},{32,0},{1,33},{33,1},{2,34},{34,2},{3,35},{35,3},{4,36},{36... | collective-permute-start | bytes 2359304 | tf_op jit(solution)/shard_map/ppermute | solution.py:21
  58.5 4.5 %collective-permute-start.2 = (bf16[128,3072]{1,0:T(8,128)(2,1)}, bf16[128,3072]{1,0:T(8,128)(2,1)}, u32[]{:S(2)}, u32[]{:S(2)}) collective-permute-start(bf16[128,3072]{1,0:T(8,128)(2,1)} %bitcast.7.refs_2_), channel_id=1, source_target_pairs={{0,32},{32,0},{1,33},{33,1},{2,34},{34,2},{3,35},{35,3},{4,36},{36... | collective-permute-start | bytes 2359304 | tf_op jit(solution)/shard_map/ppermute | solution.py:21
  60.6 0.9 copy-start.3
  61.5 0.9 copy-start.4
  73.7 1.5 copy-start.1
  84.6 23.0 %all-to-all-start.3 = ((bf16[4,80,3072]{2,1,0:T(8,128)(2,1)}), bf16[4,80,3072]{2,1,0:T(8,128)(2,1)}, u32[]{:S(2)}, u32[]{:S(2)}) async-start(bf16[4,80,3072]{2,1,0:T(8,128)(2,1)} %bitcast.56), calls=%async_computation.3 | async-start | bytes 3932160 | tf_op jit(solution)/shard_map/all_to_all | solution.py:163
  90.8 6.4 %copy-start.2 = (bf16[320,3072]{1,0:T(8,128)(2,1)S(1)}, bf16[320,3072]{1,0:T(8,128)(2,1)}, u32[]{:S(2)}) copy-start(bf16[320,3072]{1,0:T(8,128)(2,1)} %all-gather.2.cloned.1.call-done.grad_ref) | copy-start | bytes 5898244
  90.8 25.7 %collective-permute-start.6 = (f32[128,3072]{1,0:T(8,128)}, f32[128,3072]{1,0:T(8,128)}, u32[]{:S(2)}, u32[]{:S(2)}) collective-permute-start(f32[128,3072]{1,0:T(8,128)} %fusion.24), channel_id=1, source_target_pairs={{0,32},{32,0},{1,33},{33,1},{2,34},{34,2},{3,35},{35,3},{4,36},{36... | collective-permute-start | bytes 4718600 | tf_op jit(solution)/shard_map/ppermute | solution.py:21
  94.6 6.2 %copy-start.6 = (s32[24,2]{0,1:T(2,128)S(1)}, s32[24,2]{0,1:T(2,128)}, u32[]{:S(2)}) copy-start(s32[24,2]{0,1:T(2,128)} %param.9) | copy-start | bytes 580
  94.6 6.5 %copy-start.7 = (f32[24,2]{0,1:T(2,128)S(1)}, f32[24,2]{0,1:T(2,128)}, u32[]{:S(2)}) copy-start(f32[24,2]{0,1:T(2,128)} %param.10) | copy-start | bytes 580
  94.6 51.4 %collective-permute-start.7 = (f32[128,3072]{1,0:T(8,128)}, f32[128,3072]{1,0:T(8,128)}, u32[]{:S(2)}, u32[]{:S(2)}) collective-permute-start(f32[128,3072]{1,0:T(8,128)} %fusion.21), channel_id=1, source_target_pairs={{0,32},{32,0},{1,33},{33,1},{2,34},{34,2},{3,35},{35,3},{4,36},{36... | collective-permute-start | bytes 4718600 | tf_op jit(solution)/shard_map/ppermute | solution.py:21
  98.9 60.5 %collective-permute-start.8 = (f32[128,3072]{1,0:T(8,128)}, f32[128,3072]{1,0:T(8,128)}, u32[]{:S(2)}, u32[]{:S(2)}) collective-permute-start(f32[128,3072]{1,0:T(8,128)} %fusion.18), channel_id=1, source_target_pairs={{0,32},{32,0},{1,33},{33,1},{2,34},{34,2},{3,35},{35,3},{4,36},{36... | collective-permute-start | bytes 4718600 | tf_op jit(solution)/shard_map/ppermute | solution.py:21
  110.5 38.4 %all-to-all-start.4 = ((bf16[8,40,768]{2,1,0:T(8,128)(2,1)}), bf16[8,40,768]{2,1,0:T(8,128)(2,1)S(1)}, u32[]{:S(2)}, u32[]{:S(2)}) async-start(bf16[8,40,768]{2,1,0:T(8,128)(2,1)} %reshape.131), calls=%async_computation.4 | async-start | bytes 983040 | tf_op jit(solution)/shard_map/all_to_all | solution.py:163
  134.7 14.3 %collective-permute-start.5 = (bf16[40,768]{1,0:T(8,128)(2,1)}, bf16[40,768]{1,0:T(8,128)(2,1)S(1)}, u32[]{:S(2)}, u32[]{:S(2)}) collective-permute-start(bf16[40,768]{1,0:T(8,128)(2,1)} %get-tuple-element.16), channel_id=1, source_target_pairs={{0,2},{1,3},{2,0},{3,1},{4,6},{5,7},{6,4},{7,5},{8,10},{9,11},{10,... | collective-permute-start | bytes 184328 | tf_op jit(solution)/shard_map/ppermute | solution.py:173
  140.1 9.0 %collective-permute-start.4 = (bf16[40,768]{1,0:T(8,128)(2,1)S(1)}, bf16[40,768]{1,0:T(8,128)(2,1)S(1)}, u32[]{:S(2)}, u32[]{:S(2)}) collective-permute-start(bf16[40,768]{1,0:T(8,128)(2,1)S(1)} %get-tuple-element.17), channel_id=1, source_target_pairs={{0,3},{1,0},{2,1},{3,2},{4,7},{5,4},{6,5},{7,6},{8,11},{9,8},{10,9... | collective-permute-start | bytes 184328 | tf_op jit(solution)/shard_map/ppermute | solution.py:173
  144.1 7.3 %collective-permute-start.3 = (bf16[40,768]{1,0:T(8,128)(2,1)S(1)}, bf16[40,768]{1,0:T(8,128)(2,1)S(1)}, u32[]{:S(2)}, u32[]{:S(2)}) collective-permute-start(bf16[40,768]{1,0:T(8,128)(2,1)S(1)} %get-tuple-element.15), channel_id=1, source_target_pairs={{0,1},{1,2},{2,3},{3,0},{4,5},{5,6},{6,7},{7,4},{8,9},{9,10},{10,1... | collective-permute-start | bytes 184328 | tf_op jit(solution)/shard_map/ppermute | solution.py:173
  152.2 15.0 %all-to-all-start.5 = ((bf16[8,20,384]{2,1,0:T(8,128)(2,1)}), bf16[8,20,384]{2,1,0:T(8,128)(2,1)S(1)}, u32[]{:S(2)}, u32[]{:S(2)}) async-start(bf16[8,20,384]{2,1,0:T(8,128)(2,1)} %copy.45), calls=%async_computation.6 | async-start | bytes 294912 | tf_op jit(solution)/shard_map/all_to_all | solution.py:183
Sparse Core Ops, SparseCore 0:
  21.0 48.3 all-gather.1
  84.7 48.2 reduce-scatter.1
